TPU v7x, 128 devices: a whole 4x4x4 slice. The times are simulated.
128 devices in a mesh: grp: 8 (over y, core), rep: 16 (over z, x).
Axes of the slice: x: 4, y: 4, z: 4, core: 2. Of those that a mesh axis runs over, the one named last changes fastest.
Arguments:
- coefficients: bfloat16 [16384, 2048], P(('grp', 'rep')), may hold values from -100 to 100
- truncation: int32 [16], replicated, may hold values from 16 to 64
- neighbours: int32 [50, 16384], P(None, ('grp', 'rep')), may hold values from 0 to 16383, as said below
- initial: float32 [32, 16384], P(None, ('grp', 'rep')), may hold values from -6 to 6
Outputs:
- alignment: float32 [2, 50, 16384], P(None, None, ('grp', 'rep'))
- vectors: float32 [32, 16384], P(None, ('grp', 'rep'))
Inputs may be any that keep to these rules, and one draw needn't show every extreme that they name: `neighbours`: every neighbour of a particle is another particle of the same block of 2048 particles that holds it (the particles of one group of 16 devices along rep). For each device, the neighbour slots of its 128 particles that name particles of one other device number at most 64; every device has, in every draw, one other device that its slots name exactly 64 times.
All inputs are finite; a program needn't handle non-finite values.
Results may differ from a plain program's by a relative error of at most 0.0003.
Values may be sent and summed in bfloat16 or wider, within the bound.
No kernel may reach another device: no remote copies, remote signals or barrier semaphores. Data moves between devices by JAX's collectives and lax.ppermute only.
A program may use at most 128 MiB of HBM per device.

v0:
```python
import functools
import math

import jax
import jax.numpy as jnp
from jax import lax
from jax.sharding import Mesh
from jax.sharding import PartitionSpec as P

ANG = 64
RAD = 16
ANGLES = 256
NB = 50
ITERS = 3
GRP = ("grp_0", "grp_1")
REP = ("rep_0", "rep_1")
GRP_REP = ("grp_0", "grp_1", "rep_0", "rep_1")


epsilon = 1e-06


def sent_to_all(array, axis):
    peers = lax.axis_size(axis)
    return lax.all_to_all(
        jnp.broadcast_to(array[None], (peers, *array.shape)), axis, 0, 0, tiled=True
    )


def in_order(pieces, dim):
    lengths = list(pieces.shape[1:])
    lengths[dim] *= pieces.shape[0]
    return jnp.moveaxis(pieces, 0, dim).reshape(lengths)


def gathered_copies(array, axis, dim):
    pieces = sent_to_all(array, axis)
    return in_order(pieces, dim)


def one_axis_at_a_time(array, axes):
    return functools.reduce(lax.psum, axes, array)


def rotation_angle_grid(angular, samples):
    frequency = jnp.arange(angular, dtype=jnp.float32)
    sample_angle = jnp.arange(samples, dtype=jnp.float32) * (2.0 * math.pi / samples)
    phases = frequency[:, None] * sample_angle[None, :]
    transform = jnp.concatenate([jnp.cos(phases), -jnp.sin(phases)], axis=0)
    return (transform, jnp.cos(sample_angle), jnp.sin(sample_angle))


def kept_mask(truncation):
    levels = jnp.arange(ANG, dtype=jnp.int32)
    return (levels[None, :] < truncation[:, None]).astype(jnp.float32)


def pair_moments(own_rows, other_rows, weights, transform, cosine_row, sine_row):
    row_count = own_rows.shape[0]
    masked = own_rows.astype(jnp.float32).reshape(row_count, 2, RAD, ANG) * weights
    partner = other_rows.reshape(NB, row_count, 2, RAD, ANG).astype(jnp.float32)
    own_real = masked[None, :, 0]
    own_imag = masked[None, :, 1]
    partner_real = partner[:, :, 0]
    partner_imag = partner[:, :, 1]
    real_fourier_coeffs = jnp.sum(own_real * partner_real + own_imag * partner_imag, axis=2)
    imaginary_fourier_coeffs = jnp.sum(own_imag * partner_real - own_real * partner_imag, axis=2)
    spectrum = jnp.concatenate([real_fourier_coeffs, imaginary_fourier_coeffs], axis=2)
    correlation = jnp.einsum("nbk,km->nbm", spectrum, transform, precision=lax.Precision.HIGHEST)
    squared = correlation * correlation
    energy = jnp.mean(squared, axis=2)
    moment_real = jnp.mean(squared * cosine_row, axis=2)
    moment_imaginary = jnp.mean(squared * sine_row, axis=2)
    return (energy, moment_real, moment_imaginary)


def lower_inverse(lower):
    matrix_order = lower.shape[0]
    identity = jnp.eye(matrix_order, dtype=lower.dtype)
    inverse_rows = []
    for target in range(matrix_order):
        running = identity[target]
        for source in range(target):
            running = running - lower[target, source] * inverse_rows[source]
        inverse_rows.append(running / lower[target, target])
    return jnp.stack(inverse_rows)


def shards(coefficients, truncation, neighbours, initial):
    maximum_frequency = lax.Precision.HIGHEST
    groups = lax.axis_size(GRP)
    replicas = lax.axis_size(REP)
    particles = coefficients.shape[0]
    particle_total = particles * groups * replicas
    group_start = lax.axis_index(GRP) * (replicas * particles)
    in_group = neighbours - group_start
    weights = kept_mask(truncation)
    transform, cosine_row, sine_row = rotation_angle_grid(ANG, ANGLES)
    rows_all = lax.all_gather(coefficients, REP, axis=0, tiled=True)
    block_width = math.gcd(particles, 32)
    blocks = particles // block_width
    own_blocks = coefficients.reshape(blocks, block_width, coefficients.shape[1])
    index_blocks = in_group.reshape(NB, blocks, block_width).transpose(1, 0, 2)

    def one_block(operands):
        own_rows, indices = operands
        other_rows = jnp.take(rows_all, indices.reshape(-1), axis=0)
        return pair_moments(own_rows, other_rows, weights, transform, cosine_row, sine_row)

    energy, moment_real, moment_imaginary = lax.map(one_block, (own_blocks, index_blocks))
    energy = energy.transpose(1, 0, 2).reshape(NB, particles)
    moment_real = moment_real.transpose(1, 0, 2).reshape(NB, particles)
    moment_imaginary = moment_imaginary.transpose(1, 0, 2).reshape(NB, particles)
    alignment = jnp.stack([moment_real / (energy + epsilon), moment_imaginary / (energy + epsilon)])
    degree = epsilon + jnp.sum(energy, axis=0)
    vector_count = initial.shape[0] // 2
    current = initial
    factor = jnp.eye(vector_count, dtype=jnp.float32)
    for iteration in range(ITERS):
        whole = gathered_copies(current, REP, 1)
        picked = jnp.take(whole, in_group.reshape(-1), axis=1).reshape(
            current.shape[0], NB, particles
        )
        real_part = picked[:vector_count]
        imag_part = picked[vector_count:]
        apply_image_real = (
            jnp.sum(moment_real * real_part - moment_imaginary * imag_part, axis=1) / degree
        )
        apply_image_imag = (
            jnp.sum(moment_real * imag_part + moment_imaginary * real_part, axis=1) / degree
        )
        raw_matrix = one_axis_at_a_time(
            (
                jnp.dot(apply_image_real, apply_image_real.T, precision=maximum_frequency)
                + jnp.dot(apply_image_imag, apply_image_imag.T, precision=maximum_frequency)
            )
            / particle_total,
            GRP_REP,
        )
        folded = jnp.dot(
            jnp.dot(factor, raw_matrix, precision=maximum_frequency),
            factor.T,
            precision=maximum_frequency,
        )
        factor = jnp.dot(
            lower_inverse(jnp.linalg.cholesky(folded)), factor, precision=maximum_frequency
        )
        current = jnp.concatenate([apply_image_real, apply_image_imag], axis=0)
    vectors = jnp.concatenate(
        [
            jnp.dot(factor, current[:vector_count], precision=maximum_frequency),
            jnp.dot(factor, current[vector_count:], precision=maximum_frequency),
        ],
        axis=0,
    )
    return (alignment, vectors)


def solution(mesh):
    split = Mesh(mesh.devices.reshape(4, 2, 4, 4), ("grp_0", "grp_1", "rep_0", "rep_1"))
    in_specs = (P(GRP_REP, None), P(), P(None, GRP_REP), P(None, GRP_REP))
    out_specs = (P(None, None, GRP_REP), P(None, GRP_REP))
    return jax.shard_map(
        shards, mesh=split, in_specs=in_specs, out_specs=out_specs, check_vma=False
    )
```

profile of v0, /device:TPU:1, one launch (start us, length us, event | category | flops | bytes accessed | tf_op | source)
XLA Modules:
  0.0 772.1 jit_solution(4029858187510575812)
XLA Ops:
  25.6 12.6 %gather_fusion.1 = f32[6400,32]{1,0:T(8,128)} fusion(f32[32,2048]{0,1:T(8,128)S(1)} %bitcast.534, s32[7168]{0:T(1024)S(1)} %pad_clamp_fusion.1), kind=kCustom, calls=%fused_computation.1.clone | custom fusion | bytes 1664000 | tf_op jit(solution)/shard_map/jit(_take)/gather | solution.py:121
  47.3 36.8 %all-gather.2.cloned.1.call-done = bf16[2048,2048]{1,0:T(8,128)(2,1)} async-done(((bf16[128,2048]{1,0:T(8,128)(2,1)}), bf16[2048,2048]{1,0:T(8,128)(2,1)}) %all-gather.2.cloned.1.call-update) | async-done | bytes 8388624 | tf_op jit(solution)/shard_map/all_gather | solution.py:99
  84.1 276.2 %while.15 = (s32[]{:T(128)}, f32[4,50,32]{2,1,0:T(8,128)S(1)}, f32[4,50,32]{2,1,0:T(8,128)S(1)}, f32[4,50,32]{2,1,0:T(8,128)S(1)}, bf16[4,32,2048]{2,1,0:T(8,128...) while((s32[]{:T(128)}, f32[4,50,32]{2,1,0:T(8,128)S(1)}, ...), condition=%wide.region_6.7_spmd.clone, body=%wide.region_0.6_spmd.clone.sunk | while | flops 651414080 | bytes 63265596 | solution.py:110
  84.5 18.8 %gather_fusion = bf16[1600,2048]{1,0:T(8,128)(2,1)} fusion(bf16[2048,2048]{1,0:T(8,128)(2,1)} %get-tuple-element.755, s32[2048]{0:T(1024)S(1)} %pad_clamp_fusion.3), kind=kCustom, calls=%fused_computation.clone.clone.1 | custom fusion | bytes 13113600 | tf_op jit(solution)/shard_map/while/body/eval_jaxpr/jit(_take)/gather | solution.py:107
  103.2 19.3 %gather.27 = bf16[50,32,2,16,64]{4,3,2,1,0:T(8,128)(2,1)} reshape(bf16[1600,2048]{1,0:T(8,128)(2,1)} %gather_fusion) | data formatting | bytes 13107200 | tf_op jit(solution)/shard_map/while/body/eval_jaxpr/jit(_take)/gather | solution.py:107
  122.5 14.8 %select_convert_fusion.2 = f32[50,32,2,16,64]{4,3,2,1,0:T(8,128)} fusion(bf16[50,32,2,16,64]{4,3,2,1,0:T(8,128)(2,1)} %gather.27, pred[50,32]{1,0:T(8,128)(4,1)S(1)} %compare_and_fusion.3), kind=kLoop, calls=%fused_computation.11.clone.1 | loop fusion | flops 6553600 | bytes 19662400 | tf_op jit(solution)/shard_map/while/body/eval_jaxpr/convert_element_type | solution.py:61
  138.6 12.6 %add_reduce_fusion.5 = (f32[50,32,64]{2,1,0:T(8,128)S(1)}, f32[50,32,64]{2,1,0:T(8,128)S(1)}) fusion(f32[50,32,2,16,64]{4,3,2,1,0:T(8,128)} %select_convert_fusion.2, f32[32,16,64]{2,1,0:T(8,128)S(1)} %get-tuple-element.720, f32[32,16,64]{2,1,0:T(8,128)S(1)} %get-tuple-element.721), kind=kLoop, calls=%fused_computation.10.clone.1 | loop fusion | flops 12902400 | bytes 14188544 | tf_op jit(solution)/shard_map/while/body/eval_jaxpr/reduce_sum | solution.py:66
  153.5 18.8 %gather_fusion = bf16[1600,2048]{1,0:T(8,128)(2,1)} fusion(bf16[2048,2048]{1,0:T(8,128)(2,1)} %get-tuple-element.755, s32[2048]{0:T(1024)S(1)} %pad_clamp_fusion.3), kind=kCustom, calls=%fused_computation.clone.clone.1 | custom fusion | bytes 13113600 | tf_op jit(solution)/shard_map/while/body/eval_jaxpr/jit(_take)/gather | solution.py:107
  172.3 19.3 %gather.27 = bf16[50,32,2,16,64]{4,3,2,1,0:T(8,128)(2,1)} reshape(bf16[1600,2048]{1,0:T(8,128)(2,1)} %gather_fusion) | data formatting | bytes 13107200 | tf_op jit(solution)/shard_map/while/body/eval_jaxpr/jit(_take)/gather | solution.py:107
  191.6 14.8 %select_convert_fusion.2 = f32[50,32,2,16,64]{4,3,2,1,0:T(8,128)} fusion(bf16[50,32,2,16,64]{4,3,2,1,0:T(8,128)(2,1)} %gather.27, pred[50,32]{1,0:T(8,128)(4,1)S(1)} %compare_and_fusion.3), kind=kLoop, calls=%fused_computation.11.clone.1 | loop fusion | flops 6553600 | bytes 19662400 | tf_op jit(solution)/shard_map/while/body/eval_jaxpr/convert_element_type | solution.py:61
  207.7 12.6 %add_reduce_fusion.5 = (f32[50,32,64]{2,1,0:T(8,128)S(1)}, f32[50,32,64]{2,1,0:T(8,128)S(1)}) fusion(f32[50,32,2,16,64]{4,3,2,1,0:T(8,128)} %select_convert_fusion.2, f32[32,16,64]{2,1,0:T(8,128)S(1)} %get-tuple-element.720, f32[32,16,64]{2,1,0:T(8,128)S(1)} %get-tuple-element.721), kind=kLoop, calls=%fused_computation.10.clone.1 | loop fusion | flops 12902400 | bytes 14188544 | tf_op jit(solution)/shard_map/while/body/eval_jaxpr/reduce_sum | solution.py:66
  222.6 18.8 %gather_fusion = bf16[1600,2048]{1,0:T(8,128)(2,1)} fusion(bf16[2048,2048]{1,0:T(8,128)(2,1)} %get-tuple-element.755, s32[2048]{0:T(1024)S(1)} %pad_clamp_fusion.3), kind=kCustom, calls=%fused_computation.clone.clone.1 | custom fusion | bytes 13113600 | tf_op jit(solution)/shard_map/while/body/eval_jaxpr/jit(_take)/gather | solution.py:107
  241.4 19.3 %gather.27 = bf16[50,32,2,16,64]{4,3,2,1,0:T(8,128)(2,1)} reshape(bf16[1600,2048]{1,0:T(8,128)(2,1)} %gather_fusion) | data formatting | bytes 13107200 | tf_op jit(solution)/shard_map/while/body/eval_jaxpr/jit(_take)/gather | solution.py:107
  260.6 14.8 %select_convert_fusion.2 = f32[50,32,2,16,64]{4,3,2,1,0:T(8,128)} fusion(bf16[50,32,2,16,64]{4,3,2,1,0:T(8,128)(2,1)} %gather.27, pred[50,32]{1,0:T(8,128)(4,1)S(1)} %compare_and_fusion.3), kind=kLoop, calls=%fused_computation.11.clone.1 | loop fusion | flops 6553600 | bytes 19662400 | tf_op jit(solution)/shard_map/while/body/eval_jaxpr/convert_element_type | solution.py:61
  276.7 12.6 %add_reduce_fusion.5 = (f32[50,32,64]{2,1,0:T(8,128)S(1)}, f32[50,32,64]{2,1,0:T(8,128)S(1)}) fusion(f32[50,32,2,16,64]{4,3,2,1,0:T(8,128)} %select_convert_fusion.2, f32[32,16,64]{2,1,0:T(8,128)S(1)} %get-tuple-element.720, f32[32,16,64]{2,1,0:T(8,128)S(1)} %get-tuple-element.721), kind=kLoop, calls=%fused_computation.10.clone.1 | loop fusion | flops 12902400 | bytes 14188544 | tf_op jit(solution)/shard_map/while/body/eval_jaxpr/reduce_sum | solution.py:66
  291.7 18.8 %gather_fusion = bf16[1600,2048]{1,0:T(8,128)(2,1)} fusion(bf16[2048,2048]{1,0:T(8,128)(2,1)} %get-tuple-element.755, s32[2048]{0:T(1024)S(1)} %pad_clamp_fusion.3), kind=kCustom, calls=%fused_computation.clone.clone.1 | custom fusion | bytes 13113600 | tf_op jit(solution)/shard_map/while/body/eval_jaxpr/jit(_take)/gather | solution.py:107
  310.4 19.3 %gather.27 = bf16[50,32,2,16,64]{4,3,2,1,0:T(8,128)(2,1)} reshape(bf16[1600,2048]{1,0:T(8,128)(2,1)} %gather_fusion) | data formatting | bytes 13107200 | tf_op jit(solution)/shard_map/while/body/eval_jaxpr/jit(_take)/gather | solution.py:107
  329.7 14.8 %select_convert_fusion.2 = f32[50,32,2,16,64]{4,3,2,1,0:T(8,128)} fusion(bf16[50,32,2,16,64]{4,3,2,1,0:T(8,128)(2,1)} %gather.27, pred[50,32]{1,0:T(8,128)(4,1)S(1)} %compare_and_fusion.3), kind=kLoop, calls=%fused_computation.11.clone.1 | loop fusion | flops 6553600 | bytes 19662400 | tf_op jit(solution)/shard_map/while/body/eval_jaxpr/convert_element_type | solution.py:61
  345.8 12.6 %add_reduce_fusion.5 = (f32[50,32,64]{2,1,0:T(8,128)S(1)}, f32[50,32,64]{2,1,0:T(8,128)S(1)}) fusion(f32[50,32,2,16,64]{4,3,2,1,0:T(8,128)} %select_convert_fusion.2, f32[32,16,64]{2,1,0:T(8,128)S(1)} %get-tuple-element.720, f32[32,16,64]{2,1,0:T(8,128)S(1)} %get-tuple-element.721), kind=kLoop, calls=%fused_computation.10.clone.1 | loop fusion | flops 12902400 | bytes 14188544 | tf_op jit(solution)/shard_map/while/body/eval_jaxpr/reduce_sum | solution.py:66
  380.5 12.6 %gather_fusion.2 = f32[6400,32]{1,0:T(8,128)} fusion(f32[32,2048]{0,1:T(8,128)S(1)} %bitcast.535, s32[7168]{0:T(1024)S(1)} %copy-done.1), kind=kCustom, calls=%fused_computation.2.clone | custom fusion | bytes 1664000 | tf_op jit(solution)/shard_map/jit(_take)/gather | solution.py:121
  435.7 13.6 %all-reduce.2 = (f32[16,16]{1,0:T(8,128)S(1)}, f32[16,16]{1,0:T(8,128)S(1)}, f32[16,16]{1,0:T(8,128)S(1)}) all-reduce(f32[16,16]{1,0:T(8,128)S(1)} %fusion.17, f32[16,16]{1,0:T(8,128)S(1)} %fusion.16, f32[16,16]{1,0:T(8,128)S(1)} %fusion.15), channel_id=1, replica_groups=mesh['grp_0'=4,'grp_1'=2,'rep_0'=4,'rep_1'=4] {'grp_0'}, use_global_device_ids=true, to_apply=%region_10.12 | all-reduce | flops 768 | bytes 6144 | tf_op jit(solution)/shard_map/psum | solution.py:42
  491.2 84.9 %subtract_divide_fusion.30 = (f32[1,16]{1,0:T(1,128)S(1)}, f32[1,16]{1,0:T(1,128)S(1)}, f32[1,16]{1,0:T(1,128)S(1)}, f32[1,16]{1,0:T(1,128)S(1)}, f32[1,16]{1,0:...) fusion(f32[]{:T(128)} %bitcast.152, ...), kind=kLoop, calls=%fused_computation.131 | loop fusion | flops 4096 | bytes 2592 | tf_op jit(solution)/shard_map/div | solution.py:85
  585.1 84.9 %subtract_divide_fusion.15 = (f32[1,16]{1,0:T(1,128)S(1)}, f32[1,16]{1,0:T(1,128)S(1)}, f32[1,16]{1,0:T(1,128)S(1)}, f32[1,16]{1,0:T(1,128)S(1)}, f32[1,16]{1,0:...) fusion(f32[]{:T(128)} %bitcast.294, ...), kind=kLoop, calls=%fused_computation.116 | loop fusion | flops 4096 | bytes 2592 | tf_op jit(solution)/shard_map/div | solution.py:85
  679.0 84.9 %subtract_divide_fusion = (f32[1,16]{1,0:T(1,128)S(1)}, f32[1,16]{1,0:T(1,128)S(1)}, f32[1,16]{1,0:T(1,128)S(1)}, f32[1,16]{1,0:T(1,128)S(1)}, f32[1,16]{1,0:T(1...) fusion(f32[]{:T(128)} %bitcast.436, ...), kind=kLoop, calls=%fused_computation.101 | loop fusion | flops 4096 | bytes 2592 | tf_op jit(solution)/shard_map/div | solution.py:85
  (197 shorter events, 165.3 us)
Async XLA Ops:
  7.2 77.0 %all-gather.2.cloned.1.call-start = ((), (), s32[]{:S(2)}) async-start(), calls=%async_computation.3 | async-start | bytes 8912896 | tf_op jit(solution)/shard_map/all_gather | solution.py:99
  9.3 16.0 %all-to-all-start = ((f32[16,32,128]{2,1,0:T(8,128)}), f32[16,32,128]{2,1,0:T(8,128)S(1)}, u32[]{:S(2)}, u32[]{:S(2)}) async-start(f32[16,32,128]{2,1,0:T(8,128)} %broadcast_in_dim.33), calls=%async_computation | async-start | bytes 524288 | tf_op jit(solution)/shard_map/all_to_all | solution.py:25
  18.5 19.7 %copy-start.3 = (pred[6400]{0:T(1024)(128)(4,1)}, pred[6400]{0:T(1024)(128)(4,1)S(1)}, u32[]{:S(2)}) copy-start(pred[6400]{0:T(1024)(128)(4,1)S(1)} %get-tuple-element.227) | copy-start | bytes 19204
  19.6 18.7 %copy-start = (s32[7168]{0:T(1024)}, s32[7168]{0:T(1024)S(1)}, u32[]{:S(2)}) copy-start(s32[7168]{0:T(1024)S(1)} %pad_clamp_fusion.1) | copy-start | bytes 86020
  43.5 40.6 %copy-start.5 = (s32[16]{0:T(128)S(1)}, s32[16]{0:T(128)}, u32[]{:S(2)}) copy-start(s32[16]{0:T(128)} %param.10) | copy-start | bytes 196
  366.0 14.5 %copy-start.1 = (s32[7168]{0:T(1024)S(1)}, s32[7168]{0:T(1024)}, u32[]{:S(2)}) copy-start(s32[7168]{0:T(1024)} %copy-done) | copy-start | bytes 86020
  367.6 12.5 %all-to-all-start.1 = ((f32[16,32,128]{2,1,0:T(8,128)}), f32[16,32,128]{2,1,0:T(8,128)S(1)}, u32[]{:S(2)}, u32[]{:S(2)}) async-start(f32[16,32,128]{2,1,0:T(8,128)} %broadcast_in_dim.34), calls=%async_computation.1 | async-start | bytes 524288 | tf_op jit(solution)/shard_map/all_to_all | solution.py:25
  380.5 12.6 %copy-start.4 = (pred[6400]{0:T(1024)(128)(4,1)S(1)}, pred[6400]{0:T(1024)(128)(4,1)}, u32[]{:S(2)}) copy-start(pred[6400]{0:T(1024)(128)(4,1)} %copy-done.3) | copy-start | bytes 19204
  402.6 11.0 %all-to-all-start.2 = ((f32[16,32,128]{2,1,0:T(8,128)}), f32[16,32,128]{2,1,0:T(8,128)S(1)}, u32[]{:S(2)}, u32[]{:S(2)}) async-start(f32[16,32,128]{2,1,0:T(8,128)} %broadcast_in_dim.35), calls=%async_computation.2 | async-start | bytes 524288 | tf_op jit(solution)/shard_map/all_to_all | solution.py:25
  432.9 58.3 %copy-start.2 = (f32[16,16]{1,0:T(8,128)S(1)}, f32[16,16]{1,0:T(8,128)}, u32[]{:S(2)}) copy-start(f32[16,16]{1,0:T(8,128)} %fusion.32) | copy-start | bytes 3076
Sparse Core Ops, SparseCore 0:
  10.1 73.9 all-gather.1
where the time goes:
time: 785 us; the launch traced here: 772 us
  other arithmetic  406 us (52%)
  local copies, waits for them, and re-layouts  220 us (28%)
  waiting for transfers between devices  56.9 us (7%)
  blocking collectives  46.5 us (6%)
  starting transfers between devices  17 us (2%)
  between operations  14.4 us (2%)
  matrix products  10.8 us (1%)
    div x3, other arithmetic, lower_inverse(): inverse_rows.append(running / lower[target, target])  255 us
    gather x8, local copies, waits for them, and re-layouts, one_block(): other_rows = jnp.take(rows_all, indices.reshape(-1), axis=0)  152 us
    convert_element_type x4, other arithmetic, pair_moments(): partner = other_rows.reshape(NB, row_count, 2, RAD, ANG).astype(jnp.float32)  59.1 us
    reduce_sum x4, other arithmetic, pair_moments(): jnp.sum(own_real * partner_real + own_imag * partner_imag, axis=2)  50.6 us
    psum x4, blocking collectives, one_axis_at_a_time(): return functools.reduce(lax.psum, axes, array)  46.5 us
    gather x3, local copies, waits for them, and re-layouts, shards(): jnp.take(whole, in_group.reshape(-1), axis=1)  37.8 us
    all_gather x1, waiting for transfers between devices, shards(): rows_all = lax.all_gather(coefficients, REP, axis=0, tiled=True)  36.8 us
    all_to_all x3, waiting for transfers between devices, sent_to_all(): lax.all_to_all(jnp.broadcast_to(array[None], (peers, *array.shape)), axis...  19.4 us
  transfers between devices with their start and end apart: 4, of which 4 were waited for; matrix products, arithmetic and copies ran while one was open for 3% of the time, Pallas kernels for 0%

commit v1 on v0

v1 whole, which is shorter than its diff:
```python
import functools

import jax
import jax.numpy as jnp
from jax import lax
from jax.experimental import pallas as pl
from jax.experimental.pallas import tpu as pltpu
from jax.sharding import Mesh
from jax.sharding import PartitionSpec as P

ANG = 64
RAD = 16
NB = 50
NBP = 56
VEC = 16
PD = 128
CAP = 64
CW = 2048
XW = CW + 128
PEERS = 16
PAIRS = PEERS // 2
GRP = ("grp_0", "grp_1")
REP = ("rep_0", "rep_1")
GRP_REP = ("grp_0", "grp_1", "rep_0", "rep_1")
EPS = 1e-06
F32 = jnp.float32
BF16 = jnp.bfloat16
HIGHEST = lax.Precision.HIGHEST

NT = (((1,), (1,)), ((), ()))
TN = (((0,), (0,)), ((), ()))


def iota(shape, dim):
    return lax.broadcasted_iota(jnp.int32, shape, dim)


def one_hot(cond):
    return jnp.where(cond, 1.0, 0.0).astype(BF16)


def three_parts(x):
    high = x.astype(BF16)
    rest = x - high.astype(F32)
    mid = rest.astype(BF16)
    low = (rest - mid.astype(F32)).astype(BF16)
    return jnp.concatenate([high, mid, low], axis=0)


def exact_select(x, selector, dims=(((1,), (0,)), ((), ()))):
    rows = x.shape[0]
    parts = lax.dot_general(three_parts(x), selector, dims, preferred_element_type=F32)
    return parts[:rows] + (parts[rows : 2 * rows] + parts[2 * rows :])


def kept_rows(trunc_ref, rows, lanes):
    row = iota((rows, lanes), 0) % RAD
    kept = jnp.zeros((rows, lanes), jnp.int32)
    for q in range(RAD):
        kept = jnp.where(row == q, trunc_ref[q], kept)
    return kept


def slot_kernel(where_ref, nb_ref, code_ref, lists_ref, req_ref, nbp_ref, a_ref, b_ref):
    nbp_ref[...] = jnp.full((NBP, PD), -1, jnp.int32)
    nbp_ref[:NB, :] = nb_ref[...] - where_ref[0]
    local = nbp_ref[...]
    me = where_ref[1]
    owner = local >> 7
    within = local & (PD - 1)
    remote = (owner != me) & (local >= 0)
    owner = jnp.where(remote, owner, -1)
    masks = [one_hot(owner == p) for p in range(PEERS)]
    before = one_hot(iota((NBP, NBP), 0) > iota((NBP, NBP), 1))
    in_column = jnp.dot(before, jnp.concatenate(masks, axis=1), preferred_element_type=F32)
    totals = jnp.concatenate(
        [jnp.sum(m.astype(F32), axis=0, keepdims=True) for m in masks], axis=0
    )
    left = one_hot(iota((PD, PD), 0) < iota((PD, PD), 1))
    columns = jnp.dot(totals.astype(BF16), left, preferred_element_type=F32)
    rank = jnp.zeros((NBP, PD), F32)
    for p in range(PEERS):
        here = in_column[:, p * PD : (p + 1) * PD] + columns[p : p + 1, :]
        rank = jnp.where(owner == p, here, rank)
    rank = rank.astype(jnp.int32)
    code = jnp.where(remote, owner * CAP + rank, -1)
    code_ref[...] = code
    pair = code >> 7
    lane = jnp.where(remote, code & (PD - 1), -1)
    particle = iota((1, PD), 1).astype(F32) + 1.0
    rows8 = iota((PAIRS, PD), 0)
    rows128 = iota((PD, PD), 0)
    for n in range(NB):
        mine = rows8 == pair[n : n + 1, :]
        names = within[n : n + 1, :].astype(F32)
        both = jnp.concatenate(
            [jnp.where(mine, names, 0.0), jnp.where(mine, particle, 0.0)], axis=0
        )
        a_ref[:, n * PD : (n + 1) * PD] = both.astype(BF16)
        b_ref[:, n * PD : (n + 1) * PD] = one_hot(rows128 == lane[n : n + 1, :])
    lists = lax.dot_general(a_ref[...], b_ref[...], NT, preferred_element_type=F32)
    lists_ref[...] = lists
    turned = pltpu.roll(lists[:PAIRS], CAP, 1)
    for p in range(PEERS):
        row = (turned if p % 2 else lists)[p // 2 : p // 2 + 1, :]
        req_ref[p] = jnp.broadcast_to(row, (8, PD))


def wanted_row(rx_ref, r):
    even = rx_ref[2 * r][:1, :]
    odd = pltpu.roll(rx_ref[2 * r + 1], CAP, 1)[:1, :]
    return jnp.where(iota((1, PD), 1) < CAP, even, odd).astype(jnp.int32)


def pick_kernel(rx_ref, coef_ref, init_ref, out_ref, x_ref):
    r = pl.program_id(0)

    @pl.when(r == 0)
    def _():
        x_ref[:, :CW] = coef_ref[...]
        parts = three_parts(init_ref[...]).astype(F32)
        parts = jnp.concatenate([parts, jnp.zeros((32, PD), F32)], axis=0)
        x_ref[:, CW:] = parts.T.astype(BF16)

    row = jnp.broadcast_to(wanted_row(rx_ref, r), (PD, PD)).astype(F32).T
    pick = one_hot(row.astype(jnp.int32) == iota((PD, PD), 1))
    rows = jnp.dot(pick, x_ref[...], preferred_element_type=F32)
    out_ref[...] = rows.astype(BF16).reshape(2, CAP, XW)


def own_kernel(trunc_ref, coef_ref, e_ref, re_ref, im_ref, xt_ref, s_ref):
    for c in range(CW // PD):
        block = coef_ref[:, c * PD : (c + 1) * PD].astype(F32)
        xt_ref[c * PD : (c + 1) * PD, :] = block.T
    kept = kept_rows(trunc_ref, 2 * RAD, PD)

    def per_frequency(k, carry):
        rows = xt_ref[pl.ds(k, 2 * RAD, stride=ANG), :]
        masked = jnp.where(kept > k, rows, 0.0)
        turned = jnp.concatenate([masked[RAD:], -masked[:RAD]], axis=0)
        right = jnp.concatenate([masked, turned], axis=1).astype(BF16)
        s_ref[k] = lax.dot_general(
            rows.astype(BF16), right, TN, preferred_element_type=F32
        )
        return carry

    lax.fori_loop(0, ANG, per_frequency, 0, unroll=4)

    def per_rows(b, carry):
        sub = pl.ds(b * 8, 8)
        last_re = s_ref[0, sub, :PD]
        energy = last_re * last_re
        re = s_ref[1, sub, :PD]
        im = s_ref[1, sub, PD:]
        half = re * re + im * im
        first_re = last_re * re
        first_im = last_re * im
        m_re = jnp.zeros_like(re)
        m_im = jnp.zeros_like(re)
        for k in range(2, ANG):
            next_re = s_ref[k, sub, :PD]
            next_im = s_ref[k, sub, PD:]
            half = half + (next_re * next_re + next_im * next_im)
            m_re = m_re + (re * next_re + im * next_im)
            m_im = m_im + (im * next_re - re * next_im)
            re, im = next_re, next_im
        e_ref[sub, :] = energy + 0.5 * half
        re_ref[sub, :] = first_re + 0.5 * m_re
        im_ref[sub, :] = 0.5 * m_im - first_im
        return carry

    lax.fori_loop(0, PD // 8, per_rows, 0)


def far_kernel(trunc_ref, lists_ref, coef_ref, recv_ref, table_ref, cur_ref, own_ref):
    r = pl.program_id(0)

    @pl.when(r == 0)
    def _():
        lane = iota((1, PD), 1)
        for c in range(CW // PD):
            q = (2 * c) % RAD
            kept = jnp.where(lane < ANG, trunc_ref[q], trunc_ref[q + 1])
            block = coef_ref[:, c * PD : (c + 1) * PD].astype(F32)
            own_ref[:, c * PD : (c + 1) * PD] = jnp.where(
                (lane & (ANG - 1)) < kept, block, 0.0
            ).astype(BF16)

    particle = lists_ref[pl.ds(PAIRS + r, 1), :]
    row = jnp.broadcast_to(particle, (PD, PD)).T.astype(jnp.int32)
    pick = one_hot(row == iota((PD, PD), 1) + 1)
    other = recv_ref[...].reshape(PD, XW)
    sum_re = jnp.zeros((PD, PD), F32)
    sum_im = jnp.zeros((PD, PD), F32)
    half = CW // 2
    for c in range(half // PD):
        lo = slice(c * PD, (c + 1) * PD)
        hi = slice(half + c * PD, half + (c + 1) * PD)
        a_re = jnp.dot(pick, own_ref[:, lo], preferred_element_type=F32)
        a_im = jnp.dot(pick, own_ref[:, hi], preferred_element_type=F32)
        b_re = other[:, lo].astype(F32)
        b_im = other[:, hi].astype(F32)
        sum_re = sum_re + (a_re * b_re + a_im * b_im)
        sum_im = sum_im + (a_im * b_re - a_re * b_im)
    s_re = sum_re.T
    s_im = sum_im.T
    s_re = s_re[:ANG] + s_re[ANG:]
    s_im = s_im[:ANG] + s_im[ANG:]
    power = s_re * s_re + s_im * s_im
    freq = iota((ANG, PD), 0)
    next_re = pltpu.roll(s_re, ANG - 1, 0)
    next_im = pltpu.roll(s_im, ANG - 1, 0)
    zero_re = s_re[:1]
    energy = zero_re * zero_re + 0.5 * jnp.sum(
        jnp.where(freq == 0, 0.0, power), axis=0, keepdims=True
    )
    inner = (freq > 0) & (freq < ANG - 1)
    m_re = zero_re * s_re[1:2] + 0.5 * jnp.sum(
        jnp.where(inner, s_re * next_re + s_im * next_im, 0.0), axis=0, keepdims=True
    )
    m_im = 0.5 * jnp.sum(
        jnp.where(inner, s_im * next_re - s_re * next_im, 0.0), axis=0, keepdims=True
    ) - zero_re * s_im[1:2]
    table_ref[0] = jnp.concatenate(
        [energy, m_re, m_im, jnp.zeros((5, PD), F32)], axis=0
    )
    parts = other[:, CW:].astype(F32).T
    cur_ref[0] = parts[:32] + (parts[32:64] + parts[64:96])


def near_image(cur, w_re, w_im):
    weights = jnp.concatenate([w_re, w_im], axis=1)
    both = jnp.dot(cur, weights, precision=HIGHEST, preferred_element_type=F32)
    re = both[:VEC, :PD] - both[VEC:, PD:]
    im = both[VEC:, :PD] + both[:VEC, PD:]
    return jnp.concatenate([re, im], axis=0)


def far_image(slots, table_ref, lists_ref):
    values = []
    picks = []
    for r in range(PAIRS):
        m_re = table_ref[r, 1:2, :]
        m_im = table_ref[r, 2:3, :]
        c_re, c_im = slots[r][:VEC], slots[r][VEC:]
        values.append(
            jnp.concatenate([m_re * c_re - m_im * c_im, m_re * c_im + m_im * c_re], axis=0)
        )
        particle = lists_ref[PAIRS + r : PAIRS + r + 1, :].astype(jnp.int32)
        picks.append(one_hot(iota((PD, PD), 0) + 1 == particle))
    return exact_select(
        jnp.concatenate(values, axis=1), jnp.concatenate(picks, axis=1), NT
    )


def send_columns(cur, rx_ref, out_ref):
    picks = [one_hot(iota((PD, PD), 0) == wanted_row(rx_ref, r)) for r in range(PAIRS)]
    columns = exact_select(cur, jnp.concatenate(picks, axis=1))
    first = iota((VEC, PD), 1) < CAP
    for r in range(PAIRS):
        re = columns[:VEC, r * PD : (r + 1) * PD]
        im = columns[VEC:, r * PD : (r + 1) * PD]
        out_ref[2 * r] = jnp.where(first, re, pltpu.roll(im, CAP, 1))
        out_ref[2 * r + 1] = jnp.where(first, pltpu.roll(re, CAP, 1), im)


def received_columns(recv_ref):
    first = iota((VEC, PD), 1) < CAP
    slots = []
    for r in range(PAIRS):
        even = recv_ref[2 * r]
        odd = recv_ref[2 * r + 1]
        re = jnp.where(first, even, pltpu.roll(odd, CAP, 1))
        im = jnp.where(first, pltpu.roll(even, CAP, 1), odd)
        slots.append(jnp.concatenate([re, im], axis=0))
    return slots


def first_kernel(
    where_ref, nb_ref, code_ref, lists_ref, table_ref, e_ref, re_ref, im_ref,
    slots_ref, init_ref, rx_ref,
    align_ref, weights_ref, degree_ref, cur_ref, send_ref, near_ref,
):
    local = nb_ref[...] - where_ref[0]
    near = (local >> 7) == where_ref[1]
    near_ref[...] = jnp.where(near, local & (PD - 1), -1)
    rows = iota((PD, PD), 0)
    counts = jnp.zeros((PD, PD), F32)
    energy = []
    m_re = []
    m_im = []
    for n in range(NB):
        mine = rows == near_ref[n : n + 1, :]
        counts = counts + jnp.where(mine, 1.0, 0.0)
        energy.append(jnp.sum(jnp.where(mine, e_ref[...], 0.0), axis=0, keepdims=True))
        m_re.append(jnp.sum(jnp.where(mine, re_ref[...], 0.0), axis=0, keepdims=True))
        m_im.append(jnp.sum(jnp.where(mine, im_ref[...], 0.0), axis=0, keepdims=True))
    pad = [jnp.zeros((NBP - NB, PD), F32)]
    values = [jnp.concatenate(v + pad, axis=0) for v in (energy, m_re, m_im)]
    code = code_ref[...]
    pair = code >> 7
    lane = code & (PD - 1)
    for r in range(PAIRS):
        mine = pair == r
        for v in range(3):
            row = jnp.broadcast_to(table_ref[r, v : v + 1, :], (NBP, PD))
            found = jnp.take_along_axis(row, lane, axis=1, mode="promise_in_bounds")
            values[v] = jnp.where(mine, found, values[v])
    below = values[0] + EPS
    align_ref[0] = (values[1] / below)[:NB]
    align_ref[1] = (values[2] / below)[:NB]
    degree = EPS + jnp.sum(values[0], axis=0, keepdims=True)
    degree_ref[...] = jnp.broadcast_to(degree, (8, PD))
    w_re = counts * re_ref[...]
    w_im = counts * im_ref[...]
    weights_ref[0] = w_re
    weights_ref[1] = w_im
    slots = [slots_ref[r] for r in range(PAIRS)]
    image = near_image(init_ref[...], w_re, w_im) + far_image(slots, table_ref, lists_ref)
    image = image / degree
    cur_ref[...] = image
    send_columns(image, rx_ref, send_ref)


def next_image(recv_ref, cur_ref, weights_ref, degree_ref, table_ref, lists_ref):
    slots = received_columns(recv_ref)
    image = near_image(cur_ref[...], weights_ref[0], weights_ref[1])
    image = image + far_image(slots, table_ref, lists_ref)
    return image / degree_ref[:1, :]


def middle_kernel(
    recv_ref, cur_ref, weights_ref, degree_ref, table_ref, lists_ref, rx_ref,
    out_ref, send_ref,
):
    image = next_image(recv_ref, cur_ref, weights_ref, degree_ref, table_ref, lists_ref)
    out_ref[...] = image
    send_columns(image, rx_ref, send_ref)


def last_kernel(
    total, recv_ref, cur_ref, weights_ref, degree_ref, table_ref, lists_ref,
    out_ref, gram_ref,
):
    image = next_image(recv_ref, cur_ref, weights_ref, degree_ref, table_ref, lists_ref)
    out_ref[...] = image
    gram = lax.dot_general(
        image[:VEC], image[:VEC], NT, precision=HIGHEST, preferred_element_type=F32
    ) + lax.dot_general(
        image[VEC:], image[VEC:], NT, precision=HIGHEST, preferred_element_type=F32
    )
    gram = gram * (1.0 / total)
    wide = jnp.concatenate([gram] * 8, axis=1)
    mine = iota((VEC, PD), 1) // VEC == iota((VEC, PD), 0) % 8
    wide = jnp.where(mine, wide, 0.0)
    packed = jnp.concatenate(
        [
            jnp.sum(wide[:8], axis=0, keepdims=True),
            jnp.sum(wide[8:], axis=0, keepdims=True),
        ],
        axis=0,
    )
    gram_ref[...] = jnp.broadcast_to(packed[None], gram_ref.shape)


def finish_kernel(grams_ref, cur_ref, out_ref):
    packed = jnp.sum(grams_ref[...], axis=0)
    row = iota((VEC, PD), 0)
    lane = iota((VEC, PD), 1)
    wide = jnp.where(row < 8, packed[0:1, :], packed[1:2, :])
    wide = jnp.where(lane // VEC == row % 8, wide, 0.0)
    for shift in (64, 32, 16):
        wide = wide + pltpu.roll(wide, shift, 1)
    gram = wide
    re = cur_ref[:VEC, :]
    im = cur_ref[VEC:, :]
    for c in range(VEC):
        pivot = gram[c : c + 1, c : c + 1]
        scale = lax.rsqrt(pivot)
        scale = scale * (1.5 - 0.5 * pivot * scale * scale)
        column = gram[:, c : c + 1] * scale
        column = jnp.where(row[:, :1] > c, column, 0.0)
        top_gram = gram[c : c + 1, :] * scale
        top_re = re[c : c + 1, :] * scale
        top_im = im[c : c + 1, :] * scale
        here = row == c
        gram = gram - column * top_gram
        re = jnp.where(here, top_re, re - column * top_re)
        im = jnp.where(here, top_im, im - column * top_im)
    out_ref[:VEC, :] = re
    out_ref[VEC:, :] = im


def struct(shape, dtype=F32):
    return jax.ShapeDtypeStruct(shape, dtype)


SMEM = pl.BlockSpec(memory_space=pltpu.SMEM)
VMEM = pl.BlockSpec(memory_space=pltpu.VMEM)


def shards(coefficients, truncation, neighbours, initial):
    groups = lax.axis_size(GRP)
    replicas = lax.axis_size(REP)
    devices = groups * replicas
    place = jnp.stack(
        [lax.axis_index(GRP) * (replicas * PD), lax.axis_index(REP)]
    ).astype(jnp.int32)
    code, lists, requests = pl.pallas_call(
        slot_kernel,
        out_shape=(
            struct((NBP, PD), jnp.int32),
            struct((2 * PAIRS, PD)),
            struct((PEERS, 8, PD)),
        ),
        in_specs=[SMEM, VMEM],
        scratch_shapes=[
            pltpu.VMEM((NBP, PD), jnp.int32),
            pltpu.VMEM((2 * PAIRS, NB * PD), BF16),
            pltpu.VMEM((PD, NB * PD), BF16),
        ],
        name="slots",
    )(place, neighbours)
    asked = lax.all_to_all(requests, REP, 0, 0, tiled=True)
    e_own, re_own, im_own = pl.pallas_call(
        own_kernel,
        out_shape=(struct((PD, PD)),) * 3,
        in_specs=[SMEM, VMEM],
        scratch_shapes=[
            pltpu.VMEM((CW, PD), F32),
            pltpu.VMEM((ANG, PD, 2 * PD), F32),
        ],
        cost_estimate=pl.CostEstimate(
            flops=20_000_000_000, bytes_accessed=1_000_000, transcendentals=0
        ),
        name="own",
    )(truncation, coefficients)
    whole = lambda *shape: pl.BlockSpec(shape, lambda r: (0,) * len(shape))
    sent = pl.pallas_call(
        pick_kernel,
        grid=(PAIRS,),
        out_shape=struct((PEERS, CAP, XW), BF16),
        in_specs=[whole(PEERS, 8, PD), whole(PD, CW), whole(32, PD)],
        out_specs=pl.BlockSpec((2, CAP, XW), lambda r: (r, 0, 0)),
        scratch_shapes=[pltpu.VMEM((PD, XW), BF16)],
        name="pick",
    )(asked, coefficients, initial)
    received = lax.all_to_all(sent, REP, 0, 0, tiled=True)
    table, slots = pl.pallas_call(
        far_kernel,
        grid=(PAIRS,),
        out_shape=(struct((PAIRS, 8, PD)), struct((PAIRS, 32, PD))),
        in_specs=[
            SMEM,
            whole(2 * PAIRS, PD),
            whole(PD, CW),
            pl.BlockSpec((2, CAP, XW), lambda r: (r, 0, 0)),
        ],
        out_specs=(
            pl.BlockSpec((1, 8, PD), lambda r: (r, 0, 0)),
            pl.BlockSpec((1, 32, PD), lambda r: (r, 0, 0)),
        ),
        scratch_shapes=[pltpu.VMEM((PD, CW), BF16)],
        name="far",
    )(truncation, lists, coefficients, received)
    alignment, weights, degree, current, columns = pl.pallas_call(
        first_kernel,
        out_shape=(
            struct((2, NB, PD)),
            struct((2, PD, PD)),
            struct((8, PD)),
            struct((32, PD)),
            struct((PEERS, VEC, PD)),
        ),
        in_specs=[SMEM] + [VMEM] * 10,
        scratch_shapes=[pltpu.VMEM((NB, PD), jnp.int32)],
        name="first",
    )(
        place, neighbours, code, lists, table, e_own, re_own, im_own,
        slots, initial, asked,
    )
    columns = lax.all_to_all(columns, REP, 0, 0, tiled=True)
    current, columns = pl.pallas_call(
        middle_kernel,
        out_shape=(struct((32, PD)), struct((PEERS, VEC, PD))),
        name="middle",
    )(columns, current, weights, degree, table, lists, asked)
    columns = lax.all_to_all(columns, REP, 0, 0, tiled=True)
    current, gram = pl.pallas_call(
        functools.partial(last_kernel, float(PD * devices)),
        out_shape=(struct((32, PD)), struct((devices, 2, PD))),
        name="last",
    )(columns, current, weights, degree, table, lists)
    grams = lax.all_to_all(gram, GRP_REP, 0, 0, tiled=True)
    vectors = pl.pallas_call(
        finish_kernel, out_shape=struct((32, PD)), name="finish"
    )(grams, current)
    return (alignment, vectors)


def solution(mesh):
    split = Mesh(mesh.devices.reshape(4, 2, 4, 4), GRP_REP)
    in_specs = (P(GRP_REP, None), P(), P(None, GRP_REP), P(None, GRP_REP))
    out_specs = (P(None, None, GRP_REP), P(None, GRP_REP))
    return jax.shard_map(
        shards, mesh=split, in_specs=in_specs, out_specs=out_specs, check_vma=False
    )
```

time: 785 us -> 157 us (0.20); the launches traced: 772 us -> 156 us
  other arithmetic: 406 us -> 0.66 us
  local copies, waits for them, and re-layouts: 220 us -> 2.11 us
  Pallas kernels: 0 us -> 37.1 us
  between operations: 14.4 us -> 0.66 us
  matrix products: 10.8 us -> 0 us
  blocking collectives: 46.5 us -> 37 us
    div x8 -> x0, other arithmetic: 255 us -> none  [the longest x3 255 us: lower_inverse(): inverse_rows.append(running / lower[target, target])]
    gather x11 -> x0, local copies, waits for them, and re-layouts: 190 us -> none  [the longest x8 152 us: one_block(): other_rows = jnp.take(rows_all, indices.reshape(-1), axis=0)]
    convert_element_type x13 -> x0, other arithmetic: 63.7 us -> none  [the longest x4 59.1 us: pair_moments(): partner = other_rows.reshape(NB, row_count, 2, RAD, ANG).astype(jnp.float32)]
    reduce_sum x8 -> x0, other arithmetic: 60.1 us -> none  [the longest x4 50.6 us: pair_moments(): jnp.sum(own_real * partner_real + own_imag * partner_imag, axis=2)]
    psum x4 -> x0, blocking collectives: 46.5 us -> none  [one_axis_at_a_time(): return functools.reduce(lax.psum, axes, array)]
    all_to_all x3 -> x2, waiting for transfers between devices: 19.4 us -> 63.6 us  [the longest x1 54.8 us: shards(): received = lax.all_to_all(sent, REP, 0, 0, tiled=True)]
    pallas_call x0 -> x8, Pallas kernels: none -> 37.1 us  [the longest x1 8.4 us: shards(): pl.pallas_call(own_kernel, out_shape=(struct((PD, PD)),) * 3, in_specs=[S...]
    all_to_all x0 -> x3, blocking collectives: none -> 37 us  [the longest x2 22 us: shards(): columns = lax.all_to_all(columns, REP, 0, 0, tiled=True)]
  transfers between devices with their start and end apart: 4 -> 2, of which waited for: 4 -> 2; matrix products, arithmetic and copies ran while one was open for 3% -> 1% of each run, Pallas kernels for 0% -> 5%
where the time goes in v1:
time: 157 us; the launch traced here: 156 us
  waiting for transfers between devices  63.6 us (41%)
  Pallas kernels  37.1 us (24%)
  blocking collectives  37 us (24%)
  starting transfers between devices  15.3 us (10%)
  local copies, waits for them, and re-layouts  2.11 us (1%)
    all_to_all x1, waiting for transfers between devices, shards(): received = lax.all_to_all(sent, REP, 0, 0, tiled=True)  54.8 us
    all_to_all x2, blocking collectives, shards(): columns = lax.all_to_all(columns, REP, 0, 0, tiled=True)  22 us
    all_to_all x1, blocking collectives, shards(): asked = lax.all_to_all(requests, REP, 0, 0, tiled=True)  15 us
    all_to_all x1, starting transfers between devices, shards(): grams = lax.all_to_all(gram, GRP_REP, 0, 0, tiled=True)  10.7 us
    all_to_all x1, waiting for transfers between devices, shards(): grams = lax.all_to_all(gram, GRP_REP, 0, 0, tiled=True)  8.72 us
    pallas_call x1, Pallas kernels, shards(): pl.pallas_call(own_kernel, out_shape=(struct((PD, PD)),) * 3, in_specs=[S...  8.4 us
    pallas_call x1, Pallas kernels, shards(): pl.pallas_call(far_kernel, grid=(PAIRS,), out_shape=(struct((PAIRS, 8, PD...  8.17 us
    pallas_call x1, Pallas kernels, shards(): pl.pallas_call(pick_kernel, grid=(PAIRS,), out_shape=struct((PEERS, CAP,...  6.59 us
  transfers between devices with their start and end apart: 2, of which 2 were waited for; matrix products, arithmetic and copies ran while one was open for 1% of the time, Pallas kernels for 5%

profile of v1, /device:TPU:1, one launch (start us, length us, event | category | flops | bytes accessed | tf_op | source)
XLA Modules:
  0.0 156.4 jit_solution(15932975245647778610)
XLA Ops:
  0.6 0.7 pad_add_fusion.where_ref
  1.3 2.4 %slots.1 = (s32[56,128]{1,0:T(8,128)}, f32[16,128]{1,0:T(8,128)}, f32[16,8,128]{2,1,0:T(8,128)}) custom-call(s32[2]{0:T(128)} %pad_add_fusion.where_ref, s32[50,128]{1,0:T(8,128)} %nb_ref.3), custom_call_target="tpu_custom_call" | custom-call | tf_op jit(solution)/shard_map/slots/pallas_call | solution.py:409
  3.7 15.0 %all_to_all.25.rx_ref = f32[16,8,128]{2,1,0:T(8,128)} all-to-all(f32[16,8,128]{2,1,0:T(8,128)} %get-tuple-element.21), channel_id=1, replica_groups=mesh['grp_0'=4,'grp_1'=2,'rep_0'=4,'rep_1'=4] {'rep_0','rep_1'}, dimensions={0} | all-to-all | bytes 131072 | tf_op jit(solution)/shard_map/all_to_all | solution.py:424
  18.8 6.6 %pick.1 = bf16[16,64,2176]{2,1,0:T(8,128)(2,1)} custom-call(f32[16,8,128]{2,1,0:T(8,128)} %all_to_all.25.rx_ref, bf16[128,2048]{1,0:T(8,128)(2,1)} %coef_ref.5, f32[32,128]{1,0:T(8,128)} %init_ref.3), custom_call_target="tpu_custom_call" | custom-call | tf_op jit(solution)/shard_map/pick/pallas_call | solution.py:439
  25.4 4.6 %all-to-all-start.1 = ((bf16[16,64,2176]{2,1,0:T(8,128)(2,1)}), bf16[16,64,2176]{2,1,0:T(8,128)(2,1)}, u32[]{:S(2)}, u32[]{:S(2)}) async-start(bf16[16,64,2176]{2,1,0:T(8,128)(2,1)} %pick.1), calls=%async_computation.1 | async-start | bytes 8912896 | tf_op jit(solution)/shard_map/all_to_all | solution.py:448
  29.9 8.4 %own.1 = (f32[128,128]{1,0:T(8,128)}, f32[128,128]{1,0:T(8,128)}, f32[128,128]{1,0:T(8,128)}) custom-call(s32[16]{0:T(128)} %trunc_ref.3, bf16[128,2048]{1,0:T(8,128)(2,1)} %coef_ref.5), custom_call_target="tpu_custom_call" | custom-call | flops 20000000000 | bytes 1000000 | tf_op jit(solution)/shard_map/own/pallas_call | solution.py:425
  38.3 54.8 %all-to-all-done.1.recv_ref = bf16[16,64,2176]{2,1,0:T(8,128)(2,1)} async-done(((bf16[16,64,2176]{2,1,0:T(8,128)(2,1)}), bf16[16,64,2176]{2,1,0:T(8,128)(2,1)}, u32[]{:S(2)}, u32[]{:S(2)}) %all-to-all-start.1) | async-done | bytes 4456480 | tf_op jit(solution)/shard_map/all_to_all | solution.py:448
  93.1 8.2 %far.1 = (f32[8,8,128]{2,1,0:T(8,128)}, f32[8,32,128]{2,1,0:T(8,128)}) custom-call(s32[16]{0:T(128)} %trunc_ref.3, f32[16,128]{1,0:T(8,128)} %get-tuple-element.20.lists_ref, bf16[128,2048]{1,0:T(8,128)(2,1)} %coef_ref.5, bf16[16,64,2176]{2,1,0:T(8,128)(2,1)} %all-to-all-done.1.recv_ref), custom_call_target="tpu_custom_call" | custom-call | tf_op jit(solution)/shard_map/far/pallas_call | solution.py:449
  101.3 3.8 %first.1 = (f32[2,50,128]{2,1,0:T(8,128)}, f32[2,128,128]{2,1,0:T(8,128)}, f32[8,128]{1,0:T(8,128)}, f32[32,128]{1,0:T(8,128)}, f32[16,16,128]{2,1,0:T(8,128)}) custom-call(s32[2]{0:T(128)} %pad_add_fusion.where_ref, s32[50,128]{1,0:T(8,128)} %nb_ref.3, s32[56,128]{1,0:T(8,128)} %get-tuple-element.19.code_ref, f32[16,128]{1,0:T(8,128)} %get-tuple-element.20.lists_ref, ...), custom_call_target="tpu_custom_call" | custom-call | tf_op jit(solution)/shard_map/first/pallas_call | solution.py:466
  105.1 11.0 %all_to_all.26.recv_ref = f32[16,16,128]{2,1,0:T(8,128)} all-to-all(f32[16,16,128]{2,1,0:T(8,128)} %get-tuple-element.28), channel_id=1, replica_groups=mesh['grp_0'=4,'grp_1'=2,'rep_0'=4,'rep_1'=4] {'rep_0','rep_1'}, dimensions={0} | all-to-all | bytes 262144 | tf_op jit(solution)/shard_map/all_to_all | solution.py:482
  116.1 2.2 %middle.1 = (f32[32,128]{1,0:T(8,128)}, f32[16,16,128]{2,1,0:T(8,128)}) custom-call(f32[16,16,128]{2,1,0:T(8,128)} %all_to_all.26.recv_ref, f32[32,128]{1,0:T(8,128)} %get-tuple-element.29.cur_ref, f32[2,128,128]{2,1,0:T(8,128)} %get-tuple-element.30.weights_ref, f32[8,128]{1,0:T(8,128)} %get-tuple-element.31.degree_ref, ...), custom_call_target="tpu_custom_call" | custom-call | tf_op jit(solution)/shard_map/middle/pallas_call | solution.py:483
  118.3 11.0 %all_to_all.27.recv_ref = f32[16,16,128]{2,1,0:T(8,128)} all-to-all(f32[16,16,128]{2,1,0:T(8,128)} %get-tuple-element.32), channel_id=1, replica_groups=mesh['grp_0'=4,'grp_1'=2,'rep_0'=4,'rep_1'=4] {'rep_0','rep_1'}, dimensions={0} | all-to-all | bytes 262144 | tf_op jit(solution)/shard_map/all_to_all | solution.py:488
  129.3 2.2 %last.1 = (f32[32,128]{1,0:T(8,128)}, f32[128,2,128]{2,1,0:T(2,128)}) custom-call(f32[16,16,128]{2,1,0:T(8,128)} %all_to_all.27.recv_ref, f32[32,128]{1,0:T(8,128)} %get-tuple-element.33.cur_ref, f32[2,128,128]{2,1,0:T(8,128)} %get-tuple-element.30.weights_ref, f32[8,128]{1,0:T(8,128)} %get-tuple-element.31.degree_ref, ...), custom_call_target="tpu_custom_call" | custom-call | tf_op jit(solution)/shard_map/last/pallas_call | solution.py:489
  131.6 10.7 %all-to-all-start.4 = ((f32[128,2,128]{2,1,0:T(2,128)}), f32[128,2,128]{2,1,0:T(2,128)S(1)}, u32[]{:S(2)}, u32[]{:S(2)}) async-start(f32[128,2,128]{2,1,0:T(2,128)} %get-tuple-element.34), calls=%async_computation.4 | async-start | bytes 262144 | tf_op jit(solution)/shard_map/all_to_all | solution.py:494
  142.3 1.5 copy.6
  143.8 8.7 %all-to-all-done.4.grams_ref = f32[128,2,128]{2,1,0:T(2,128)S(1)} async-done(((f32[128,2,128]{2,1,0:T(2,128)}), f32[128,2,128]{2,1,0:T(2,128)S(1)}, u32[]{:S(2)}, u32[]{:S(2)}) %all-to-all-start.4) | async-done | bytes 131104 | tf_op jit(solution)/shard_map/all_to_all | solution.py:494
  152.5 0.0 copy-start
  152.5 0.6 copy-done
  153.1 3.2 %finish.1 = f32[32,128]{1,0:T(8,128)} custom-call(f32[128,2,128]{2,1,0:T(2,128)} %copy-done, f32[32,128]{1,0:T(8,128)} %get-tuple-element.35.cur_ref), custom_call_target="tpu_custom_call" | custom-call | tf_op jit(solution)/shard_map/finish/pallas_call | solution.py:495
Async XLA Ops:
  25.4 67.8 %all-to-all-start.1 = ((bf16[16,64,2176]{2,1,0:T(8,128)(2,1)}), bf16[16,64,2176]{2,1,0:T(8,128)(2,1)}, u32[]{:S(2)}, u32[]{:S(2)}) async-start(bf16[16,64,2176]{2,1,0:T(8,128)(2,1)} %pick.1), calls=%async_computation.1 | async-start | bytes 8912896 | tf_op jit(solution)/shard_map/all_to_all | solution.py:448
  131.6 20.9 %all-to-all-start.4 = ((f32[128,2,128]{2,1,0:T(2,128)}), f32[128,2,128]{2,1,0:T(2,128)S(1)}, u32[]{:S(2)}, u32[]{:S(2)}) async-start(f32[128,2,128]{2,1,0:T(2,128)} %get-tuple-element.34), calls=%async_computation.4 | async-start | bytes 262144 | tf_op jit(solution)/shard_map/all_to_all | solution.py:494
  152.5 0.6 copy-start

commit v2 on v1

--- a/solution.py
+++ b/solution.py
@@ -16,7 +16,10 @@
 PD = 128
 CAP = 64
 CW = 2048
-XW = CW + 128
+FULL = RAD * ANG
+LEAST = 256
+STEP = 64
+HEAD = 2 * VEC
 PEERS = 16
 PAIRS = PEERS // 2
 GRP = ("grp_0", "grp_1")
@@ -47,6 +50,12 @@
     return jnp.concatenate([high, mid, low], axis=0)
 
 
+def two_parts(x):
+    high = x.astype(BF16)
+    rest = (x - high.astype(F32)).astype(BF16)
+    return jnp.concatenate([high, rest], axis=0)
+
+
 def exact_select(x, selector, dims=(((1,), (0,)), ((), ()))):
     rows = x.shape[0]
     parts = lax.dot_general(three_parts(x), selector, dims, preferred_element_type=F32)
@@ -61,7 +70,9 @@
     return kept
 
 
-def slot_kernel(where_ref, nb_ref, code_ref, lists_ref, req_ref, nbp_ref, a_ref, b_ref):
+def slot_kernel(
+    where_ref, nb_ref, code_ref, lists_ref, names_ref, req_ref, nbp_ref, a_ref, b_ref
+):
     nbp_ref[...] = jnp.full((NBP, PD), -1, jnp.int32)
     nbp_ref[:NB, :] = nb_ref[...] - where_ref[0]
     local = nbp_ref[...]
@@ -99,33 +110,62 @@
         a_ref[:, n * PD : (n + 1) * PD] = both.astype(BF16)
         b_ref[:, n * PD : (n + 1) * PD] = one_hot(rows128 == lane[n : n + 1, :])
     lists = lax.dot_general(a_ref[...], b_ref[...], NT, preferred_element_type=F32)
-    lists_ref[...] = lists
-    turned = pltpu.roll(lists[:PAIRS], CAP, 1)
+    lists_ref[...] = lists[PAIRS:]
+    turned = pltpu.roll(lists, CAP, 1)
+    first = iota((2 * PAIRS, PD), 1) < CAP
+    both = (jnp.where(first, lists, turned), jnp.where(first, turned, lists))
     for p in range(PEERS):
-        row = (turned if p % 2 else lists)[p // 2 : p // 2 + 1, :]
-        req_ref[p] = jnp.broadcast_to(row, (8, PD))
+        rows = both[p % 2]
+        r = p // 2
+        req_ref[p] = jnp.broadcast_to(rows[r : r + 1, :], (8, PD))
+        names_ref[p : p + 1, :] = rows[PAIRS + r : PAIRS + r + 1, :]
 
 
 def wanted_row(rx_ref, r):
     even = rx_ref[2 * r][:1, :]
-    odd = pltpu.roll(rx_ref[2 * r + 1], CAP, 1)[:1, :]
+    odd = rx_ref[2 * r + 1][:1, :]
     return jnp.where(iota((1, PD), 1) < CAP, even, odd).astype(jnp.int32)
 
 
-def pick_kernel(rx_ref, coef_ref, init_ref, out_ref, x_ref):
+def pack_kernel(trunc_ref, coef_ref, init_ref, out_ref, f_ref, re_ref, im_ref):
+    init = init_ref[...]
+    parts = two_parts(jnp.concatenate([init[:VEC], init[VEC:]], axis=1))
+    out_ref[:HEAD, :] = parts
+    blocks = CW // PD
+    for c in range(blocks):
+        block = coef_ref[:, c * PD : (c + 1) * PD].astype(F32)
+        f_ref[c * PD : (c + 1) * PD, :] = block.T
+    offset = 0
+    for q in range(RAD):
+        here = pl.ds(offset, ANG)
+        re_ref[here, :] = f_ref[q * ANG : (q + 1) * ANG, :]
+        im_ref[here, :] = f_ref[(RAD + q) * ANG : (RAD + q + 1) * ANG, :]
+        offset = offset + trunc_ref[q]
+    for b in range(FULL // PD):
+        rows = slice(b * PD, (b + 1) * PD)
+        kept = iota((PD, PD), 0) + b * PD < offset
+        out_ref[HEAD + b * PD : HEAD + (b + 1) * PD, :PD] = jnp.where(
+            kept, re_ref[rows, :], 0.0
+        ).astype(BF16)
+        out_ref[HEAD + b * PD : HEAD + (b + 1) * PD, PD:] = jnp.where(
+            kept, im_ref[rows, :], 0.0
+        ).astype(BF16)
+
+
+def pick_kernel(size, rx_ref, pack_ref, out_ref):
     r = pl.program_id(0)
-
-    @pl.when(r == 0)
-    def _():
-        x_ref[:, :CW] = coef_ref[...]
-        parts = three_parts(init_ref[...]).astype(F32)
-        parts = jnp.concatenate([parts, jnp.zeros((32, PD), F32)], axis=0)
-        x_ref[:, CW:] = parts.T.astype(BF16)
-
-    row = jnp.broadcast_to(wanted_row(rx_ref, r), (PD, PD)).astype(F32).T
-    pick = one_hot(row.astype(jnp.int32) == iota((PD, PD), 1))
-    rows = jnp.dot(pick, x_ref[...], preferred_element_type=F32)
-    out_ref[...] = rows.astype(BF16).reshape(2, CAP, XW)
+    rows = iota((PD, PD), 0)
+    first = iota((PD, PD), 1) < CAP
+    sides = []
+    for p in range(2):
+        picked = rows == rx_ref[2 * r + p][:1, :].astype(jnp.int32)
+        top = one_hot(picked & first)
+        bottom = one_hot(picked & jnp.logical_not(first))
+        sides.append(jnp.concatenate([top, bottom], axis=0))
+    side = jnp.concatenate(sides, axis=1)
+    chosen = jnp.dot(pack_ref[:size, :], side, preferred_element_type=F32).astype(BF16)
+    out_ref[0] = chosen[:, :PD]
+    out_ref[1] = chosen[:, PD:]
 
 
 def own_kernel(trunc_ref, coef_ref, e_ref, re_ref, im_ref, xt_ref, s_ref):
@@ -172,42 +212,55 @@
     lax.fori_loop(0, PD // 8, per_rows, 0)
 
 
-def far_kernel(trunc_ref, lists_ref, coef_ref, recv_ref, table_ref, cur_ref, own_ref):
+def far_kernel(
+    size, trunc_ref, names_ref, pack_ref, recv_ref, table_ref, cur_ref,
+    same_ref, cross_ref, other_ref,
+):
     r = pl.program_id(0)
+    kept = size - HEAD
 
     @pl.when(r == 0)
     def _():
-        lane = iota((1, PD), 1)
-        for c in range(CW // PD):
-            q = (2 * c) % RAD
-            kept = jnp.where(lane < ANG, trunc_ref[q], trunc_ref[q + 1])
-            block = coef_ref[:, c * PD : (c + 1) * PD].astype(F32)
-            own_ref[:, c * PD : (c + 1) * PD] = jnp.where(
-                (lane & (ANG - 1)) < kept, block, 0.0
-            ).astype(BF16)
-
-    particle = lists_ref[pl.ds(PAIRS + r, 1), :]
-    row = jnp.broadcast_to(particle, (PD, PD)).T.astype(jnp.int32)
-    pick = one_hot(row == iota((PD, PD), 1) + 1)
-    other = recv_ref[...].reshape(PD, XW)
-    sum_re = jnp.zeros((PD, PD), F32)
-    sum_im = jnp.zeros((PD, PD), F32)
-    half = CW // 2
-    for c in range(half // PD):
-        lo = slice(c * PD, (c + 1) * PD)
-        hi = slice(half + c * PD, half + (c + 1) * PD)
-        a_re = jnp.dot(pick, own_ref[:, lo], preferred_element_type=F32)
-        a_im = jnp.dot(pick, own_ref[:, hi], preferred_element_type=F32)
-        b_re = other[:, lo].astype(F32)
-        b_im = other[:, hi].astype(F32)
-        sum_re = sum_re + (a_re * b_re + a_im * b_im)
-        sum_im = sum_im + (a_im * b_re - a_re * b_im)
-    s_re = sum_re.T
-    s_im = sum_im.T
-    s_re = s_re[:ANG] + s_re[ANG:]
-    s_im = s_im[:ANG] + s_im[ANG:]
+        same_ref[kept:, :] = jnp.zeros((ANG, PD), F32)
+        cross_ref[kept:, :] = jnp.zeros((ANG, PD), F32)
+        other_ref[kept:, :] = jnp.zeros((ANG, PD), F32)
+
+    first = iota((PD, PD), 1) < CAP
+    freq = iota((ANG, PD), 0)
+    halves = []
+    for p in range(2):
+        named = iota((PD, PD), 0) + 1 == names_ref[pl.ds(2 * r + p, 1), :].astype(jnp.int32)
+        low = one_hot(named & first)
+        high = one_hot(named & jnp.logical_not(first))
+        side = jnp.concatenate(
+            [
+                jnp.concatenate([low, high], axis=1),
+                jnp.concatenate([high, low], axis=1),
+            ],
+            axis=0,
+        )
+        mine = jnp.dot(pack_ref[HEAD:size, :], side, preferred_element_type=F32)
+        same_ref[:kept, :] = mine[:, :PD]
+        cross_ref[:kept, :] = mine[:, PD:]
+        other_ref[:kept, :] = recv_ref[p, HEAD:, :].astype(F32)
+        sum_re = jnp.zeros((ANG, PD), F32)
+        sum_im = jnp.zeros((ANG, PD), F32)
+        offset = 0
+        for q in range(RAD):
+            here = pl.ds(offset, ANG)
+            other = jnp.where(freq < trunc_ref[q], other_ref[here, :], 0.0)
+            sum_re = sum_re + same_ref[here, :] * other
+            sum_im = sum_im + cross_ref[here, :] * other
+            offset = offset + trunc_ref[q]
+        halves.append((sum_re, sum_im))
+        parts = recv_ref[p, :HEAD, :].astype(F32)
+        cur_ref[p] = parts[:VEC] + parts[VEC:]
+    first = first[:ANG]
+    s_re = jnp.where(first, halves[0][0], halves[1][0])
+    s_re = s_re + pltpu.roll(jnp.where(first, halves[1][0], halves[0][0]), CAP, 1)
+    s_im = pltpu.roll(jnp.where(first, halves[1][1], halves[0][1]), CAP, 1)
+    s_im = jnp.where(first, halves[0][1] - s_im, s_im - halves[1][1])
     power = s_re * s_re + s_im * s_im
-    freq = iota((ANG, PD), 0)
     next_re = pltpu.roll(s_re, ANG - 1, 0)
     next_im = pltpu.roll(s_im, ANG - 1, 0)
     zero_re = s_re[:1]
@@ -224,8 +277,6 @@
     table_ref[0] = jnp.concatenate(
         [energy, m_re, m_im, jnp.zeros((5, PD), F32)], axis=0
     )
-    parts = other[:, CW:].astype(F32).T
-    cur_ref[0] = parts[:32] + (parts[32:64] + parts[64:96])
 
 
 def near_image(cur, w_re, w_im):
@@ -246,7 +297,7 @@
         values.append(
             jnp.concatenate([m_re * c_re - m_im * c_im, m_re * c_im + m_im * c_re], axis=0)
         )
-        particle = lists_ref[PAIRS + r : PAIRS + r + 1, :].astype(jnp.int32)
+        particle = lists_ref[r : r + 1, :].astype(jnp.int32)
         picks.append(one_hot(iota((PD, PD), 0) + 1 == particle))
     return exact_select(
         jnp.concatenate(values, axis=1), jnp.concatenate(picks, axis=1), NT
@@ -315,7 +366,7 @@
     w_im = counts * im_ref[...]
     weights_ref[0] = w_re
     weights_ref[1] = w_im
-    slots = [slots_ref[r] for r in range(PAIRS)]
+    slots = received_columns(slots_ref)
     image = near_image(init_ref[...], w_re, w_im) + far_image(slots, table_ref, lists_ref)
     image = image / degree
     cur_ref[...] = image
@@ -399,30 +450,21 @@
 VMEM = pl.BlockSpec(memory_space=pltpu.VMEM)
 
 
-def shards(coefficients, truncation, neighbours, initial):
-    groups = lax.axis_size(GRP)
-    replicas = lax.axis_size(REP)
-    devices = groups * replicas
-    place = jnp.stack(
-        [lax.axis_index(GRP) * (replicas * PD), lax.axis_index(REP)]
-    ).astype(jnp.int32)
-    code, lists, requests = pl.pallas_call(
-        slot_kernel,
-        out_shape=(
-            struct((NBP, PD), jnp.int32),
-            struct((2 * PAIRS, PD)),
-            struct((PEERS, 8, PD)),
-        ),
-        in_specs=[SMEM, VMEM],
-        scratch_shapes=[
-            pltpu.VMEM((NBP, PD), jnp.int32),
-            pltpu.VMEM((2 * PAIRS, NB * PD), BF16),
-            pltpu.VMEM((PD, NB * PD), BF16),
-        ],
-        name="slots",
-    )(place, neighbours)
-    asked = lax.all_to_all(requests, REP, 0, 0, tiled=True)
-    e_own, re_own, im_own = pl.pallas_call(
+def whole(*shape):
+    return pl.BlockSpec(shape, lambda r: (0,) * len(shape))
+
+
+def exchange(size, truncation, coefficients, names, asked, packed):
+    sent = pl.pallas_call(
+        functools.partial(pick_kernel, size),
+        grid=(PAIRS,),
+        out_shape=struct((PEERS, size, PD), BF16),
+        in_specs=[whole(PEERS, 8, PD), whole(HEAD + FULL, 2 * PD)],
+        out_specs=pl.BlockSpec((2, size, PD), lambda r: (r, 0, 0)),
+        name="pick",
+    )(asked, packed)
+    received = lax.all_to_all(sent, REP, 0, 0, tiled=True)
+    own = pl.pallas_call(
         own_kernel,
         out_shape=(struct((PD, PD)),) * 3,
         in_specs=[SMEM, VMEM],
@@ -435,34 +477,72 @@
         ),
         name="own",
     )(truncation, coefficients)
-    whole = lambda *shape: pl.BlockSpec(shape, lambda r: (0,) * len(shape))
-    sent = pl.pallas_call(
-        pick_kernel,
+    far = pl.pallas_call(
+        functools.partial(far_kernel, size),
         grid=(PAIRS,),
-        out_shape=struct((PEERS, CAP, XW), BF16),
-        in_specs=[whole(PEERS, 8, PD), whole(PD, CW), whole(32, PD)],
-        out_specs=pl.BlockSpec((2, CAP, XW), lambda r: (r, 0, 0)),
-        scratch_shapes=[pltpu.VMEM((PD, XW), BF16)],
-        name="pick",
-    )(asked, coefficients, initial)
-    received = lax.all_to_all(sent, REP, 0, 0, tiled=True)
-    table, slots = pl.pallas_call(
-        far_kernel,
-        grid=(PAIRS,),
-        out_shape=(struct((PAIRS, 8, PD)), struct((PAIRS, 32, PD))),
+        out_shape=(struct((PAIRS, 8, PD)), struct((PEERS, VEC, PD))),
         in_specs=[
             SMEM,
-            whole(2 * PAIRS, PD),
-            whole(PD, CW),
-            pl.BlockSpec((2, CAP, XW), lambda r: (r, 0, 0)),
+            whole(PEERS, PD),
+            whole(HEAD + FULL, 2 * PD),
+            pl.BlockSpec((2, size, PD), lambda r: (r, 0, 0)),
         ],
         out_specs=(
             pl.BlockSpec((1, 8, PD), lambda r: (r, 0, 0)),
-            pl.BlockSpec((1, 32, PD), lambda r: (r, 0, 0)),
+            pl.BlockSpec((2, VEC, PD), lambda r: (r, 0, 0)),
         ),
-        scratch_shapes=[pltpu.VMEM((PD, CW), BF16)],
+        scratch_shapes=[pltpu.VMEM((size - HEAD + ANG, PD), F32)] * 3,
         name="far",
-    )(truncation, lists, coefficients, received)
+    )(truncation, names, packed, received)
+    return (*own, *far)
+
+
+def shards(coefficients, truncation, neighbours, initial):
+    groups = lax.axis_size(GRP)
+    replicas = lax.axis_size(REP)
+    devices = groups * replicas
+    place = jnp.stack(
+        [lax.axis_index(GRP) * (replicas * PD), lax.axis_index(REP)]
+    ).astype(jnp.int32)
+    code, lists, names, requests = pl.pallas_call(
+        slot_kernel,
+        out_shape=(
+            struct((NBP, PD), jnp.int32),
+            struct((PAIRS, PD)),
+            struct((PEERS, PD)),
+            struct((PEERS, 8, PD)),
+        ),
+        in_specs=[SMEM, VMEM],
+        scratch_shapes=[
+            pltpu.VMEM((NBP, PD), jnp.int32),
+            pltpu.VMEM((2 * PAIRS, NB * PD), BF16),
+            pltpu.VMEM((PD, NB * PD), BF16),
+        ],
+        name="slots",
+    )(place, neighbours)
+    asked = lax.all_to_all(requests, REP, 0, 0, tiled=True)
+    packed = pl.pallas_call(
+        pack_kernel,
+        out_shape=struct((HEAD + FULL, 2 * PD), BF16),
+        in_specs=[SMEM, VMEM, VMEM],
+        scratch_shapes=[
+            pltpu.VMEM((CW, PD), F32),
+            pltpu.VMEM((FULL + ANG, PD), F32),
+            pltpu.VMEM((FULL + ANG, PD), F32),
+        ],
+        cost_estimate=pl.CostEstimate(
+            flops=5_000_000_000, bytes_accessed=1_000_000, transcendentals=0
+        ),
+        name="pack",
+    )(truncation, coefficients, initial)
+    sizes = list(range(LEAST, FULL + 1, STEP))
+    total = jnp.sum(truncation)
+    which = jnp.clip((total - LEAST + STEP - 1) // STEP, 0, len(sizes) - 1)
+    e_own, re_own, im_own, table, slots = lax.switch(
+        which,
+        [functools.partial(exchange, HEAD + size) for size in sizes],
+        truncation, coefficients, names, asked, packed,
+    )
     alignment, weights, degree, current, columns = pl.pallas_call(
         first_kernel,
         out_shape=(

time: 157 us -> 132 us (0.84); the launches traced: 156 us -> 130 us
  waiting for transfers between devices: 63.6 us -> 41.2 us
  blocking collectives: 37 us -> 23.1 us
  starting transfers between devices: 15.3 us -> 22 us
    all_to_all x1 -> x2, waiting for transfers between devices: 54.8 us -> 32.5 us  [the longest x1 28.8 us: exchange(): received = lax.all_to_all(sent, REP, 0, 0, tiled=True)]
    all_to_all x1 -> x0, blocking collectives: 15 us -> none  [shards(): asked = lax.all_to_all(requests, REP, 0, 0, tiled=True)]
    all_to_all x1 -> x2, starting transfers between devices: 4.55 us -> 12.1 us  [the longest x1 8.41 us: shards(): asked = lax.all_to_all(requests, REP, 0, 0, tiled=True)]
    pallas_call x3 -> x4, Pallas kernels: 23.2 us -> 22.6 us  [the longest x1 8.42 us: exchange(): pl.pallas_call(own_kernel, out_shape=(struct((PD, PD)),) * 3, in_specs=[S...]
  transfers between devices with their start and end apart: 2 -> 3, of which waited for: 2 -> 3; matrix products, arithmetic and copies ran while one was open for 1% -> 2% of each run, Pallas kernels for 5% -> 8%
where the time goes in v2:
time: 132 us; the launch traced here: 130 us
  waiting for transfers between devices  41.2 us (31%)
  Pallas kernels  36.4 us (28%)
  blocking collectives  23.1 us (18%)
  starting transfers between devices  22 us (17%)
  local copies, waits for them, and re-layouts  3.63 us (3%)
  between operations  1.38 us (1%)
    all_to_all x1, waiting for transfers between devices, exchange(): received = lax.all_to_all(sent, REP, 0, 0, tiled=True)  28.8 us
    all_to_all x2, blocking collectives, shards(): columns = lax.all_to_all(columns, REP, 0, 0, tiled=True)  23.1 us
    all_to_all x1, starting transfers between devices, shards(): grams = lax.all_to_all(gram, GRP_REP, 0, 0, tiled=True)  9.81 us
    all_to_all x1, waiting for transfers between devices, shards(): grams = lax.all_to_all(gram, GRP_REP, 0, 0, tiled=True)  8.72 us
    pallas_call x1, Pallas kernels, exchange(): pl.pallas_call(own_kernel, out_shape=(struct((PD, PD)),) * 3, in_specs=[S...  8.42 us
    pallas_call x1, Pallas kernels, exchange(): pl.pallas_call(functools.partial(far_kernel, size), grid=(PAIRS,), out_sh...  8.42 us
    all_to_all x1, starting transfers between devices, shards(): asked = lax.all_to_all(requests, REP, 0, 0, tiled=True)  8.41 us
    pallas_call x1, Pallas kernels, exchange(): pl.pallas_call(functools.partial(pick_kernel, size), grid=(PAIRS,), out_s...  4.28 us
  transfers between devices with their start and end apart: 3, of which 3 were waited for; matrix products, arithmetic and copies ran while one was open for 2% of the time, Pallas kernels for 8%

profile of v2, /device:TPU:1, one launch (start us, length us, event | category | flops | bytes accessed | tf_op | source)
XLA Modules:
  0.0 129.6 jit_solution(1993301720515203319)
XLA Ops:
  0.6 0.6 pad_add_fusion.where_ref
  1.2 2.4 %slots.1 = (s32[56,128]{1,0:T(8,128)}, f32[8,128]{1,0:T(8,128)}, f32[16,128]{1,0:T(8,128)S(1)}, f32[16,8,128]{2,1,0:T(8,128)}) custom-call(s32[2]{0:T(128)} %pad_add_fusion.where_ref, s32[50,128]{1,0:T(8,128)} %nb_ref.3), custom_call_target="tpu_custom_call" | custom-call | tf_op jit(solution)/shard_map/slots/pallas_call | solution.py:507
  3.7 8.4 %all-to-all-start.13 = ((f32[16,8,128]{2,1,0:T(8,128)}), f32[16,8,128]{2,1,0:T(8,128)S(1)}, u32[]{:S(2)}, u32[]{:S(2)}) async-start(f32[16,8,128]{2,1,0:T(8,128)} %get-tuple-element.282), calls=%async_computation.13 | async-start | bytes 131072 | tf_op jit(solution)/shard_map/all_to_all | solution.py:523
  12.1 0.0 copy-start.8
  12.1 1.4 %pack.1 = bf16[1056,256]{1,0:T(8,128)(2,1)S(1)} custom-call(s32[16]{0:T(128)} %trunc_ref.1, bf16[128,2048]{1,0:T(8,128)(2,1)} %coef_ref.1, f32[32,128]{1,0:T(8,128)} %init_ref.3), custom_call_target="tpu_custom_call" | custom-call | flops 5000000000 | bytes 1000000 | tf_op jit(solution)/shard_map/pack/pallas_call | solution.py:524
  13.6 0.6 reduce_sum.9
  14.9 3.7 %all-to-all-done.13.rx_ref = f32[16,8,128]{2,1,0:T(8,128)S(1)} async-done(((f32[16,8,128]{2,1,0:T(8,128)}), f32[16,8,128]{2,1,0:T(8,128)S(1)}, u32[]{:S(2)}, u32[]{:S(2)}) %all-to-all-start.13) | async-done | bytes 65568 | tf_op jit(solution)/shard_map/all_to_all | solution.py:523
  18.6 55.8 %conditional.1 = (f32[128,128]{1,0:T(8,128)}, f32[128,128]{1,0:T(8,128)}, f32[128,128]{1,0:T(8,128)}, f32[8,8,128]{2,1,0:T(8,128)S(1)}, f32[16,16,128]{2,1,0:T(8,128)S(1)}) conditional(s32[]{:T(128)} %clamp.3, (s32[16]{0:T(128)S(1)}, bf16[128,2048]{1,0:T(8,128)(2,1)S(1)}, f32[16,8,128]{2,1,0:T(8,128)S(1)}, ...), branch_computations={%region_1.2_spmd, %region_2.3_spmd, %region_3.4_spmd, %region_4.5_... | conditional | flops 20000000000 | bytes 22364864 | solution.py:541
  18.6 4.3 %pick.19 = bf16[16,672,128]{2,1,0:T(8,128)(2,1)} custom-call(f32[16,8,128]{2,1,0:T(8,128)S(1)} %get-tuple-element.197.rx_ref, bf16[1056,256]{1,0:T(8,128)(2,1)S(1)} %get-tuple-element.196.pack_ref), custom_call_target="tpu_custom_call" | custom-call | tf_op jit(solution)/shard_map/cond/branch_6_fun/pick/pallas_call | solution.py:458
  22.9 3.7 %all-to-all-start.6 = ((bf16[16,672,128]{2,1,0:T(8,128)(2,1)}), bf16[16,672,128]{2,1,0:T(8,128)(2,1)S(1)}, u32[]{:S(2)}, u32[]{:S(2)}) async-start(bf16[16,672,128]{2,1,0:T(8,128)(2,1)} %pick.19), calls=%async_computation.6 | async-start | bytes 5505024 | tf_op jit(solution)/shard_map/cond/branch_6_fun/all_to_all | solution.py:466
  26.6 8.4 %own.19 = (f32[128,128]{1,0:T(8,128)}, f32[128,128]{1,0:T(8,128)}, f32[128,128]{1,0:T(8,128)}) custom-call(s32[16]{0:T(128)S(1)} %get-tuple-element.190.trunc_ref, bf16[128,2048]{1,0:T(8,128)(2,1)} %copy-done.11), custom_call_target="tpu_custom_call" | custom-call | flops 20000000000 | bytes 1000000 | tf_op jit(solution)/shard_map/cond/branch_6_fun/own/pallas_call | solution.py:467
  35.1 28.8 %all-to-all-done.6.recv_ref = bf16[16,672,128]{2,1,0:T(8,128)(2,1)S(1)} async-done(((bf16[16,672,128]{2,1,0:T(8,128)(2,1)}), bf16[16,672,128]{2,1,0:T(8,128)(2,1)S(1)}, u32[]{:S(2)}, u32[]{:S(2)}) %all-to-all-start.6) | async-done | bytes 2752544 | tf_op jit(solution)/shard_map/cond/branch_6_fun/all_to_all | solution.py:466
  63.8 1.5 %copy-done = bf16[16,672,128]{2,1,0:T(8,128)(2,1)} copy-done((bf16[16,672,128]{2,1,0:T(8,128)(2,1)}, bf16[16,672,128]{2,1,0:T(8,128)(2,1)S(1)}, u32[]{:S(2)}) %copy-start) | copy-done | bytes 2752536 | tf_op jit(solution)/shard_map/cond
  65.3 8.4 %far.19 = (f32[8,8,128]{2,1,0:T(8,128)S(1)}, f32[16,16,128]{2,1,0:T(8,128)S(1)}) custom-call(s32[16]{0:T(128)S(1)} %get-tuple-element.190.trunc_ref, f32[16,128]{1,0:T(8,128)S(1)} %get-tuple-element.195.names_ref, bf16[1056,256]{1,0:T(8,128)(2,1)S(1)} %get-tuple-element.196.pack_ref, bf16[16,672,128]{2,1,0:T(8,128)(2,1)} %copy-done), custom_call_target="tpu_custom_call" | custom-call | tf_op jit(solution)/shard_map/cond/branch_6_fun/far/pallas_call | solution.py:480
  74.4 3.7 %first.1 = (f32[2,50,128]{2,1,0:T(8,128)}, f32[2,128,128]{2,1,0:T(8,128)}, f32[8,128]{1,0:T(8,128)}, f32[32,128]{1,0:T(8,128)}, f32[16,16,128]{2,1,0:T(8,128)}) custom-call(s32[2]{0:T(128)} %pad_add_fusion.where_ref, s32[50,128]{1,0:T(8,128)} %nb_ref.3, s32[56,128]{1,0:T(8,128)} %get-tuple-element.280.code_ref, f32[8,128]{1,0:T(8,128)} %get-tuple-element.281.lists_ref, ...), custom_call_target="tpu_custom_call" | custom-call | tf_op jit(solution)/shard_map/first/pallas_call | solution.py:546
  78.2 12.1 %all_to_all.72.recv_ref = f32[16,16,128]{2,1,0:T(8,128)} all-to-all(f32[16,16,128]{2,1,0:T(8,128)} %get-tuple-element.290), channel_id=1, replica_groups=mesh['grp_0'=4,'grp_1'=2,'rep_0'=4,'rep_1'=4] {'rep_0','rep_1'}, dimensions={0} | all-to-all | bytes 262144 | tf_op jit(solution)/shard_map/all_to_all | solution.py:562
  90.3 2.2 %middle.1 = (f32[32,128]{1,0:T(8,128)}, f32[16,16,128]{2,1,0:T(8,128)}) custom-call(f32[16,16,128]{2,1,0:T(8,128)} %all_to_all.72.recv_ref, f32[32,128]{1,0:T(8,128)} %get-tuple-element.291.cur_ref, f32[2,128,128]{2,1,0:T(8,128)} %get-tuple-element.292.weights_ref, f32[8,128]{1,0:T(8,128)} %get-tuple-element.293.degree_ref, ...), custom_call_target="tpu_custom_call" | custom-call | tf_op jit(solution)/shard_map/middle/pallas_call | solution.py:563
  92.5 11.0 %all_to_all.73.recv_ref = f32[16,16,128]{2,1,0:T(8,128)} all-to-all(f32[16,16,128]{2,1,0:T(8,128)} %get-tuple-element.294), channel_id=1, replica_groups=mesh['grp_0'=4,'grp_1'=2,'rep_0'=4,'rep_1'=4] {'rep_0','rep_1'}, dimensions={0} | all-to-all | bytes 262144 | tf_op jit(solution)/shard_map/all_to_all | solution.py:568
  103.5 2.2 %last.1 = (f32[32,128]{1,0:T(8,128)}, f32[128,2,128]{2,1,0:T(2,128)}) custom-call(f32[16,16,128]{2,1,0:T(8,128)} %all_to_all.73.recv_ref, f32[32,128]{1,0:T(8,128)} %get-tuple-element.295.cur_ref, f32[2,128,128]{2,1,0:T(8,128)} %get-tuple-element.292.weights_ref, f32[8,128]{1,0:T(8,128)} %get-tuple-element.293.degree_ref, ...), custom_call_target="tpu_custom_call" | custom-call | tf_op jit(solution)/shard_map/last/pallas_call | solution.py:569
  105.7 9.8 %all-to-all-start.16 = ((f32[128,2,128]{2,1,0:T(2,128)}), f32[128,2,128]{2,1,0:T(2,128)S(1)}, u32[]{:S(2)}, u32[]{:S(2)}) async-start(f32[128,2,128]{2,1,0:T(2,128)} %get-tuple-element.296), calls=%async_computation.16 | async-start | bytes 262144 | tf_op jit(solution)/shard_map/all_to_all | solution.py:574
  115.6 1.5 %copy.6 = f32[2,50,128]{2,0,1:T(2,128)} copy(f32[2,50,128]{2,1,0:T(8,128)} %get-tuple-element.298) | data formatting | bytes 102400
  117.0 8.7 %all-to-all-done.16.grams_ref = f32[128,2,128]{2,1,0:T(2,128)S(1)} async-done(((f32[128,2,128]{2,1,0:T(2,128)}), f32[128,2,128]{2,1,0:T(2,128)S(1)}, u32[]{:S(2)}, u32[]{:S(2)}) %all-to-all-start.16) | async-done | bytes 131104 | tf_op jit(solution)/shard_map/all_to_all | solution.py:574
  125.7 0.7 copy-done.7
  126.4 3.2 %finish.1 = f32[32,128]{1,0:T(8,128)} custom-call(f32[128,2,128]{2,1,0:T(2,128)} %copy-done.7, f32[32,128]{1,0:T(8,128)} %get-tuple-element.297.cur_ref), custom_call_target="tpu_custom_call" | custom-call | tf_op jit(solution)/shard_map/finish/pallas_call | solution.py:575
  (7 shorter events, 0.0 us)
Async XLA Ops:
  3.7 14.9 %all-to-all-start.13 = ((f32[16,8,128]{2,1,0:T(8,128)}), f32[16,8,128]{2,1,0:T(8,128)S(1)}, u32[]{:S(2)}, u32[]{:S(2)}) async-start(f32[16,8,128]{2,1,0:T(8,128)} %get-tuple-element.282), calls=%async_computation.13 | async-start | bytes 131072 | tf_op jit(solution)/shard_map/all_to_all | solution.py:523
  12.1 1.5 %copy-start.8 = (s32[16]{0:T(128)S(1)}, s32[16]{0:T(128)}, u32[]{:S(2)}) copy-start(s32[16]{0:T(128)} %trunc_ref.1) | copy-start | bytes 196
  12.1 6.5 %copy-start.9 = (bf16[128,2048]{1,0:T(8,128)(2,1)S(1)}, bf16[128,2048]{1,0:T(8,128)(2,1)}, u32[]{:S(2)}) copy-start(bf16[128,2048]{1,0:T(8,128)(2,1)} %coef_ref.1) | copy-start | bytes 1572868
  18.6 4.3 %copy-start.11 = (bf16[128,2048]{1,0:T(8,128)(2,1)}, bf16[128,2048]{1,0:T(8,128)(2,1)S(1)}, u32[]{:S(2)}) copy-start(bf16[128,2048]{1,0:T(8,128)(2,1)S(1)} %get-tuple-element.191.coef_ref) | copy-start | bytes 1572868 | tf_op jit(solution)/shard_map/cond
  22.9 40.9 %all-to-all-start.6 = ((bf16[16,672,128]{2,1,0:T(8,128)(2,1)}), bf16[16,672,128]{2,1,0:T(8,128)(2,1)S(1)}, u32[]{:S(2)}, u32[]{:S(2)}) async-start(bf16[16,672,128]{2,1,0:T(8,128)(2,1)} %pick.19), calls=%async_computation.6 | async-start | bytes 5505024 | tf_op jit(solution)/shard_map/cond/branch_6_fun/all_to_all | solution.py:466
  63.8 1.5 %copy-start = (bf16[16,672,128]{2,1,0:T(8,128)(2,1)}, bf16[16,672,128]{2,1,0:T(8,128)(2,1)S(1)}, u32[]{:S(2)}) copy-start(bf16[16,672,128]{2,1,0:T(8,128)(2,1)S(1)} %all-to-all-done.6.recv_ref) | copy-start | bytes 8257540 | tf_op jit(solution)/shard_map/cond
  105.7 20.0 %all-to-all-start.16 = ((f32[128,2,128]{2,1,0:T(2,128)}), f32[128,2,128]{2,1,0:T(2,128)S(1)}, u32[]{:S(2)}, u32[]{:S(2)}) async-start(f32[128,2,128]{2,1,0:T(2,128)} %get-tuple-element.296), calls=%async_computation.16 | async-start | bytes 262144 | tf_op jit(solution)/shard_map/all_to_all | solution.py:574
  125.7 0.7 copy-start.7

commit v3 on v2

--- a/solution.py
+++ b/solution.py
@@ -17,11 +17,11 @@
 CAP = 64
 CW = 2048
 FULL = RAD * ANG
-LEAST = 256
-STEP = 64
+SIZES = (384, 512, 576, 640, 704, 768, 896, FULL)
 HEAD = 2 * VEC
 PEERS = 16
 PAIRS = PEERS // 2
+WIDE = 4
 GRP = ("grp_0", "grp_1")
 REP = ("rep_0", "rep_1")
 GRP_REP = ("grp_0", "grp_1", "rep_0", "rep_1")
@@ -127,29 +127,29 @@
     return jnp.where(iota((1, PD), 1) < CAP, even, odd).astype(jnp.int32)
 
 
-def pack_kernel(trunc_ref, coef_ref, init_ref, out_ref, f_ref, re_ref, im_ref):
+def local_kernel(
+    trunc_ref, coef_ref, init_ref, out_ref, e_ref, re_ref, im_ref,
+    f_ref, wide_re_ref, wide_im_ref, s_ref,
+):
     init = init_ref[...]
     parts = two_parts(jnp.concatenate([init[:VEC], init[VEC:]], axis=1))
     out_ref[:HEAD, :] = parts
-    blocks = CW // PD
-    for c in range(blocks):
+    for c in range(CW // PD):
         block = coef_ref[:, c * PD : (c + 1) * PD].astype(F32)
         f_ref[c * PD : (c + 1) * PD, :] = block.T
     offset = 0
     for q in range(RAD):
         here = pl.ds(offset, ANG)
-        re_ref[here, :] = f_ref[q * ANG : (q + 1) * ANG, :]
-        im_ref[here, :] = f_ref[(RAD + q) * ANG : (RAD + q + 1) * ANG, :]
+        wide_re_ref[here, :] = f_ref[q * ANG : (q + 1) * ANG, :]
+        wide_im_ref[here, :] = f_ref[(RAD + q) * ANG : (RAD + q + 1) * ANG, :]
         offset = offset + trunc_ref[q]
     for b in range(FULL // PD):
         rows = slice(b * PD, (b + 1) * PD)
+        to = slice(HEAD + b * PD, HEAD + (b + 1) * PD)
         kept = iota((PD, PD), 0) + b * PD < offset
-        out_ref[HEAD + b * PD : HEAD + (b + 1) * PD, :PD] = jnp.where(
-            kept, re_ref[rows, :], 0.0
-        ).astype(BF16)
-        out_ref[HEAD + b * PD : HEAD + (b + 1) * PD, PD:] = jnp.where(
-            kept, im_ref[rows, :], 0.0
-        ).astype(BF16)
+        out_ref[to, :PD] = jnp.where(kept, wide_re_ref[rows, :], 0.0).astype(BF16)
+        out_ref[to, PD:] = jnp.where(kept, wide_im_ref[rows, :], 0.0).astype(BF16)
+    own_pairs(trunc_ref, e_ref, re_ref, im_ref, f_ref, s_ref)
 
 
 def pick_kernel(size, rx_ref, pack_ref, out_ref):
@@ -157,21 +157,18 @@
     rows = iota((PD, PD), 0)
     first = iota((PD, PD), 1) < CAP
     sides = []
-    for p in range(2):
-        picked = rows == rx_ref[2 * r + p][:1, :].astype(jnp.int32)
+    for p in range(WIDE):
+        picked = rows == rx_ref[WIDE * r + p][:1, :].astype(jnp.int32)
         top = one_hot(picked & first)
         bottom = one_hot(picked & jnp.logical_not(first))
         sides.append(jnp.concatenate([top, bottom], axis=0))
     side = jnp.concatenate(sides, axis=1)
     chosen = jnp.dot(pack_ref[:size, :], side, preferred_element_type=F32).astype(BF16)
-    out_ref[0] = chosen[:, :PD]
-    out_ref[1] = chosen[:, PD:]
-
-
-def own_kernel(trunc_ref, coef_ref, e_ref, re_ref, im_ref, xt_ref, s_ref):
-    for c in range(CW // PD):
-        block = coef_ref[:, c * PD : (c + 1) * PD].astype(F32)
-        xt_ref[c * PD : (c + 1) * PD, :] = block.T
+    for p in range(WIDE):
+        out_ref[p] = chosen[:, p * PD : (p + 1) * PD]
+
+
+def own_pairs(trunc_ref, e_ref, re_ref, im_ref, xt_ref, s_ref):
     kept = kept_rows(trunc_ref, 2 * RAD, PD)
 
     def per_frequency(k, carry):
@@ -214,69 +211,73 @@
 
 def far_kernel(
     size, trunc_ref, names_ref, pack_ref, recv_ref, table_ref, cur_ref,
-    same_ref, cross_ref, other_ref,
+    mine_ref, other_ref, cross_ref,
 ):
     r = pl.program_id(0)
     kept = size - HEAD
 
     @pl.when(r == 0)
     def _():
-        same_ref[kept:, :] = jnp.zeros((ANG, PD), F32)
+        for p in range(WIDE):
+            mine_ref[p, kept:, :] = jnp.zeros((ANG, PD), F32)
+        other_ref[kept:, :] = jnp.zeros((ANG, PD), F32)
         cross_ref[kept:, :] = jnp.zeros((ANG, PD), F32)
-        other_ref[kept:, :] = jnp.zeros((ANG, PD), F32)
 
     first = iota((PD, PD), 1) < CAP
+    sides = []
+    for p in range(WIDE):
+        name = names_ref[pl.ds(WIDE * r + p, 1), :].astype(jnp.int32)
+        named = iota((PD, PD), 0) + 1 == name
+        low = one_hot(named & first)
+        high = one_hot(named & jnp.logical_not(first))
+        sides.append(jnp.concatenate([low, high], axis=0))
+    mine = jnp.dot(
+        pack_ref[HEAD:size, :], jnp.concatenate(sides, axis=1), preferred_element_type=F32
+    )
+    for p in range(WIDE):
+        mine_ref[p, :kept, :] = mine[:, p * PD : (p + 1) * PD]
     freq = iota((ANG, PD), 0)
     halves = []
-    for p in range(2):
-        named = iota((PD, PD), 0) + 1 == names_ref[pl.ds(2 * r + p, 1), :].astype(jnp.int32)
-        low = one_hot(named & first)
-        high = one_hot(named & jnp.logical_not(first))
-        side = jnp.concatenate(
-            [
-                jnp.concatenate([low, high], axis=1),
-                jnp.concatenate([high, low], axis=1),
-            ],
-            axis=0,
-        )
-        mine = jnp.dot(pack_ref[HEAD:size, :], side, preferred_element_type=F32)
-        same_ref[:kept, :] = mine[:, :PD]
-        cross_ref[:kept, :] = mine[:, PD:]
-        other_ref[:kept, :] = recv_ref[p, HEAD:, :].astype(F32)
+    for p in range(WIDE):
+        arrived = recv_ref[p, HEAD:, :].astype(F32)
+        other_ref[:kept, :] = arrived
+        cross_ref[:kept, :] = pltpu.roll(arrived, CAP, 1)
         sum_re = jnp.zeros((ANG, PD), F32)
         sum_im = jnp.zeros((ANG, PD), F32)
         offset = 0
         for q in range(RAD):
             here = pl.ds(offset, ANG)
-            other = jnp.where(freq < trunc_ref[q], other_ref[here, :], 0.0)
-            sum_re = sum_re + same_ref[here, :] * other
-            sum_im = sum_im + cross_ref[here, :] * other
+            own = jnp.where(freq < trunc_ref[q], mine_ref[p, here, :], 0.0)
+            sum_re = sum_re + own * other_ref[here, :]
+            sum_im = sum_im + own * cross_ref[here, :]
             offset = offset + trunc_ref[q]
         halves.append((sum_re, sum_im))
         parts = recv_ref[p, :HEAD, :].astype(F32)
         cur_ref[p] = parts[:VEC] + parts[VEC:]
     first = first[:ANG]
-    s_re = jnp.where(first, halves[0][0], halves[1][0])
-    s_re = s_re + pltpu.roll(jnp.where(first, halves[1][0], halves[0][0]), CAP, 1)
-    s_im = pltpu.roll(jnp.where(first, halves[1][1], halves[0][1]), CAP, 1)
-    s_im = jnp.where(first, halves[0][1] - s_im, s_im - halves[1][1])
-    power = s_re * s_re + s_im * s_im
-    next_re = pltpu.roll(s_re, ANG - 1, 0)
-    next_im = pltpu.roll(s_im, ANG - 1, 0)
-    zero_re = s_re[:1]
-    energy = zero_re * zero_re + 0.5 * jnp.sum(
-        jnp.where(freq == 0, 0.0, power), axis=0, keepdims=True
-    )
     inner = (freq > 0) & (freq < ANG - 1)
-    m_re = zero_re * s_re[1:2] + 0.5 * jnp.sum(
-        jnp.where(inner, s_re * next_re + s_im * next_im, 0.0), axis=0, keepdims=True
-    )
-    m_im = 0.5 * jnp.sum(
-        jnp.where(inner, s_im * next_re - s_re * next_im, 0.0), axis=0, keepdims=True
-    ) - zero_re * s_im[1:2]
-    table_ref[0] = jnp.concatenate(
-        [energy, m_re, m_im, jnp.zeros((5, PD), F32)], axis=0
-    )
+    for b in range(WIDE // 2):
+        even, odd = halves[2 * b], halves[2 * b + 1]
+        s_re = jnp.where(first, even[0], odd[0])
+        s_re = s_re + pltpu.roll(jnp.where(first, odd[0], even[0]), CAP, 1)
+        s_im = pltpu.roll(jnp.where(first, odd[1], even[1]), CAP, 1)
+        s_im = jnp.where(first, s_im - even[1], odd[1] - s_im)
+        power = s_re * s_re + s_im * s_im
+        next_re = pltpu.roll(s_re, ANG - 1, 0)
+        next_im = pltpu.roll(s_im, ANG - 1, 0)
+        zero_re = s_re[:1]
+        energy = zero_re * zero_re + 0.5 * jnp.sum(
+            jnp.where(freq == 0, 0.0, power), axis=0, keepdims=True
+        )
+        m_re = zero_re * s_re[1:2] + 0.5 * jnp.sum(
+            jnp.where(inner, s_re * next_re + s_im * next_im, 0.0), axis=0, keepdims=True
+        )
+        m_im = 0.5 * jnp.sum(
+            jnp.where(inner, s_im * next_re - s_re * next_im, 0.0), axis=0, keepdims=True
+        ) - zero_re * s_im[1:2]
+        table_ref[b] = jnp.concatenate(
+            [energy, m_re, m_im, jnp.zeros((5, PD), F32)], axis=0
+        )
 
 
 def near_image(cur, w_re, w_im):
@@ -454,47 +455,38 @@
     return pl.BlockSpec(shape, lambda r: (0,) * len(shape))
 
 
-def exchange(size, truncation, coefficients, names, asked, packed):
+def exchange(size, truncation, names, asked, packed):
+    steps = PEERS // WIDE
     sent = pl.pallas_call(
         functools.partial(pick_kernel, size),
-        grid=(PAIRS,),
+        grid=(steps,),
         out_shape=struct((PEERS, size, PD), BF16),
         in_specs=[whole(PEERS, 8, PD), whole(HEAD + FULL, 2 * PD)],
-        out_specs=pl.BlockSpec((2, size, PD), lambda r: (r, 0, 0)),
+        out_specs=pl.BlockSpec((WIDE, size, PD), lambda r: (r, 0, 0)),
         name="pick",
     )(asked, packed)
     received = lax.all_to_all(sent, REP, 0, 0, tiled=True)
-    own = pl.pallas_call(
-        own_kernel,
-        out_shape=(struct((PD, PD)),) * 3,
-        in_specs=[SMEM, VMEM],
-        scratch_shapes=[
-            pltpu.VMEM((CW, PD), F32),
-            pltpu.VMEM((ANG, PD, 2 * PD), F32),
-        ],
-        cost_estimate=pl.CostEstimate(
-            flops=20_000_000_000, bytes_accessed=1_000_000, transcendentals=0
-        ),
-        name="own",
-    )(truncation, coefficients)
-    far = pl.pallas_call(
+    return pl.pallas_call(
         functools.partial(far_kernel, size),
-        grid=(PAIRS,),
+        grid=(steps,),
         out_shape=(struct((PAIRS, 8, PD)), struct((PEERS, VEC, PD))),
         in_specs=[
             SMEM,
             whole(PEERS, PD),
             whole(HEAD + FULL, 2 * PD),
-            pl.BlockSpec((2, size, PD), lambda r: (r, 0, 0)),
+            pl.BlockSpec((WIDE, size, PD), lambda r: (r, 0, 0)),
         ],
         out_specs=(
-            pl.BlockSpec((1, 8, PD), lambda r: (r, 0, 0)),
-            pl.BlockSpec((2, VEC, PD), lambda r: (r, 0, 0)),
+            pl.BlockSpec((WIDE // 2, 8, PD), lambda r: (r, 0, 0)),
+            pl.BlockSpec((WIDE, VEC, PD), lambda r: (r, 0, 0)),
         ),
-        scratch_shapes=[pltpu.VMEM((size - HEAD + ANG, PD), F32)] * 3,
+        scratch_shapes=[
+            pltpu.VMEM((WIDE, size - HEAD + ANG, PD), F32),
+            pltpu.VMEM((size - HEAD + ANG, PD), F32),
+            pltpu.VMEM((size - HEAD + ANG, PD), F32),
+        ],
         name="far",
     )(truncation, names, packed, received)
-    return (*own, *far)
 
 
 def shards(coefficients, truncation, neighbours, initial):
@@ -521,27 +513,27 @@
         name="slots",
     )(place, neighbours)
     asked = lax.all_to_all(requests, REP, 0, 0, tiled=True)
-    packed = pl.pallas_call(
-        pack_kernel,
-        out_shape=struct((HEAD + FULL, 2 * PD), BF16),
+    packed, e_own, re_own, im_own = pl.pallas_call(
+        local_kernel,
+        out_shape=(struct((HEAD + FULL, 2 * PD), BF16),) + (struct((PD, PD)),) * 3,
         in_specs=[SMEM, VMEM, VMEM],
         scratch_shapes=[
             pltpu.VMEM((CW, PD), F32),
             pltpu.VMEM((FULL + ANG, PD), F32),
             pltpu.VMEM((FULL + ANG, PD), F32),
+            pltpu.VMEM((ANG, PD, 2 * PD), F32),
         ],
         cost_estimate=pl.CostEstimate(
-            flops=5_000_000_000, bytes_accessed=1_000_000, transcendentals=0
+            flops=20_000_000_000, bytes_accessed=1_000_000, transcendentals=0
         ),
-        name="pack",
+        name="local",
     )(truncation, coefficients, initial)
-    sizes = list(range(LEAST, FULL + 1, STEP))
     total = jnp.sum(truncation)
-    which = jnp.clip((total - LEAST + STEP - 1) // STEP, 0, len(sizes) - 1)
-    e_own, re_own, im_own, table, slots = lax.switch(
+    which = jnp.sum(total > jnp.array(SIZES[:-1], jnp.int32)).astype(jnp.int32)
+    table, slots = lax.switch(
         which,
-        [functools.partial(exchange, HEAD + size) for size in sizes],
-        truncation, coefficients, names, asked, packed,
+        [functools.partial(exchange, HEAD + size) for size in SIZES],
+        truncation, names, asked, packed,
     )
     alignment, weights, degree, current, columns = pl.pallas_call(
         first_kernel,

time: 132 us -> 130 us (0.985); the launches traced: 130 us -> 129 us
  blocking collectives: 23.1 us -> 62.7 us
  waiting for transfers between devices: 41.2 us -> 8.72 us
  Pallas kernels: 36.4 us -> 32.2 us
  starting transfers between devices: 22 us -> 18.7 us
  other arithmetic: 1.24 us -> 3.12 us
  local copies, waits for them, and re-layouts: 3.63 us -> 2.13 us
    all_to_all x0 -> x1, blocking collectives: none -> 40.7 us  [exchange(): received = lax.all_to_all(sent, REP, 0, 0, tiled=True)]
    all_to_all x1 -> x0, waiting for transfers between devices: 28.8 us -> none  [exchange(): received = lax.all_to_all(sent, REP, 0, 0, tiled=True)]
    pallas_call x4 -> x3, Pallas kernels: 22.6 us -> 18.4 us  [the longest x1 8.59 us: shards(): pl.pallas_call(local_kernel, out_shape=(struct((HEAD + FULL, 2 * PD), BF1...]
    all_to_all x1 -> x0, starting transfers between devices: 3.73 us -> none  [exchange(): received = lax.all_to_all(sent, REP, 0, 0, tiled=True)]
    all_to_all x1, waiting for transfers between devices: 3.73 us -> 0.01 us  [shards(): asked = lax.all_to_all(requests, REP, 0, 0, tiled=True)]
    cond x4 -> x0, local copies, waits for them, and re-layouts: 1.5 us -> none
  transfers between devices with their start and end apart: 3 -> 2, of which waited for: 3 -> 1; matrix products, arithmetic and copies ran while one was open for 2% -> 3% of each run, Pallas kernels for 8% -> 7%
where the time goes in v3:
time: 130 us; the launch traced here: 129 us
  blocking collectives  62.7 us (48%)
  Pallas kernels  32.2 us (25%)
  starting transfers between devices  18.7 us (14%)
  waiting for transfers between devices  8.72 us (7%)
  other arithmetic  3.12 us (2%)
  local copies, waits for them, and re-layouts  2.13 us (2%)
    all_to_all x1, blocking collectives, exchange(): received = lax.all_to_all(sent, REP, 0, 0, tiled=True)  40.7 us
    all_to_all x2, blocking collectives, shards(): columns = lax.all_to_all(columns, REP, 0, 0, tiled=True)  22 us
    all_to_all x1, starting transfers between devices, shards(): grams = lax.all_to_all(gram, GRP_REP, 0, 0, tiled=True)  10.3 us
    all_to_all x1, waiting for transfers between devices, shards(): grams = lax.all_to_all(gram, GRP_REP, 0, 0, tiled=True)  8.72 us
    pallas_call x1, Pallas kernels, shards(): pl.pallas_call(local_kernel, out_shape=(struct((HEAD + FULL, 2 * PD), BF1...  8.59 us
    all_to_all x1, starting transfers between devices, shards(): asked = lax.all_to_all(requests, REP, 0, 0, tiled=True)  8.42 us
    pallas_call x1, Pallas kernels, exchange(): pl.pallas_call(functools.partial(far_kernel, size), grid=(steps,), out_sh...  6.98 us
    pallas_call x1, Pallas kernels, shards(): pl.pallas_call(first_kernel, out_shape=(struct((2, NB, PD)), struct((2, P...  3.71 us
  transfers between devices with their start and end apart: 2, of which 1 were waited for; matrix products, arithmetic and copies ran while one was open for 3% of the time, Pallas kernels for 7%

profile of v3, /device:TPU:1, one launch (start us, length us, event | category | flops | bytes accessed | tf_op | source)
XLA Modules:
  0.0 129.1 jit_solution(4335591136856546600)
XLA Ops:
  0.6 0.6 pad_add_fusion.where_ref
  1.2 2.4 %slots.1 = (s32[56,128]{1,0:T(8,128)}, f32[8,128]{1,0:T(8,128)}, f32[16,128]{1,0:T(8,128)S(1)}, f32[16,8,128]{2,1,0:T(8,128)}) custom-call(s32[2]{0:T(128)} %pad_add_fusion.where_ref, s32[50,128]{1,0:T(8,128)} %nb_ref.3), custom_call_target="tpu_custom_call" | custom-call | tf_op jit(solution)/shard_map/slots/pallas_call | solution.py:499
  3.6 8.4 %all-to-all-start.8 = ((f32[16,8,128]{2,1,0:T(8,128)}), f32[16,8,128]{2,1,0:T(8,128)S(1)}, u32[]{:S(2)}, u32[]{:S(2)}) async-start(f32[16,8,128]{2,1,0:T(8,128)} %get-tuple-element.119), calls=%async_computation.8 | async-start | bytes 131072 | tf_op jit(solution)/shard_map/all_to_all | solution.py:515
  12.1 1.3 %reduce_sum.18 = s32[]{:T(128)} reduce(s32[16]{0:T(128)} %trunc_ref.1, s32[]{:T(128)} %constant.27.clone.1), dimensions={0}, to_apply=%region_0.0 | reduce | flops 15 | bytes 72 | tf_op jit(solution)/shard_map/reduce_sum | solution.py:531
  13.3 0.0 copy-start.2
  13.3 8.6 %local.1 = (bf16[1056,256]{1,0:T(8,128)(2,1)S(1)}, f32[128,128]{1,0:T(8,128)}, f32[128,128]{1,0:T(8,128)}, f32[128,128]{1,0:T(8,128)}) custom-call(s32[16]{0:T(128)} %trunc_ref.1, bf16[128,2048]{1,0:T(8,128)(2,1)} %coef_ref.1, f32[32,128]{1,0:T(8,128)} %init_ref.3), custom_call_target="tpu_custom_call" | custom-call | flops 20000000000 | bytes 1000000 | tf_op jit(solution)/shard_map/local/pallas_call | solution.py:516
  21.9 0.0 copy-done.2
  21.9 1.3 fusion
  23.8 0.0 all-to-all-done.8.rx_ref
  23.8 0.0 copy-done.1
  23.8 50.8 %conditional.1 = ((f32[8,8,128]{2,1,0:T(8,128)S(1)}, f32[16,16,128]{2,1,0:T(8,128)S(1)})) conditional(s32[]{:T(128)} %clamp.3, (f32[16,8,128]{2,1,0:T(8,128)S(1)}, bf16[1056,256]{1,0:T(8,128)(2,1)S(1)}, s32[16]{0:T(128)S(1)}, f32[16,128]{1,0:T(8,128)S(1)}) %tuple.51, (f32[16,8,128]{2,1,0:T(8,128)S(1)}, ...), branch_computations={%region_2.0_spmd, %region_3.0_spmd, %region_4.0_spmd, %region_5.0_... | conditional | bytes 8650760 | solution.py:533
  23.8 2.8 %pick.11 = bf16[16,672,128]{2,1,0:T(8,128)(2,1)} custom-call(f32[16,8,128]{2,1,0:T(8,128)S(1)} %get-tuple-element.79.rx_ref, bf16[1056,256]{1,0:T(8,128)(2,1)S(1)} %get-tuple-element.78.pack_ref), custom_call_target="tpu_custom_call" | custom-call | tf_op jit(solution)/shard_map/cond/branch_3_fun/pick/pallas_call | solution.py:460
  26.7 40.7 %all_to_all.55.recv_ref = bf16[16,672,128]{2,1,0:T(8,128)(2,1)} all-to-all(bf16[16,672,128]{2,1,0:T(8,128)(2,1)} %pick.11), channel_id=1, replica_groups=mesh['grp_0'=4,'grp_1'=2,'rep_0'=4,'rep_1'=4] {'rep_0','rep_1'}, dimensions={0} | all-to-all | bytes 5505024 | tf_op jit(solution)/shard_map/cond/branch_3_fun/all_to_all | solution.py:468
  67.4 7.0 %far.11 = (f32[8,8,128]{2,1,0:T(8,128)S(1)}, f32[16,16,128]{2,1,0:T(8,128)S(1)}) custom-call(s32[16]{0:T(128)S(1)} %get-tuple-element.76.trunc_ref, f32[16,128]{1,0:T(8,128)S(1)} %get-tuple-element.77.names_ref, bf16[1056,256]{1,0:T(8,128)(2,1)S(1)} %get-tuple-element.78.pack_ref, bf16[16,672,128]{2,1,0:T(8,128)(2,1)} %all_to_all.55.recv_ref), custom_call_target="tpu_custom_call" | custom-call | tf_op jit(solution)/shard_map/cond/branch_3_fun/far/pallas_call | solution.py:469
  74.6 3.7 %first.1 = (f32[2,50,128]{2,1,0:T(8,128)}, f32[2,128,128]{2,1,0:T(8,128)}, f32[8,128]{1,0:T(8,128)}, f32[32,128]{1,0:T(8,128)}, f32[16,16,128]{2,1,0:T(8,128)}) custom-call(s32[2]{0:T(128)} %pad_add_fusion.where_ref, s32[50,128]{1,0:T(8,128)} %nb_ref.3, s32[56,128]{1,0:T(8,128)} %get-tuple-element.117.code_ref, f32[8,128]{1,0:T(8,128)} %get-tuple-element.118.lists_ref, ...), custom_call_target="tpu_custom_call" | custom-call | tf_op jit(solution)/shard_map/first/pallas_call | solution.py:538
  78.3 11.0 %all_to_all.60.recv_ref = f32[16,16,128]{2,1,0:T(8,128)} all-to-all(f32[16,16,128]{2,1,0:T(8,128)} %get-tuple-element.128), channel_id=1, replica_groups=mesh['grp_0'=4,'grp_1'=2,'rep_0'=4,'rep_1'=4] {'rep_0','rep_1'}, dimensions={0} | all-to-all | bytes 262144 | tf_op jit(solution)/shard_map/all_to_all | solution.py:554
  89.3 2.2 %middle.1 = (f32[32,128]{1,0:T(8,128)}, f32[16,16,128]{2,1,0:T(8,128)}) custom-call(f32[16,16,128]{2,1,0:T(8,128)} %all_to_all.60.recv_ref, f32[32,128]{1,0:T(8,128)} %get-tuple-element.129.cur_ref, f32[2,128,128]{2,1,0:T(8,128)} %get-tuple-element.130.weights_ref, f32[8,128]{1,0:T(8,128)} %get-tuple-element.131.degree_ref, ...), custom_call_target="tpu_custom_call" | custom-call | tf_op jit(solution)/shard_map/middle/pallas_call | solution.py:555
  91.5 11.0 %all_to_all.61.recv_ref = f32[16,16,128]{2,1,0:T(8,128)} all-to-all(f32[16,16,128]{2,1,0:T(8,128)} %get-tuple-element.132), channel_id=1, replica_groups=mesh['grp_0'=4,'grp_1'=2,'rep_0'=4,'rep_1'=4] {'rep_0','rep_1'}, dimensions={0} | all-to-all | bytes 262144 | tf_op jit(solution)/shard_map/all_to_all | solution.py:560
  102.5 2.2 %last.1 = (f32[32,128]{1,0:T(8,128)}, f32[128,2,128]{2,1,0:T(2,128)}) custom-call(f32[16,16,128]{2,1,0:T(8,128)} %all_to_all.61.recv_ref, f32[32,128]{1,0:T(8,128)} %get-tuple-element.133.cur_ref, f32[2,128,128]{2,1,0:T(8,128)} %get-tuple-element.130.weights_ref, f32[8,128]{1,0:T(8,128)} %get-tuple-element.131.degree_ref, ...), custom_call_target="tpu_custom_call" | custom-call | tf_op jit(solution)/shard_map/last/pallas_call | solution.py:561
  104.8 10.3 %all-to-all-start.11 = ((f32[128,2,128]{2,1,0:T(2,128)}), f32[128,2,128]{2,1,0:T(2,128)S(1)}, u32[]{:S(2)}, u32[]{:S(2)}) async-start(f32[128,2,128]{2,1,0:T(2,128)} %get-tuple-element.134), calls=%async_computation.11 | async-start | bytes 262144 | tf_op jit(solution)/shard_map/all_to_all | solution.py:566
  115.0 1.5 %copy.7 = f32[2,50,128]{2,0,1:T(2,128)} copy(f32[2,50,128]{2,1,0:T(8,128)} %get-tuple-element.136) | data formatting | bytes 102400
  116.5 8.7 %all-to-all-done.11.grams_ref = f32[128,2,128]{2,1,0:T(2,128)S(1)} async-done(((f32[128,2,128]{2,1,0:T(2,128)}), f32[128,2,128]{2,1,0:T(2,128)S(1)}, u32[]{:S(2)}, u32[]{:S(2)}) %all-to-all-start.11) | async-done | bytes 131104 | tf_op jit(solution)/shard_map/all_to_all | solution.py:566
  125.2 0.7 copy-done
  125.9 3.2 %finish.1 = f32[32,128]{1,0:T(8,128)} custom-call(f32[128,2,128]{2,1,0:T(2,128)} %copy-done, f32[32,128]{1,0:T(8,128)} %get-tuple-element.135.cur_ref), custom_call_target="tpu_custom_call" | custom-call | tf_op jit(solution)/shard_map/finish/pallas_call | solution.py:567
  (2 shorter events, 0.0 us)
Async XLA Ops:
  3.6 20.2 %all-to-all-start.8 = ((f32[16,8,128]{2,1,0:T(8,128)}), f32[16,8,128]{2,1,0:T(8,128)S(1)}, u32[]{:S(2)}, u32[]{:S(2)}) async-start(f32[16,8,128]{2,1,0:T(8,128)} %get-tuple-element.119), calls=%async_computation.8 | async-start | bytes 131072 | tf_op jit(solution)/shard_map/all_to_all | solution.py:515
  13.3 8.6 %copy-start.2 = (s32[7]{0:T(128)S(1)}, s32[7]{0:T(128)}, u32[]{:S(2)}) copy-start(s32[7]{0:T(128)} %constant.29.clone) | copy-start | bytes 88
  13.3 10.5 %copy-start.1 = (s32[16]{0:T(128)S(1)}, s32[16]{0:T(128)}, u32[]{:S(2)}) copy-start(s32[16]{0:T(128)} %trunc_ref.1) | copy-start | bytes 196
  104.8 20.5 %all-to-all-start.11 = ((f32[128,2,128]{2,1,0:T(2,128)}), f32[128,2,128]{2,1,0:T(2,128)S(1)}, u32[]{:S(2)}, u32[]{:S(2)}) async-start(f32[128,2,128]{2,1,0:T(2,128)} %get-tuple-element.134), calls=%async_computation.11 | async-start | bytes 262144 | tf_op jit(solution)/shard_map/all_to_all | solution.py:566
  125.2 0.7 copy-start

commit v4 on v3

--- a/solution.py
+++ b/solution.py
@@ -70,13 +70,29 @@
     return kept
 
 
+def place():
+    index = [lax.axis_index(name) for name in GRP_REP]
+    size = [lax.axis_size(name) for name in GRP_REP]
+    group = index[0] * size[1] + index[1]
+    member = index[2] * size[3] + index[3]
+    return group * (size[2] * size[3] * PD), member
+
+
 def slot_kernel(
-    where_ref, nb_ref, code_ref, lists_ref, names_ref, req_ref, nbp_ref, a_ref, b_ref
+    trunc_ref, nb_ref, which_ref, code_ref, lists_ref, names_ref, req_ref,
+    nbp_ref, a_ref, b_ref,
 ):
+    total = trunc_ref[0]
+    for q in range(1, RAD):
+        total = total + trunc_ref[q]
+    which = jnp.int32(0)
+    for size in SIZES[:-1]:
+        which = which + (total > size).astype(jnp.int32)
+    which_ref[0] = which
+    start, me = place()
     nbp_ref[...] = jnp.full((NBP, PD), -1, jnp.int32)
-    nbp_ref[:NB, :] = nb_ref[...] - where_ref[0]
+    nbp_ref[:NB, :] = nb_ref[...] - start
     local = nbp_ref[...]
-    me = where_ref[1]
     owner = local >> 7
     within = local & (PD - 1)
     remote = (owner != me) & (local >= 0)
@@ -181,7 +197,7 @@
         )
         return carry
 
-    lax.fori_loop(0, ANG, per_frequency, 0, unroll=4)
+    lax.fori_loop(0, ANG, per_frequency, 0, unroll=8)
 
     def per_rows(b, carry):
         sub = pl.ds(b * 8, 8)
@@ -211,7 +227,7 @@
 
 def far_kernel(
     size, trunc_ref, names_ref, pack_ref, recv_ref, table_ref, cur_ref,
-    mine_ref, other_ref, cross_ref,
+    same_ref, cross_ref,
 ):
     r = pl.program_id(0)
     kept = size - HEAD
@@ -219,9 +235,8 @@
     @pl.when(r == 0)
     def _():
         for p in range(WIDE):
-            mine_ref[p, kept:, :] = jnp.zeros((ANG, PD), F32)
-        other_ref[kept:, :] = jnp.zeros((ANG, PD), F32)
-        cross_ref[kept:, :] = jnp.zeros((ANG, PD), F32)
+            same_ref[p, kept:, :] = jnp.zeros((ANG, PD), F32)
+            cross_ref[p, kept:, :] = jnp.zeros((ANG, PD), F32)
 
     first = iota((PD, PD), 1) < CAP
     sides = []
@@ -234,26 +249,26 @@
     mine = jnp.dot(
         pack_ref[HEAD:size, :], jnp.concatenate(sides, axis=1), preferred_element_type=F32
     )
-    for p in range(WIDE):
-        mine_ref[p, :kept, :] = mine[:, p * PD : (p + 1) * PD]
     freq = iota((ANG, PD), 0)
     halves = []
     for p in range(WIDE):
         arrived = recv_ref[p, HEAD:, :].astype(F32)
-        other_ref[:kept, :] = arrived
-        cross_ref[:kept, :] = pltpu.roll(arrived, CAP, 1)
+        own = mine[:, p * PD : (p + 1) * PD]
+        same_ref[p, :kept, :] = own * arrived
+        cross_ref[p, :kept, :] = own * pltpu.roll(arrived, CAP, 1)
+        parts = recv_ref[p, :HEAD, :].astype(F32)
+        cur_ref[p] = parts[:VEC] + parts[VEC:]
+    for p in range(WIDE):
         sum_re = jnp.zeros((ANG, PD), F32)
         sum_im = jnp.zeros((ANG, PD), F32)
         offset = 0
         for q in range(RAD):
             here = pl.ds(offset, ANG)
-            own = jnp.where(freq < trunc_ref[q], mine_ref[p, here, :], 0.0)
-            sum_re = sum_re + own * other_ref[here, :]
-            sum_im = sum_im + own * cross_ref[here, :]
+            inside = freq < trunc_ref[q]
+            sum_re = sum_re + jnp.where(inside, same_ref[p, here, :], 0.0)
+            sum_im = sum_im + jnp.where(inside, cross_ref[p, here, :], 0.0)
             offset = offset + trunc_ref[q]
         halves.append((sum_re, sum_im))
-        parts = recv_ref[p, :HEAD, :].astype(F32)
-        cur_ref[p] = parts[:VEC] + parts[VEC:]
     first = first[:ANG]
     inner = (freq > 0) & (freq < ANG - 1)
     for b in range(WIDE // 2):
@@ -329,12 +344,13 @@
 
 
 def first_kernel(
-    where_ref, nb_ref, code_ref, lists_ref, table_ref, e_ref, re_ref, im_ref,
+    nb_ref, code_ref, lists_ref, table_ref, e_ref, re_ref, im_ref,
     slots_ref, init_ref, rx_ref,
     align_ref, weights_ref, degree_ref, cur_ref, send_ref, near_ref,
 ):
-    local = nb_ref[...] - where_ref[0]
-    near = (local >> 7) == where_ref[1]
+    start, me = place()
+    local = nb_ref[...] - start
+    near = (local >> 7) == me
     near_ref[...] = jnp.where(near, local & (PD - 1), -1)
     rows = iota((PD, PD), 0)
     counts = jnp.zeros((PD, PD), F32)
@@ -423,20 +439,19 @@
     wide = jnp.where(lane // VEC == row % 8, wide, 0.0)
     for shift in (64, 32, 16):
         wide = wide + pltpu.roll(wide, shift, 1)
-    gram = wide
+    columns = [jnp.broadcast_to(wide[:, c : c + 1], (VEC, PD)) for c in range(VEC)]
     re = cur_ref[:VEC, :]
     im = cur_ref[VEC:, :]
     for c in range(VEC):
-        pivot = gram[c : c + 1, c : c + 1]
+        pivot = columns[c][c : c + 1, :]
         scale = lax.rsqrt(pivot)
         scale = scale * (1.5 - 0.5 * pivot * scale * scale)
-        column = gram[:, c : c + 1] * scale
-        column = jnp.where(row[:, :1] > c, column, 0.0)
-        top_gram = gram[c : c + 1, :] * scale
+        column = jnp.where(row > c, columns[c] * scale, 0.0)
+        for d in range(c + 1, VEC):
+            columns[d] = columns[d] - column * (columns[d][c : c + 1, :] * scale)
         top_re = re[c : c + 1, :] * scale
         top_im = im[c : c + 1, :] * scale
         here = row == c
-        gram = gram - column * top_gram
         re = jnp.where(here, top_re, re - column * top_re)
         im = jnp.where(here, top_im, im - column * top_im)
     out_ref[:VEC, :] = re
@@ -449,6 +464,10 @@
 
 SMEM = pl.BlockSpec(memory_space=pltpu.SMEM)
 VMEM = pl.BlockSpec(memory_space=pltpu.VMEM)
+
+
+def grant(mib):
+    return pltpu.CompilerParams(vmem_limit_bytes=mib << 20)
 
 
 def whole(*shape):
@@ -463,6 +482,7 @@
         out_shape=struct((PEERS, size, PD), BF16),
         in_specs=[whole(PEERS, 8, PD), whole(HEAD + FULL, 2 * PD)],
         out_specs=pl.BlockSpec((WIDE, size, PD), lambda r: (r, 0, 0)),
+        compiler_params=grant(16),
         name="pick",
     )(asked, packed)
     received = lax.all_to_all(sent, REP, 0, 0, tiled=True)
@@ -482,9 +502,9 @@
         ),
         scratch_shapes=[
             pltpu.VMEM((WIDE, size - HEAD + ANG, PD), F32),
-            pltpu.VMEM((size - HEAD + ANG, PD), F32),
-            pltpu.VMEM((size - HEAD + ANG, PD), F32),
+            pltpu.VMEM((WIDE, size - HEAD + ANG, PD), F32),
         ],
+        compiler_params=grant(20),
         name="far",
     )(truncation, names, packed, received)
 
@@ -493,25 +513,25 @@
     groups = lax.axis_size(GRP)
     replicas = lax.axis_size(REP)
     devices = groups * replicas
-    place = jnp.stack(
-        [lax.axis_index(GRP) * (replicas * PD), lax.axis_index(REP)]
-    ).astype(jnp.int32)
-    code, lists, names, requests = pl.pallas_call(
+    which, code, lists, names, requests = pl.pallas_call(
         slot_kernel,
         out_shape=(
+            struct((1,), jnp.int32),
             struct((NBP, PD), jnp.int32),
             struct((PAIRS, PD)),
             struct((PEERS, PD)),
             struct((PEERS, 8, PD)),
         ),
         in_specs=[SMEM, VMEM],
+        out_specs=(SMEM, VMEM, VMEM, VMEM, VMEM),
+        compiler_params=grant(6),
         scratch_shapes=[
             pltpu.VMEM((NBP, PD), jnp.int32),
             pltpu.VMEM((2 * PAIRS, NB * PD), BF16),
             pltpu.VMEM((PD, NB * PD), BF16),
         ],
         name="slots",
-    )(place, neighbours)
+    )(truncation, neighbours)
     asked = lax.all_to_all(requests, REP, 0, 0, tiled=True)
     packed, e_own, re_own, im_own = pl.pallas_call(
         local_kernel,
@@ -526,12 +546,11 @@
         cost_estimate=pl.CostEstimate(
             flops=20_000_000_000, bytes_accessed=1_000_000, transcendentals=0
         ),
+        compiler_params=grant(20),
         name="local",
     )(truncation, coefficients, initial)
-    total = jnp.sum(truncation)
-    which = jnp.sum(total > jnp.array(SIZES[:-1], jnp.int32)).astype(jnp.int32)
     table, slots = lax.switch(
-        which,
+        which[0],
         [functools.partial(exchange, HEAD + size) for size in SIZES],
         truncation, names, asked, packed,
     )
@@ -544,28 +563,34 @@
             struct((32, PD)),
             struct((PEERS, VEC, PD)),
         ),
-        in_specs=[SMEM] + [VMEM] * 10,
+        in_specs=[VMEM] * 10,
+        compiler_params=grant(6),
         scratch_shapes=[pltpu.VMEM((NB, PD), jnp.int32)],
         name="first",
     )(
-        place, neighbours, code, lists, table, e_own, re_own, im_own,
+        neighbours, code, lists, table, e_own, re_own, im_own,
         slots, initial, asked,
     )
     columns = lax.all_to_all(columns, REP, 0, 0, tiled=True)
     current, columns = pl.pallas_call(
         middle_kernel,
         out_shape=(struct((32, PD)), struct((PEERS, VEC, PD))),
+        compiler_params=grant(6),
         name="middle",
     )(columns, current, weights, degree, table, lists, asked)
     columns = lax.all_to_all(columns, REP, 0, 0, tiled=True)
     current, gram = pl.pallas_call(
         functools.partial(last_kernel, float(PD * devices)),
         out_shape=(struct((32, PD)), struct((devices, 2, PD))),
+        compiler_params=grant(6),
         name="last",
     )(columns, current, weights, degree, table, lists)
     grams = lax.all_to_all(gram, GRP_REP, 0, 0, tiled=True)
     vectors = pl.pallas_call(
-        finish_kernel, out_shape=struct((32, PD)), name="finish"
+        finish_kernel,
+        out_shape=struct((32, PD)),
+        compiler_params=grant(6),
+        name="finish",
     )(grams, current)
     return (alignment, vectors)
 

time: 130 us -> 115 us (0.88); the launches traced: 129 us -> 116 us
  Pallas kernels: 32.2 us -> 20.1 us
  other arithmetic: 3.12 us -> 0 us
    all_to_all x1, blocking collectives: 40.7 us -> 43.5 us  [exchange(): received = lax.all_to_all(sent, REP, 0, 0, tiled=True)]
    all_to_all x2, blocking collectives: 22 us -> 19.4 us  [shards(): columns = lax.all_to_all(columns, REP, 0, 0, tiled=True)]
    reduce_sum x2 -> x0, other arithmetic: 2.57 us -> none  [the longest x1 1.29 us: shards(): total = jnp.sum(truncation)]
    pallas_call x1, Pallas kernels: 8.59 us -> 6.08 us  [shards(): pl.pallas_call(local_kernel, out_shape=(struct((HEAD + FULL, 2 * PD), BF1...]
    pallas_call x1, Pallas kernels: 6.98 us -> 4.86 us  [exchange(): pl.pallas_call(functools.partial(far_kernel, size), grid=(steps,), out_sh...]
    pallas_call x2, Pallas kernels: 5.66 us -> 3.66 us  [the longest x1 2.35 us: shards(): pl.pallas_call(slot_kernel, out_shape=(struct((1,), jnp.int32), struct((N...]
    pallas_call x1, Pallas kernels: 2.22 us -> 0.58 us  [shards(): pl.pallas_call(middle_kernel, out_shape=(struct((32, PD)), struct((PEERS,...]
    pallas_call x1, Pallas kernels: 3.71 us -> 2.14 us  [shards(): pl.pallas_call(first_kernel, out_shape=(struct((2, NB, PD)), struct((2, P...]
  transfers between devices with their start and end apart: 2 -> 2, of which waited for: 1 -> 1; matrix products, arithmetic and copies ran while one was open for 3% -> 1% of each run, Pallas kernels for 7% -> 5%
where the time goes in v4:
time: 115 us; the launch traced here: 116 us
  blocking collectives  62.9 us (55%)
  Pallas kernels  20.1 us (17%)
  starting transfers between devices  18.6 us (16%)
  waiting for transfers between devices  9.54 us (8%)
  local copies, waits for them, and re-layouts  3.16 us (3%)
  between operations  1.39 us (1%)
    all_to_all x1, blocking collectives, exchange(): received = lax.all_to_all(sent, REP, 0, 0, tiled=True)  43.5 us
    all_to_all x2, blocking collectives, shards(): columns = lax.all_to_all(columns, REP, 0, 0, tiled=True)  19.4 us
    all_to_all x1, starting transfers between devices, shards(): grams = lax.all_to_all(gram, GRP_REP, 0, 0, tiled=True)  10.2 us
    all_to_all x1, waiting for transfers between devices, shards(): grams = lax.all_to_all(gram, GRP_REP, 0, 0, tiled=True)  9.54 us
    all_to_all x1, starting transfers between devices, shards(): asked = lax.all_to_all(requests, REP, 0, 0, tiled=True)  8.43 us
    pallas_call x1, Pallas kernels, shards(): pl.pallas_call(local_kernel, out_shape=(struct((HEAD + FULL, 2 * PD), BF1...  6.08 us
    pallas_call x1, Pallas kernels, exchange(): pl.pallas_call(functools.partial(far_kernel, size), grid=(steps,), out_sh...  4.86 us
    unnamed x13, local copies, waits for them, and re-layouts  3.16 us
  transfers between devices with their start and end apart: 2, of which 1 were waited for; matrix products, arithmetic and copies ran while one was open for 1% of the time, Pallas kernels for 5%

profile of v4, /device:TPU:1, one launch (start us, length us, event | category | flops | bytes accessed | tf_op | source)
XLA Modules:
  0.0 115.9 jit_solution(8846777966710404628)
XLA Ops:
  0.6 0.0 copy-start
  0.6 0.7 copy-done
  1.4 2.4 %slots.1 = (s32[1]{0:T(128)}, s32[56,128]{1,0:T(8,128)S(1)}, f32[8,128]{1,0:T(8,128)S(1)}, f32[16,128]{1,0:T(8,128)S(1)}, f32[16,8,128]{2,1,0:T(8,128)}) custom-call(s32[16]{0:T(128)} %trunc_ref.3, s32[50,128]{1,0:T(8,128)S(1)} %copy-done), custom_call_target="tpu_custom_call" | custom-call | tf_op jit(solution)/shard_map/slots/pallas_call | solution.py:516
  3.7 8.4 %all-to-all-start.8 = ((f32[16,8,128]{2,1,0:T(8,128)}), f32[16,8,128]{2,1,0:T(8,128)S(1)}, u32[]{:S(2)}, u32[]{:S(2)}) async-start(f32[16,8,128]{2,1,0:T(8,128)} %get-tuple-element.121), calls=%async_computation.8 | async-start | bytes 131072 | tf_op jit(solution)/shard_map/all_to_all | solution.py:535
  12.2 0.0 copy-start.2
  12.2 0.7 copy-done.2
  12.9 1.0 copy-done.4
  13.9 6.1 %local.1 = (bf16[1056,256]{1,0:T(8,128)(2,1)S(1)}, f32[128,128]{1,0:T(8,128)S(1)}, f32[128,128]{1,0:T(8,128)S(1)}, f32[128,128]{1,0:T(8,128)S(1)}) custom-call(s32[16]{0:T(128)} %trunc_ref.3, bf16[128,2048]{1,0:T(8,128)(2,1)S(1)} %copy-done.4, f32[32,128]{1,0:T(8,128)S(1)} %copy-done.2), custom_call_target="tpu_custom_call" | custom-call | flops 20000000000 | bytes 1000000 | tf_op jit(solution)/shard_map/local/pallas_call | solution.py:536
  20.7 0.0 all-to-all-done.8.rx_ref
  20.7 0.0 copy-start.1
  20.7 0.0 copy-start.3
  20.7 50.2 %conditional.1 = ((f32[8,8,128]{2,1,0:T(8,128)S(1)}, f32[16,16,128]{2,1,0:T(8,128)S(1)})) conditional(s32[]{:T(128)} %bitcast, (f32[16,8,128]{2,1,0:T(8,128)S(1)}, bf16[1056,256]{1,0:T(8,128)(2,1)S(1)}, s32[16]{0:T(128)S(1)}, f32[16,128]{1,0:T(8,128)S(1)}) %tuple.51, (f32[16,8,128]{2,1,0:T(8,128)S(1)}, ...), branch_computations={%region_0.0_spmd, %region_1.0_spmd, %region_2.0_spmd, %region_3.0_... | conditional | bytes 8650760 | solution.py:552
  20.8 1.5 %pick.12 = bf16[16,736,128]{2,1,0:T(8,128)(2,1)S(1)} custom-call(f32[16,8,128]{2,1,0:T(8,128)S(1)} %get-tuple-element.83.rx_ref, bf16[1056,256]{1,0:T(8,128)(2,1)S(1)} %get-tuple-element.82.pack_ref), custom_call_target="tpu_custom_call" | custom-call | tf_op jit(solution)/shard_map/cond/branch_4_fun/pick/pallas_call | solution.py:479
  22.3 43.5 %all_to_all.56.recv_ref = bf16[16,736,128]{2,1,0:T(8,128)(2,1)S(1)} all-to-all(bf16[16,736,128]{2,1,0:T(8,128)(2,1)S(1)} %pick.12), channel_id=1, replica_groups=mesh['grp_0'=4,'grp_1'=2,'rep_0'=4,'rep_1'=4] {'rep_0','rep_1'}, dimensions={0} | all-to-all | bytes 6029312 | tf_op jit(solution)/shard_map/cond/branch_4_fun/all_to_all | solution.py:488
  65.8 4.9 %far.12 = (f32[8,8,128]{2,1,0:T(8,128)S(1)}, f32[16,16,128]{2,1,0:T(8,128)S(1)}) custom-call(s32[16]{0:T(128)S(1)} %get-tuple-element.80.trunc_ref, f32[16,128]{1,0:T(8,128)S(1)} %get-tuple-element.81.names_ref, bf16[1056,256]{1,0:T(8,128)(2,1)S(1)} %get-tuple-element.82.pack_ref, bf16[16,736,128]{2,1,0:T(8,128)(2,1)S(1)} %all_to_all.56.recv_ref), custom_call_target="tpu_custom_call" | custom-call | tf_op jit(solution)/shard_map/cond/branch_4_fun/far/pallas_call | solution.py:489
  70.9 2.1 %first.1 = (f32[2,50,128]{2,1,0:T(8,128)S(1)}, f32[2,128,128]{2,1,0:T(8,128)S(1)}, f32[8,128]{1,0:T(8,128)S(1)}, f32[32,128]{1,0:T(8,128)S(1)}, f32[16,16,128]{2,1,0:T(8,128)S(1)}) custom-call(s32[50,128]{1,0:T(8,128)S(1)} %copy-done.1, s32[56,128]{1,0:T(8,128)S(1)} %get-tuple-element.118.code_ref, f32[8,128]{1,0:T(8,128)S(1)} %get-tuple-element.119.lists_ref, ...), custom_call_target="tpu_custom_call" | custom-call | tf_op jit(solution)/shard_map/first/pallas_call | solution.py:557
  73.0 9.5 %all_to_all.60.recv_ref = f32[16,16,128]{2,1,0:T(8,128)S(1)} all-to-all(f32[16,16,128]{2,1,0:T(8,128)S(1)} %get-tuple-element.130), channel_id=1, replica_groups=mesh['grp_0'=4,'grp_1'=2,'rep_0'=4,'rep_1'=4] {'rep_0','rep_1'}, dimensions={0} | all-to-all | bytes 262144 | tf_op jit(solution)/shard_map/all_to_all | solution.py:574
  82.5 0.6 middle.1
  83.1 9.9 %all_to_all.61.recv_ref = f32[16,16,128]{2,1,0:T(8,128)S(1)} all-to-all(f32[16,16,128]{2,1,0:T(8,128)S(1)} %get-tuple-element.134), channel_id=1, replica_groups=mesh['grp_0'=4,'grp_1'=2,'rep_0'=4,'rep_1'=4] {'rep_0','rep_1'}, dimensions={0} | all-to-all | bytes 262144 | tf_op jit(solution)/shard_map/all_to_all | solution.py:581
  93.0 1.2 %last.1 = (f32[32,128]{1,0:T(8,128)S(1)}, f32[128,2,128]{2,1,0:T(2,128)}) custom-call(f32[16,16,128]{2,1,0:T(8,128)S(1)} %all_to_all.61.recv_ref, f32[32,128]{1,0:T(8,128)S(1)} %get-tuple-element.135.cur_ref, f32[2,128,128]{2,1,0:T(8,128)S(1)} %get-tuple-element.132.weights_ref, f32[8,128]{1,0:T(8,128)S(1)} %get-tuple-element.133.degree_ref, ...), custom_call_target="tpu_custom_call" | custom-call | tf_op jit(solution)/shard_map/last/pallas_call | solution.py:582
  94.2 10.2 %all-to-all-start.11 = ((f32[128,2,128]{2,1,0:T(2,128)}), f32[128,2,128]{2,1,0:T(2,128)S(1)}, u32[]{:S(2)}, u32[]{:S(2)}) async-start(f32[128,2,128]{2,1,0:T(2,128)} %get-tuple-element.136), calls=%async_computation.11 | async-start | bytes 262144 | tf_op jit(solution)/shard_map/all_to_all | solution.py:588
  104.4 0.6 copy.6
  105.0 9.5 %all-to-all-done.11.grams_ref = f32[128,2,128]{2,1,0:T(2,128)S(1)} async-done(((f32[128,2,128]{2,1,0:T(2,128)}), f32[128,2,128]{2,1,0:T(2,128)S(1)}, u32[]{:S(2)}, u32[]{:S(2)}) %all-to-all-start.11) | async-done | bytes 131104 | tf_op jit(solution)/shard_map/all_to_all | solution.py:588
  114.6 1.3 %finish.1 = f32[32,128]{1,0:T(8,128)} custom-call(f32[128,2,128]{2,1,0:T(2,128)S(1)} %all-to-all-done.11.grams_ref, f32[32,128]{1,0:T(8,128)S(1)} %get-tuple-element.137.cur_ref), custom_call_target="tpu_custom_call" | custom-call | tf_op jit(solution)/shard_map/finish/pallas_call | solution.py:589
  (5 shorter events, 0.0 us)
Async XLA Ops:
  0.6 0.8 copy-start
  3.7 16.9 %all-to-all-start.8 = ((f32[16,8,128]{2,1,0:T(8,128)}), f32[16,8,128]{2,1,0:T(8,128)S(1)}, u32[]{:S(2)}, u32[]{:S(2)}) async-start(f32[16,8,128]{2,1,0:T(8,128)} %get-tuple-element.121), calls=%async_computation.8 | async-start | bytes 131072 | tf_op jit(solution)/shard_map/all_to_all | solution.py:535
  12.2 0.7 copy-start.2
  12.9 1.0 copy-start.4
  13.9 6.8 %copy-start.5 = (s32[16]{0:T(128)S(1)}, s32[16]{0:T(128)}, u32[]{:S(2)}) copy-start(s32[16]{0:T(128)} %trunc_ref.3) | copy-start | bytes 196
  20.7 50.2 %copy-start.1 = (s32[50,128]{1,0:T(8,128)S(1)}, s32[50,128]{1,0:T(8,128)}, u32[]{:S(2)}) copy-start(s32[50,128]{1,0:T(8,128)} %nb_ref.3) | copy-start | bytes 76804
  20.7 50.2 %copy-start.3 = (f32[32,128]{1,0:T(8,128)S(1)}, f32[32,128]{1,0:T(8,128)}, u32[]{:S(2)}) copy-start(f32[32,128]{1,0:T(8,128)} %init_ref.3) | copy-start | bytes 49156
  94.2 20.4 %all-to-all-start.11 = ((f32[128,2,128]{2,1,0:T(2,128)}), f32[128,2,128]{2,1,0:T(2,128)S(1)}, u32[]{:S(2)}, u32[]{:S(2)}) async-start(f32[128,2,128]{2,1,0:T(2,128)} %get-tuple-element.136), calls=%async_computation.11 | async-start | bytes 262144 | tf_op jit(solution)/shard_map/all_to_all | solution.py:588

commit v5 on v4

--- a/solution.py
+++ b/solution.py
@@ -17,7 +17,7 @@
 CAP = 64
 CW = 2048
 FULL = RAD * ANG
-SIZES = (384, 512, 576, 640, 704, 768, 896, FULL)
+SIZES = (384, 512, 544, 576, 608, 640, 672, 704, 736, 768, 896, FULL)
 HEAD = 2 * VEC
 PEERS = 16
 PAIRS = PEERS // 2
@@ -79,9 +79,17 @@
 
 
 def slot_kernel(
-    trunc_ref, nb_ref, which_ref, code_ref, lists_ref, names_ref, req_ref,
-    nbp_ref, a_ref, b_ref,
+    trunc_ref, nb_hbm, coef_hbm, init_hbm,
+    which_ref, code_ref, lists_ref, names_ref, req_ref, coef_ref, init_ref,
+    nb_ref, nbp_ref, a_ref, b_ref, sem_ref,
 ):
+    bring = (
+        pltpu.make_async_copy(coef_hbm, coef_ref, sem_ref.at[0]),
+        pltpu.make_async_copy(init_hbm, init_ref, sem_ref.at[1]),
+    )
+    slots = pltpu.make_async_copy(nb_hbm, nb_ref, sem_ref.at[2])
+    for copy in (slots,) + bring:
+        copy.start()
     total = trunc_ref[0]
     for q in range(1, RAD):
         total = total + trunc_ref[q]
@@ -90,6 +98,7 @@
         which = which + (total > size).astype(jnp.int32)
     which_ref[0] = which
     start, me = place()
+    slots.wait()
     nbp_ref[...] = jnp.full((NBP, PD), -1, jnp.int32)
     nbp_ref[:NB, :] = nb_ref[...] - start
     local = nbp_ref[...]
@@ -135,6 +144,8 @@
         r = p // 2
         req_ref[p] = jnp.broadcast_to(rows[r : r + 1, :], (8, PD))
         names_ref[p : p + 1, :] = rows[PAIRS + r : PAIRS + r + 1, :]
+    for copy in bring:
+        copy.wait()
 
 
 def wanted_row(rx_ref, r):
@@ -351,20 +362,18 @@
     start, me = place()
     local = nb_ref[...] - start
     near = (local >> 7) == me
-    near_ref[...] = jnp.where(near, local & (PD - 1), -1)
-    rows = iota((PD, PD), 0)
+    near_ref[...] = jnp.full((PD, PD), -1.0, F32)
+    near_ref[:NB, :] = jnp.where(near, local & (PD - 1), -1).astype(F32)
+    rows = iota((PD, PD), 0).astype(F32)
     counts = jnp.zeros((PD, PD), F32)
-    energy = []
-    m_re = []
-    m_im = []
     for n in range(NB):
-        mine = rows == near_ref[n : n + 1, :]
-        counts = counts + jnp.where(mine, 1.0, 0.0)
-        energy.append(jnp.sum(jnp.where(mine, e_ref[...], 0.0), axis=0, keepdims=True))
-        m_re.append(jnp.sum(jnp.where(mine, re_ref[...], 0.0), axis=0, keepdims=True))
-        m_im.append(jnp.sum(jnp.where(mine, im_ref[...], 0.0), axis=0, keepdims=True))
-    pad = [jnp.zeros((NBP - NB, PD), F32)]
-    values = [jnp.concatenate(v + pad, axis=0) for v in (energy, m_re, m_im)]
+        counts = counts + jnp.where(rows == near_ref[n : n + 1, :], 1.0, 0.0)
+    named = near_ref[...].T.astype(jnp.int32)
+    inside = jnp.maximum(named, 0)
+    values = []
+    for ref, sign in ((e_ref, 1.0), (re_ref, 1.0), (im_ref, -1.0)):
+        found = jnp.take_along_axis(ref[...], inside, axis=1, mode="promise_in_bounds")
+        values.append(jnp.where(named >= 0, sign * found, 0.0).T[:NBP])
     code = code_ref[...]
     pair = code >> 7
     lane = code & (PD - 1)
@@ -375,8 +384,8 @@
             found = jnp.take_along_axis(row, lane, axis=1, mode="promise_in_bounds")
             values[v] = jnp.where(mine, found, values[v])
     below = values[0] + EPS
-    align_ref[0] = (values[1] / below)[:NB]
-    align_ref[1] = (values[2] / below)[:NB]
+    align_ref[:, 0, :] = (values[1] / below)[:NB]
+    align_ref[:, 1, :] = (values[2] / below)[:NB]
     degree = EPS + jnp.sum(values[0], axis=0, keepdims=True)
     degree_ref[...] = jnp.broadcast_to(degree, (8, PD))
     w_re = counts * re_ref[...]
@@ -464,6 +473,7 @@
 
 SMEM = pl.BlockSpec(memory_space=pltpu.SMEM)
 VMEM = pl.BlockSpec(memory_space=pltpu.VMEM)
+HBM = pl.BlockSpec(memory_space=pltpu.HBM)
 
 
 def grant(mib):
@@ -513,7 +523,7 @@
     groups = lax.axis_size(GRP)
     replicas = lax.axis_size(REP)
     devices = groups * replicas
-    which, code, lists, names, requests = pl.pallas_call(
+    which, code, lists, names, requests, coefficients, initial = pl.pallas_call(
         slot_kernel,
         out_shape=(
             struct((1,), jnp.int32),
@@ -521,17 +531,27 @@
             struct((PAIRS, PD)),
             struct((PEERS, PD)),
             struct((PEERS, 8, PD)),
+            struct((PD, CW), BF16),
+            struct((32, PD)),
         ),
-        in_specs=[SMEM, VMEM],
-        out_specs=(SMEM, VMEM, VMEM, VMEM, VMEM),
+        in_specs=[SMEM, HBM, HBM, HBM],
+        out_specs=(SMEM,) + (VMEM,) * 6,
         compiler_params=grant(6),
         scratch_shapes=[
+            pltpu.VMEM((NB, PD), jnp.int32),
             pltpu.VMEM((NBP, PD), jnp.int32),
             pltpu.VMEM((2 * PAIRS, NB * PD), BF16),
             pltpu.VMEM((PD, NB * PD), BF16),
+            pltpu.SemaphoreType.DMA((3,)),
         ],
         name="slots",
-    )(truncation, neighbours)
+    )(
+        truncation,
+        *(
+            pltpu.with_memory_space_constraint(x, pltpu.HBM)
+            for x in (neighbours, coefficients, initial)
+        ),
+    )
     asked = lax.all_to_all(requests, REP, 0, 0, tiled=True)
     packed, e_own, re_own, im_own = pl.pallas_call(
         local_kernel,
@@ -557,7 +577,7 @@
     alignment, weights, degree, current, columns = pl.pallas_call(
         first_kernel,
         out_shape=(
-            struct((2, NB, PD)),
+            struct((NB, 2, PD)),
             struct((2, PD, PD)),
             struct((8, PD)),
             struct((32, PD)),
@@ -565,7 +585,7 @@
         ),
         in_specs=[VMEM] * 10,
         compiler_params=grant(6),
-        scratch_shapes=[pltpu.VMEM((NB, PD), jnp.int32)],
+        scratch_shapes=[pltpu.VMEM((PD, PD), F32)],
         name="first",
     )(
         neighbours, code, lists, table, e_own, re_own, im_own,
@@ -592,7 +612,7 @@
         compiler_params=grant(6),
         name="finish",
     )(grams, current)
-    return (alignment, vectors)
+    return (jnp.transpose(alignment, (1, 0, 2)), vectors)
 
 
 def solution(mesh):

time: 115 us -> 108 us (0.939)
  blocking collectives: 62.9 us -> 79 us
  starting transfers between devices: 18.6 us -> 8.43 us
  waiting for transfers between devices: 9.54 us -> 0.01 us
  local copies, waits for them, and re-layouts: 3.16 us -> 0.01 us
    all_to_all x0 -> x1, blocking collectives: none -> 20.2 us  [shards(): grams = lax.all_to_all(gram, GRP_REP, 0, 0, tiled=True)]
    all_to_all x1 -> x0, starting transfers between devices: 10.2 us -> none  [shards(): grams = lax.all_to_all(gram, GRP_REP, 0, 0, tiled=True)]
    all_to_all x1 -> x0, waiting for transfers between devices: 9.54 us -> none  [shards(): grams = lax.all_to_all(gram, GRP_REP, 0, 0, tiled=True)]
    all_to_all x1, blocking collectives: 43.5 us -> 39.3 us  [exchange(): received = lax.all_to_all(sent, REP, 0, 0, tiled=True)]
    unnamed x13 -> x4, local copies, waits for them, and re-layouts: 3.16 us -> 0.01 us
  transfers between devices with their start and end apart: 2 -> 1, of which waited for: 1 -> 0; matrix products, arithmetic and copies ran while one was open for 1% -> 0% of each run, Pallas kernels for 5% -> 6%
where the time goes in v5:
time: 108 us; the launch traced here: 109 us
  blocking collectives  79 us (73%)
  Pallas kernels  19.4 us (18%)
  starting transfers between devices  8.43 us (8%)
  between operations  1.36 us (1%)
    all_to_all x1, blocking collectives, exchange(): received = lax.all_to_all(sent, REP, 0, 0, tiled=True)  39.3 us
    all_to_all x1, blocking collectives, shards(): grams = lax.all_to_all(gram, GRP_REP, 0, 0, tiled=True)  20.2 us
    all_to_all x2, blocking collectives, shards(): columns = lax.all_to_all(columns, REP, 0, 0, tiled=True)  19.6 us
    all_to_all x1, starting transfers between devices, shards(): asked = lax.all_to_all(requests, REP, 0, 0, tiled=True)  8.43 us
    pallas_call x1, Pallas kernels, shards(): pl.pallas_call(local_kernel, out_shape=(struct((HEAD + FULL, 2 * PD), BF1...  6.08 us
    pallas_call x1, Pallas kernels, exchange(): pl.pallas_call(functools.partial(far_kernel, size), grid=(steps,), out_sh...  4.56 us
    pallas_call x1, Pallas kernels, shards(): pl.pallas_call(slot_kernel, out_shape=(struct((1,), jnp.int32), struct((N...  3.12 us
  transfers between devices with their start and end apart: 1, of which 0 were waited for; matrix products, arithmetic and copies ran while one was open for 0% of the time, Pallas kernels for 6%

profile of v5, /device:TPU:1, one launch (start us, length us, event | category | flops | bytes accessed | tf_op | source)
XLA Modules:
  0.0 108.5 jit_solution(178432310303383858)
XLA Ops:
  0.6 3.1 %slots.1 = (s32[1]{0:T(128)}, s32[56,128]{1,0:T(8,128)S(1)}, f32[8,128]{1,0:T(8,128)S(1)}, f32[16,128]{1,0:T(8,128)S(1)}, f32[16,8,128]{2,1,0:T(8,128)}, /*index...) custom-call(s32[16]{0:T(128)} %trunc_ref.3, s32[50,128]{1,0:T(8,128)} %nb_ref.1, bf16[128,2048]{1,0:T(8,128)(2,1)} %coef_hbm.1, ...), custom_call_target="tpu_custom_call" | custom-call | tf_op jit(solution)/shard_map/slots/pallas_call | solution.py:526
  3.8 8.4 %all-to-all-start.12 = ((f32[16,8,128]{2,1,0:T(8,128)}), f32[16,8,128]{2,1,0:T(8,128)S(1)}, u32[]{:S(2)}, u32[]{:S(2)}) async-start(f32[16,8,128]{2,1,0:T(8,128)} %get-tuple-element.171), calls=%async_computation.12 | async-start | bytes 131072 | tf_op jit(solution)/shard_map/all_to_all | solution.py:555
  12.2 0.0 copy-start.1
  12.2 6.1 %local.1 = (bf16[1056,256]{1,0:T(8,128)(2,1)S(1)}, f32[128,128]{1,0:T(8,128)S(1)}, f32[128,128]{1,0:T(8,128)S(1)}, f32[128,128]{1,0:T(8,128)S(1)}) custom-call(s32[16]{0:T(128)} %trunc_ref.3, bf16[128,2048]{1,0:T(8,128)(2,1)S(1)} %get-tuple-element.172.coef_ref, f32[32,128]{1,0:T(8,128)S(1)} %get-tuple-element.173.init_ref), custom_call_target="tpu_custom_call" | custom-call | flops 20000000000 | bytes 1000000 | tf_op jit(solution)/shard_map/local/pallas_call | solution.py:556
  18.9 0.0 all-to-all-done.12.rx_ref
  19.0 0.0 copy-done.1
  19.0 0.0 copy-start
  19.0 45.6 %conditional.1 = ((f32[8,8,128]{2,1,0:T(8,128)S(1)}, f32[16,16,128]{2,1,0:T(8,128)S(1)})) conditional(s32[]{:T(128)} %bitcast, (f32[16,8,128]{2,1,0:T(8,128)S(1)}, bf16[1056,256]{1,0:T(8,128)(2,1)S(1)}, s32[16]{0:T(128)S(1)}, f32[16,128]{1,0:T(8,128)S(1)}) %tuple.70, (f32[16,8,128]{2,1,0:T(8,128)S(1)}, ...), branch_computations={%region_0.0_spmd, %region_1.0_spmd, %region_2.0_spmd, %region_3.0_... | conditional | bytes 8650760 | solution.py:572
  19.0 1.4 %pick.16 = bf16[16,640,128]{2,1,0:T(8,128)(2,1)S(1)} custom-call(f32[16,8,128]{2,1,0:T(8,128)S(1)} %get-tuple-element.115.rx_ref, bf16[1056,256]{1,0:T(8,128)(2,1)S(1)} %get-tuple-element.114.pack_ref), custom_call_target="tpu_custom_call" | custom-call | tf_op jit(solution)/shard_map/cond/branch_4_fun/pick/pallas_call | solution.py:489
  20.5 39.3 %all_to_all.72.recv_ref = bf16[16,640,128]{2,1,0:T(8,128)(2,1)S(1)} all-to-all(bf16[16,640,128]{2,1,0:T(8,128)(2,1)S(1)} %pick.16), channel_id=1, replica_groups=mesh['grp_0'=4,'grp_1'=2,'rep_0'=4,'rep_1'=4] {'rep_0','rep_1'}, dimensions={0} | all-to-all | bytes 5242880 | tf_op jit(solution)/shard_map/cond/branch_4_fun/all_to_all | solution.py:498
  59.7 4.6 %far.16 = (f32[8,8,128]{2,1,0:T(8,128)S(1)}, f32[16,16,128]{2,1,0:T(8,128)S(1)}) custom-call(s32[16]{0:T(128)S(1)} %get-tuple-element.112.trunc_ref, f32[16,128]{1,0:T(8,128)S(1)} %get-tuple-element.113.names_ref, bf16[1056,256]{1,0:T(8,128)(2,1)S(1)} %get-tuple-element.114.pack_ref, bf16[16,640,128]{2,1,0:T(8,128)(2,1)S(1)} %all_to_all.72.recv_ref), custom_call_target="tpu_custom_call" | custom-call | tf_op jit(solution)/shard_map/cond/branch_4_fun/far/pallas_call | solution.py:499
  64.5 0.0 copy-done
  64.5 1.7 %first.1 = (f32[50,2,128]{2,1,0:T(2,128)}, f32[2,128,128]{2,1,0:T(8,128)S(1)}, f32[8,128]{1,0:T(8,128)S(1)}, f32[32,128]{1,0:T(8,128)S(1)}, f32[16,16,128]{2,1,0:T(8,128)S(1)}) custom-call(s32[50,128]{1,0:T(8,128)S(1)} %copy-done, s32[56,128]{1,0:T(8,128)S(1)} %get-tuple-element.168.code_ref, f32[8,128]{1,0:T(8,128)S(1)} %get-tuple-element.169.lists_ref, ...), custom_call_target="tpu_custom_call" | custom-call | tf_op jit(solution)/shard_map/first/pallas_call | solution.py:577
  66.3 9.6 %all_to_all.80.recv_ref = f32[16,16,128]{2,1,0:T(8,128)S(1)} all-to-all(f32[16,16,128]{2,1,0:T(8,128)S(1)} %get-tuple-element.182), channel_id=1, replica_groups=mesh['grp_0'=4,'grp_1'=2,'rep_0'=4,'rep_1'=4] {'rep_0','rep_1'}, dimensions={0} | all-to-all | bytes 262144 | tf_op jit(solution)/shard_map/all_to_all | solution.py:594
  75.9 0.6 middle.1
  76.5 9.9 %all_to_all.81.recv_ref = f32[16,16,128]{2,1,0:T(8,128)S(1)} all-to-all(f32[16,16,128]{2,1,0:T(8,128)S(1)} %get-tuple-element.186), channel_id=1, replica_groups=mesh['grp_0'=4,'grp_1'=2,'rep_0'=4,'rep_1'=4] {'rep_0','rep_1'}, dimensions={0} | all-to-all | bytes 262144 | tf_op jit(solution)/shard_map/all_to_all | solution.py:601
  86.4 0.6 last.1
  87.0 20.2 %all_to_all.82.grams_ref = f32[128,2,128]{2,1,0:T(2,128)S(1)} all-to-all(f32[128,2,128]{2,1,0:T(2,128)S(1)} %get-tuple-element.188), channel_id=1, replica_groups=mesh['grp_0'=4,'grp_1'=2,'rep_0'=4,'rep_1'=4] {'grp_0','grp_1','rep_0','..., dimensions={0} | all-to-all | bytes 262144 | tf_op jit(solution)/shard_map/all_to_all | solution.py:608
  107.2 1.3 %finish.1 = f32[32,128]{1,0:T(8,128)} custom-call(f32[128,2,128]{2,1,0:T(2,128)S(1)} %all_to_all.82.grams_ref, f32[32,128]{1,0:T(8,128)S(1)} %get-tuple-element.189.cur_ref), custom_call_target="tpu_custom_call" | custom-call | tf_op jit(solution)/shard_map/finish/pallas_call | solution.py:609
Async XLA Ops:
  3.8 15.2 %all-to-all-start.12 = ((f32[16,8,128]{2,1,0:T(8,128)}), f32[16,8,128]{2,1,0:T(8,128)S(1)}, u32[]{:S(2)}, u32[]{:S(2)}) async-start(f32[16,8,128]{2,1,0:T(8,128)} %get-tuple-element.171), calls=%async_computation.12 | async-start | bytes 131072 | tf_op jit(solution)/shard_map/all_to_all | solution.py:555
  12.2 6.8 %copy-start.1 = (s32[16]{0:T(128)S(1)}, s32[16]{0:T(128)}, u32[]{:S(2)}) copy-start(s32[16]{0:T(128)} %trunc_ref.3) | copy-start | bytes 196
  19.0 45.6 %copy-start = (s32[50,128]{1,0:T(8,128)S(1)}, s32[50,128]{1,0:T(8,128)}, u32[]{:S(2)}) copy-start(s32[50,128]{1,0:T(8,128)} %nb_ref.1) | copy-start | bytes 76804

commit v6 on v5

--- a/solution.py
+++ b/solution.py
@@ -22,6 +22,7 @@
 PEERS = 16
 PAIRS = PEERS // 2
 WIDE = 4
+GROUP = 8
 GRP = ("grp_0", "grp_1")
 REP = ("rep_0", "rep_1")
 GRP_REP = ("grp_0", "grp_1", "rep_0", "rep_1")
@@ -197,43 +198,51 @@
 
 def own_pairs(trunc_ref, e_ref, re_ref, im_ref, xt_ref, s_ref):
     kept = kept_rows(trunc_ref, 2 * RAD, PD)
-
-    def per_frequency(k, carry):
-        rows = xt_ref[pl.ds(k, 2 * RAD, stride=ANG), :]
-        masked = jnp.where(kept > k, rows, 0.0)
-        turned = jnp.concatenate([masked[RAD:], -masked[:RAD]], axis=0)
-        right = jnp.concatenate([masked, turned], axis=1).astype(BF16)
-        s_ref[k] = lax.dot_general(
-            rows.astype(BF16), right, TN, preferred_element_type=F32
-        )
-        return carry
-
-    lax.fori_loop(0, ANG, per_frequency, 0, unroll=8)
-
-    def per_rows(b, carry):
-        sub = pl.ds(b * 8, 8)
-        last_re = s_ref[0, sub, :PD]
-        energy = last_re * last_re
-        re = s_ref[1, sub, :PD]
-        im = s_ref[1, sub, PD:]
-        half = re * re + im * im
-        first_re = last_re * re
-        first_im = last_re * im
-        m_re = jnp.zeros_like(re)
-        m_im = jnp.zeros_like(re)
-        for k in range(2, ANG):
-            next_re = s_ref[k, sub, :PD]
-            next_im = s_ref[k, sub, PD:]
-            half = half + (next_re * next_re + next_im * next_im)
-            m_re = m_re + (re * next_re + im * next_im)
-            m_im = m_im + (im * next_re - re * next_im)
-            re, im = next_re, next_im
-        e_ref[sub, :] = energy + 0.5 * half
-        re_ref[sub, :] = first_re + 0.5 * m_re
-        im_ref[sub, :] = 0.5 * m_im - first_im
-        return carry
-
-    lax.fori_loop(0, PD // 8, per_rows, 0)
+    e_ref[...] = jnp.zeros((PD, PD), F32)
+    re_ref[...] = jnp.zeros((PD, PD), F32)
+    im_ref[...] = jnp.zeros((PD, PD), F32)
+
+    def sums(first):
+        for b in range(PD // 8):
+            sub = slice(b * 8, (b + 1) * 8)
+            energy = e_ref[sub, :]
+            m_re = re_ref[sub, :]
+            m_im = im_ref[sub, :]
+            before = max(first - 1, 0)
+            re = s_ref[before, sub, :PD]
+            im = s_ref[before, sub, PD:]
+            for k in range(first, first + GROUP):
+                if k == 0:
+                    energy = energy + re * re
+                    continue
+                next_re = s_ref[k, sub, :PD]
+                next_im = s_ref[k, sub, PD:]
+                half_re = 0.5 * next_re
+                half_im = 0.5 * next_im
+                energy = energy + (half_re * next_re + half_im * next_im)
+                if k == 1:
+                    m_re = m_re + re * next_re
+                    m_im = m_im - re * next_im
+                else:
+                    m_re = m_re + (re * half_re + im * half_im)
+                    m_im = m_im + (im * half_re - re * half_im)
+                re, im = next_re, next_im
+            e_ref[sub, :] = energy
+            re_ref[sub, :] = m_re
+            im_ref[sub, :] = m_im
+
+    for first in range(0, ANG, GROUP):
+        for k in range(first, first + GROUP):
+            rows = xt_ref[pl.ds(k, 2 * RAD, stride=ANG), :]
+            masked = rows if k < 16 else jnp.where(kept > k, rows, 0.0)
+            turned = jnp.concatenate([masked[RAD:], -masked[:RAD]], axis=0)
+            right = jnp.concatenate([masked, turned], axis=1).astype(BF16)
+            s_ref[k] = lax.dot_general(
+                rows.astype(BF16), right, TN, preferred_element_type=F32
+            )
+        if first > 0:
+            sums(first - GROUP)
+    sums(ANG - GROUP)
 
 
 def far_kernel(
@@ -269,17 +278,19 @@
         cross_ref[p, :kept, :] = own * pltpu.roll(arrived, CAP, 1)
         parts = recv_ref[p, :HEAD, :].astype(F32)
         cur_ref[p] = parts[:VEC] + parts[VEC:]
-    for p in range(WIDE):
-        sum_re = jnp.zeros((ANG, PD), F32)
-        sum_im = jnp.zeros((ANG, PD), F32)
+    for b in range(WIDE // 2):
+        both = (2 * b, 2 * b + 1)
+        totals = [[jnp.zeros((ANG, PD), F32)] * 2 for _ in both]
         offset = 0
         for q in range(RAD):
             here = pl.ds(offset, ANG)
             inside = freq < trunc_ref[q]
-            sum_re = sum_re + jnp.where(inside, same_ref[p, here, :], 0.0)
-            sum_im = sum_im + jnp.where(inside, cross_ref[p, here, :], 0.0)
+            for p in both:
+                for v, ref in enumerate((same_ref, cross_ref)):
+                    total = totals[p % 2][v]
+                    totals[p % 2][v] = total + jnp.where(inside, ref[p, here, :], 0.0)
             offset = offset + trunc_ref[q]
-        halves.append((sum_re, sum_im))
+        halves.extend(totals)
     first = first[:ANG]
     inner = (freq > 0) & (freq < ANG - 1)
     for b in range(WIDE // 2):

time: 108 us -> 108 us (level); the launches traced: 109 us -> 110 us
  Pallas kernels: 19.4 us -> 17.6 us
  waiting for transfers between devices: 0.01 us -> 1.76 us
  blocking collectives: 79 us -> 80.5 us
    pallas_call x1, Pallas kernels: 6.08 us -> 4.09 us  [shards(): pl.pallas_call(local_kernel, out_shape=(struct((HEAD + FULL, 2 * PD), BF1...]
    all_to_all x1, waiting for transfers between devices: 0.01 us -> 1.76 us  [shards(): asked = lax.all_to_all(requests, REP, 0, 0, tiled=True)]
    all_to_all x1, blocking collectives: 39.3 us -> 40.6 us  [exchange(): received = lax.all_to_all(sent, REP, 0, 0, tiled=True)]
  transfers between devices with their start and end apart: 1 -> 1, of which waited for: 0 -> 1; matrix products, arithmetic and copies ran while one was open for 0% -> 0% of each run, Pallas kernels for 6% -> 4%
where the time goes in v6:
time: 108 us; the launch traced here: 110 us
  blocking collectives  80.5 us (75%)
  Pallas kernels  17.6 us (16%)
  starting transfers between devices  8.43 us (8%)
  waiting for transfers between devices  1.76 us (2%)
  between operations  1.34 us (1%)
    all_to_all x1, blocking collectives, exchange(): received = lax.all_to_all(sent, REP, 0, 0, tiled=True)  40.6 us
    all_to_all x1, blocking collectives, shards(): grams = lax.all_to_all(gram, GRP_REP, 0, 0, tiled=True)  20.8 us
    all_to_all x2, blocking collectives, shards(): columns = lax.all_to_all(columns, REP, 0, 0, tiled=True)  19.2 us
    all_to_all x1, starting transfers between devices, shards(): asked = lax.all_to_all(requests, REP, 0, 0, tiled=True)  8.43 us
    pallas_call x1, Pallas kernels, exchange(): pl.pallas_call(functools.partial(far_kernel, size), grid=(steps,), out_sh...  4.74 us
    pallas_call x1, Pallas kernels, shards(): pl.pallas_call(local_kernel, out_shape=(struct((HEAD + FULL, 2 * PD), BF1...  4.09 us
    pallas_call x1, Pallas kernels, shards(): pl.pallas_call(slot_kernel, out_shape=(struct((1,), jnp.int32), struct((N...  3.12 us
  transfers between devices with their start and end apart: 1, of which 1 were waited for; matrix products, arithmetic and copies ran while one was open for 0% of the time, Pallas kernels for 4%

profile of v6, /device:TPU:1, one launch (start us, length us, event | category | flops | bytes accessed | tf_op | source)
XLA Modules:
  0.0 109.7 jit_solution(7350726582878263295)
XLA Ops:
  0.6 3.1 %slots.1 = (s32[1]{0:T(128)}, s32[56,128]{1,0:T(8,128)S(1)}, f32[8,128]{1,0:T(8,128)S(1)}, f32[16,128]{1,0:T(8,128)S(1)}, f32[16,8,128]{2,1,0:T(8,128)}, /*index...) custom-call(s32[16]{0:T(128)} %trunc_ref.3, s32[50,128]{1,0:T(8,128)} %nb_ref.1, bf16[128,2048]{1,0:T(8,128)(2,1)} %coef_hbm.1, ...), custom_call_target="tpu_custom_call" | custom-call | tf_op jit(solution)/shard_map/slots/pallas_call | solution.py:537
  3.8 8.4 %all-to-all-start.12 = ((f32[16,8,128]{2,1,0:T(8,128)}), f32[16,8,128]{2,1,0:T(8,128)S(1)}, u32[]{:S(2)}, u32[]{:S(2)}) async-start(f32[16,8,128]{2,1,0:T(8,128)} %get-tuple-element.171), calls=%async_computation.12 | async-start | bytes 131072 | tf_op jit(solution)/shard_map/all_to_all | solution.py:566
  12.2 0.0 copy-start.1
  12.2 4.1 %local.1 = (bf16[1056,256]{1,0:T(8,128)(2,1)S(1)}, f32[128,128]{1,0:T(8,128)S(1)}, f32[128,128]{1,0:T(8,128)S(1)}, f32[128,128]{1,0:T(8,128)S(1)}) custom-call(s32[16]{0:T(128)} %trunc_ref.3, bf16[128,2048]{1,0:T(8,128)(2,1)S(1)} %get-tuple-element.172.coef_ref, f32[32,128]{1,0:T(8,128)S(1)} %get-tuple-element.173.init_ref), custom_call_target="tpu_custom_call" | custom-call | flops 20000000000 | bytes 1000000 | tf_op jit(solution)/shard_map/local/pallas_call | solution.py:567
  17.0 1.8 %all-to-all-done.12.rx_ref = f32[16,8,128]{2,1,0:T(8,128)S(1)} async-done(((f32[16,8,128]{2,1,0:T(8,128)}), f32[16,8,128]{2,1,0:T(8,128)S(1)}, u32[]{:S(2)}, u32[]{:S(2)}) %all-to-all-start.12) | async-done | bytes 65568 | tf_op jit(solution)/shard_map/all_to_all | solution.py:566
  18.7 0.0 copy-done.1
  18.7 0.0 copy-start
  18.7 46.8 %conditional.1 = ((f32[8,8,128]{2,1,0:T(8,128)S(1)}, f32[16,16,128]{2,1,0:T(8,128)S(1)})) conditional(s32[]{:T(128)} %bitcast, (f32[16,8,128]{2,1,0:T(8,128)S(1)}, bf16[1056,256]{1,0:T(8,128)(2,1)S(1)}, s32[16]{0:T(128)S(1)}, f32[16,128]{1,0:T(8,128)S(1)}) %tuple.70, (f32[16,8,128]{2,1,0:T(8,128)S(1)}, ...), branch_computations={%region_0.0_spmd, %region_1.0_spmd, %region_2.0_spmd, %region_3.0_... | conditional | bytes 8650760 | solution.py:583
  18.7 1.5 %pick.18 = bf16[16,704,128]{2,1,0:T(8,128)(2,1)S(1)} custom-call(f32[16,8,128]{2,1,0:T(8,128)S(1)} %get-tuple-element.123.rx_ref, bf16[1056,256]{1,0:T(8,128)(2,1)S(1)} %get-tuple-element.122.pack_ref), custom_call_target="tpu_custom_call" | custom-call | tf_op jit(solution)/shard_map/cond/branch_6_fun/pick/pallas_call | solution.py:500
  20.2 40.6 %all_to_all.74.recv_ref = bf16[16,704,128]{2,1,0:T(8,128)(2,1)S(1)} all-to-all(bf16[16,704,128]{2,1,0:T(8,128)(2,1)S(1)} %pick.18), channel_id=1, replica_groups=mesh['grp_0'=4,'grp_1'=2,'rep_0'=4,'rep_1'=4] {'rep_0','rep_1'}, dimensions={0} | all-to-all | bytes 5767168 | tf_op jit(solution)/shard_map/cond/branch_6_fun/all_to_all | solution.py:509
  60.8 4.7 %far.18 = (f32[8,8,128]{2,1,0:T(8,128)S(1)}, f32[16,16,128]{2,1,0:T(8,128)S(1)}) custom-call(s32[16]{0:T(128)S(1)} %get-tuple-element.120.trunc_ref, f32[16,128]{1,0:T(8,128)S(1)} %get-tuple-element.121.names_ref, bf16[1056,256]{1,0:T(8,128)(2,1)S(1)} %get-tuple-element.122.pack_ref, bf16[16,704,128]{2,1,0:T(8,128)(2,1)S(1)} %all_to_all.74.recv_ref), custom_call_target="tpu_custom_call" | custom-call | tf_op jit(solution)/shard_map/cond/branch_6_fun/far/pallas_call | solution.py:510
  65.5 0.0 copy-done
  65.5 1.7 %first.1 = (f32[50,2,128]{2,1,0:T(2,128)}, f32[2,128,128]{2,1,0:T(8,128)S(1)}, f32[8,128]{1,0:T(8,128)S(1)}, f32[32,128]{1,0:T(8,128)S(1)}, f32[16,16,128]{2,1,0:T(8,128)S(1)}) custom-call(s32[50,128]{1,0:T(8,128)S(1)} %copy-done, s32[56,128]{1,0:T(8,128)S(1)} %get-tuple-element.168.code_ref, f32[8,128]{1,0:T(8,128)S(1)} %get-tuple-element.169.lists_ref, ...), custom_call_target="tpu_custom_call" | custom-call | tf_op jit(solution)/shard_map/first/pallas_call | solution.py:588
  67.3 9.5 %all_to_all.80.recv_ref = f32[16,16,128]{2,1,0:T(8,128)S(1)} all-to-all(f32[16,16,128]{2,1,0:T(8,128)S(1)} %get-tuple-element.182), channel_id=1, replica_groups=mesh['grp_0'=4,'grp_1'=2,'rep_0'=4,'rep_1'=4] {'rep_0','rep_1'}, dimensions={0} | all-to-all | bytes 262144 | tf_op jit(solution)/shard_map/all_to_all | solution.py:605
  76.8 0.6 middle.1
  77.4 9.6 %all_to_all.81.recv_ref = f32[16,16,128]{2,1,0:T(8,128)S(1)} all-to-all(f32[16,16,128]{2,1,0:T(8,128)S(1)} %get-tuple-element.186), channel_id=1, replica_groups=mesh['grp_0'=4,'grp_1'=2,'rep_0'=4,'rep_1'=4] {'rep_0','rep_1'}, dimensions={0} | all-to-all | bytes 262144 | tf_op jit(solution)/shard_map/all_to_all | solution.py:612
  87.0 0.6 last.1
  87.6 20.8 %all_to_all.82.grams_ref = f32[128,2,128]{2,1,0:T(2,128)S(1)} all-to-all(f32[128,2,128]{2,1,0:T(2,128)S(1)} %get-tuple-element.188), channel_id=1, replica_groups=mesh['grp_0'=4,'grp_1'=2,'rep_0'=4,'rep_1'=4] {'grp_0','grp_1','rep_0','..., dimensions={0} | all-to-all | bytes 262144 | tf_op jit(solution)/shard_map/all_to_all | solution.py:619
  108.4 1.3 %finish.1 = f32[32,128]{1,0:T(8,128)} custom-call(f32[128,2,128]{2,1,0:T(2,128)S(1)} %all_to_all.82.grams_ref, f32[32,128]{1,0:T(8,128)S(1)} %get-tuple-element.189.cur_ref), custom_call_target="tpu_custom_call" | custom-call | tf_op jit(solution)/shard_map/finish/pallas_call | solution.py:620
Async XLA Ops:
  3.8 15.0 %all-to-all-start.12 = ((f32[16,8,128]{2,1,0:T(8,128)}), f32[16,8,128]{2,1,0:T(8,128)S(1)}, u32[]{:S(2)}, u32[]{:S(2)}) async-start(f32[16,8,128]{2,1,0:T(8,128)} %get-tuple-element.171), calls=%async_computation.12 | async-start | bytes 131072 | tf_op jit(solution)/shard_map/all_to_all | solution.py:566
  12.2 6.5 %copy-start.1 = (s32[16]{0:T(128)S(1)}, s32[16]{0:T(128)}, u32[]{:S(2)}) copy-start(s32[16]{0:T(128)} %trunc_ref.3) | copy-start | bytes 196
  18.7 46.8 %copy-start = (s32[50,128]{1,0:T(8,128)S(1)}, s32[50,128]{1,0:T(8,128)}, u32[]{:S(2)}) copy-start(s32[50,128]{1,0:T(8,128)} %nb_ref.1) | copy-start | bytes 76804

commit v7 on v6

--- a/solution.py
+++ b/solution.py
@@ -181,19 +181,23 @@
 
 
 def pick_kernel(size, rx_ref, pack_ref, out_ref):
-    r = pl.program_id(0)
     rows = iota((PD, PD), 0)
     first = iota((PD, PD), 1) < CAP
-    sides = []
-    for p in range(WIDE):
-        picked = rows == rx_ref[WIDE * r + p][:1, :].astype(jnp.int32)
-        top = one_hot(picked & first)
-        bottom = one_hot(picked & jnp.logical_not(first))
-        sides.append(jnp.concatenate([top, bottom], axis=0))
-    side = jnp.concatenate(sides, axis=1)
-    chosen = jnp.dot(pack_ref[:size, :], side, preferred_element_type=F32).astype(BF16)
-    for p in range(WIDE):
-        out_ref[p] = chosen[:, p * PD : (p + 1) * PD]
+
+    def step(r, carry):
+        sides = []
+        for p in range(WIDE):
+            picked = rows == rx_ref[WIDE * r + p][:1, :].astype(jnp.int32)
+            top = one_hot(picked & first)
+            bottom = one_hot(picked & jnp.logical_not(first))
+            sides.append(jnp.concatenate([top, bottom], axis=0))
+        side = jnp.concatenate(sides, axis=1)
+        chosen = jnp.dot(pack_ref[:size, :], side, preferred_element_type=F32)
+        for p in range(WIDE):
+            out_ref[WIDE * r + p] = chosen[:, p * PD : (p + 1) * PD].astype(BF16)
+        return carry
+
+    lax.fori_loop(0, PEERS // WIDE, step, 0)
 
 
 def own_pairs(trunc_ref, e_ref, re_ref, im_ref, xt_ref, s_ref):
@@ -249,15 +253,26 @@
     size, trunc_ref, names_ref, pack_ref, recv_ref, table_ref, cur_ref,
     same_ref, cross_ref,
 ):
-    r = pl.program_id(0)
     kept = size - HEAD
-
-    @pl.when(r == 0)
-    def _():
-        for p in range(WIDE):
-            same_ref[p, kept:, :] = jnp.zeros((ANG, PD), F32)
-            cross_ref[p, kept:, :] = jnp.zeros((ANG, PD), F32)
-
+    for p in range(WIDE):
+        same_ref[p, kept:, :] = jnp.zeros((ANG, PD), F32)
+        cross_ref[p, kept:, :] = jnp.zeros((ANG, PD), F32)
+
+    def step(r, carry):
+        far_step(
+            size, r, trunc_ref, names_ref, pack_ref, recv_ref, table_ref, cur_ref,
+            same_ref, cross_ref,
+        )
+        return carry
+
+    lax.fori_loop(0, PEERS // WIDE, step, 0)
+
+
+def far_step(
+    size, r, trunc_ref, names_ref, pack_ref, recv_ref, table_ref, cur_ref,
+    same_ref, cross_ref,
+):
+    kept = size - HEAD
     first = iota((PD, PD), 1) < CAP
     sides = []
     for p in range(WIDE):
@@ -272,12 +287,12 @@
     freq = iota((ANG, PD), 0)
     halves = []
     for p in range(WIDE):
-        arrived = recv_ref[p, HEAD:, :].astype(F32)
+        arrived = recv_ref[WIDE * r + p, HEAD:, :].astype(F32)
         own = mine[:, p * PD : (p + 1) * PD]
         same_ref[p, :kept, :] = own * arrived
         cross_ref[p, :kept, :] = own * pltpu.roll(arrived, CAP, 1)
-        parts = recv_ref[p, :HEAD, :].astype(F32)
-        cur_ref[p] = parts[:VEC] + parts[VEC:]
+        parts = recv_ref[WIDE * r + p, :HEAD, :].astype(F32)
+        cur_ref[WIDE * r + p] = parts[:VEC] + parts[VEC:]
     for b in range(WIDE // 2):
         both = (2 * b, 2 * b + 1)
         totals = [[jnp.zeros((ANG, PD), F32)] * 2 for _ in both]
@@ -312,7 +327,7 @@
         m_im = 0.5 * jnp.sum(
             jnp.where(inner, s_im * next_re - s_re * next_im, 0.0), axis=0, keepdims=True
         ) - zero_re * s_im[1:2]
-        table_ref[b] = jnp.concatenate(
+        table_ref[WIDE // 2 * r + b] = jnp.concatenate(
             [energy, m_re, m_im, jnp.zeros((5, PD), F32)], axis=0
         )
 
@@ -491,36 +506,21 @@
     return pltpu.CompilerParams(vmem_limit_bytes=mib << 20)
 
 
-def whole(*shape):
-    return pl.BlockSpec(shape, lambda r: (0,) * len(shape))
-
-
 def exchange(size, truncation, names, asked, packed):
-    steps = PEERS // WIDE
     sent = pl.pallas_call(
         functools.partial(pick_kernel, size),
-        grid=(steps,),
         out_shape=struct((PEERS, size, PD), BF16),
-        in_specs=[whole(PEERS, 8, PD), whole(HEAD + FULL, 2 * PD)],
-        out_specs=pl.BlockSpec((WIDE, size, PD), lambda r: (r, 0, 0)),
+        in_specs=[VMEM, VMEM],
+        out_specs=VMEM,
         compiler_params=grant(16),
         name="pick",
     )(asked, packed)
     received = lax.all_to_all(sent, REP, 0, 0, tiled=True)
     return pl.pallas_call(
         functools.partial(far_kernel, size),
-        grid=(steps,),
         out_shape=(struct((PAIRS, 8, PD)), struct((PEERS, VEC, PD))),
-        in_specs=[
-            SMEM,
-            whole(PEERS, PD),
-            whole(HEAD + FULL, 2 * PD),
-            pl.BlockSpec((WIDE, size, PD), lambda r: (r, 0, 0)),
-        ],
-        out_specs=(
-            pl.BlockSpec((WIDE // 2, 8, PD), lambda r: (r, 0, 0)),
-            pl.BlockSpec((WIDE, VEC, PD), lambda r: (r, 0, 0)),
-        ),
+        in_specs=[SMEM, VMEM, VMEM, VMEM],
+        out_specs=(VMEM, VMEM),
         scratch_shapes=[
             pltpu.VMEM((WIDE, size - HEAD + ANG, PD), F32),
             pltpu.VMEM((WIDE, size - HEAD + ANG, PD), F32),

time: 108 us -> 107 us (level)
  no operation moved by 1% of the time
where the time goes in v7:
time: 107 us; the launch traced here: 109 us
  blocking collectives  80.5 us (75%)
  Pallas kernels  17.4 us (16%)
  starting transfers between devices  8.43 us (8%)
  waiting for transfers between devices  1.75 us (2%)
  between operations  1.34 us (1%)
    all_to_all x1, blocking collectives, exchange(): received = lax.all_to_all(sent, REP, 0, 0, tiled=True)  40.6 us
    all_to_all x1, blocking collectives, shards(): grams = lax.all_to_all(gram, GRP_REP, 0, 0, tiled=True)  20.4 us
    all_to_all x2, blocking collectives, shards(): columns = lax.all_to_all(columns, REP, 0, 0, tiled=True)  19.5 us
    all_to_all x1, starting transfers between devices, shards(): asked = lax.all_to_all(requests, REP, 0, 0, tiled=True)  8.43 us
    pallas_call x1, Pallas kernels, exchange(): pl.pallas_call(functools.partial(far_kernel, size), out_shape=(struct((PA...  4.51 us
    pallas_call x1, Pallas kernels, shards(): pl.pallas_call(local_kernel, out_shape=(struct((HEAD + FULL, 2 * PD), BF1...  4.1 us
    pallas_call x1, Pallas kernels, shards(): pl.pallas_call(slot_kernel, out_shape=(struct((1,), jnp.int32), struct((N...  3.12 us
  transfers between devices with their start and end apart: 1, of which 1 were waited for; matrix products, arithmetic and copies ran while one was open for 0% of the time, Pallas kernels for 4%

profile of v7, /device:TPU:1, one launch (start us, length us, event | category | flops | bytes accessed | tf_op | source)
XLA Modules:
  0.0 109.4 jit_solution(5100573420761733770)
XLA Ops:
  0.6 3.1 %slots.1 = (s32[1]{0:T(128)}, s32[56,128]{1,0:T(8,128)S(1)}, f32[8,128]{1,0:T(8,128)S(1)}, f32[16,128]{1,0:T(8,128)S(1)}, f32[16,8,128]{2,1,0:T(8,128)}, /*index...) custom-call(s32[16]{0:T(128)} %trunc_ref.3, s32[50,128]{1,0:T(8,128)} %nb_ref.1, bf16[128,2048]{1,0:T(8,128)(2,1)} %coef_hbm.1, ...), custom_call_target="tpu_custom_call" | custom-call | tf_op jit(solution)/shard_map/slots/pallas_call | solution.py:537
  3.8 8.4 %all-to-all-start.12 = ((f32[16,8,128]{2,1,0:T(8,128)}), f32[16,8,128]{2,1,0:T(8,128)S(1)}, u32[]{:S(2)}, u32[]{:S(2)}) async-start(f32[16,8,128]{2,1,0:T(8,128)} %get-tuple-element.171), calls=%async_computation.12 | async-start | bytes 131072 | tf_op jit(solution)/shard_map/all_to_all | solution.py:566
  12.2 0.0 copy-start.1
  12.2 4.1 %local.1 = (bf16[1056,256]{1,0:T(8,128)(2,1)S(1)}, f32[128,128]{1,0:T(8,128)S(1)}, f32[128,128]{1,0:T(8,128)S(1)}, f32[128,128]{1,0:T(8,128)S(1)}) custom-call(s32[16]{0:T(128)} %trunc_ref.3, bf16[128,2048]{1,0:T(8,128)(2,1)S(1)} %get-tuple-element.172.coef_ref, f32[32,128]{1,0:T(8,128)S(1)} %get-tuple-element.173.init_ref), custom_call_target="tpu_custom_call" | custom-call | flops 20000000000 | bytes 1000000 | tf_op jit(solution)/shard_map/local/pallas_call | solution.py:567
  17.0 1.8 %all-to-all-done.12.rx_ref = f32[16,8,128]{2,1,0:T(8,128)S(1)} async-done(((f32[16,8,128]{2,1,0:T(8,128)}), f32[16,8,128]{2,1,0:T(8,128)S(1)}, u32[]{:S(2)}, u32[]{:S(2)}) %all-to-all-start.12) | async-done | bytes 65568 | tf_op jit(solution)/shard_map/all_to_all | solution.py:566
  18.7 0.0 copy-done.1
  18.7 0.0 copy-start
  18.7 46.6 %conditional.1 = ((f32[8,8,128]{2,1,0:T(8,128)S(1)}, f32[16,16,128]{2,1,0:T(8,128)S(1)})) conditional(s32[]{:T(128)} %bitcast, (f32[16,8,128]{2,1,0:T(8,128)S(1)}, bf16[1056,256]{1,0:T(8,128)(2,1)S(1)}, s32[16]{0:T(128)S(1)}, f32[16,128]{1,0:T(8,128)S(1)}) %tuple.70, (f32[16,8,128]{2,1,0:T(8,128)S(1)}, ...), branch_computations={%region_0.0_spmd, %region_1.0_spmd, %region_2.0_spmd, %region_3.0_... | conditional | bytes 8650760 | solution.py:583
  18.7 1.5 %pick.18 = bf16[16,704,128]{2,1,0:T(8,128)(2,1)S(1)} custom-call(f32[16,8,128]{2,1,0:T(8,128)S(1)} %get-tuple-element.123.rx_ref, bf16[1056,256]{1,0:T(8,128)(2,1)S(1)} %get-tuple-element.122.pack_ref), custom_call_target="tpu_custom_call" | custom-call | tf_op jit(solution)/shard_map/cond/branch_6_fun/pick/pallas_call | solution.py:510
  20.2 40.6 %all_to_all.74.recv_ref = bf16[16,704,128]{2,1,0:T(8,128)(2,1)S(1)} all-to-all(bf16[16,704,128]{2,1,0:T(8,128)(2,1)S(1)} %pick.18), channel_id=1, replica_groups=mesh['grp_0'=4,'grp_1'=2,'rep_0'=4,'rep_1'=4] {'rep_0','rep_1'}, dimensions={0} | all-to-all | bytes 5767168 | tf_op jit(solution)/shard_map/cond/branch_6_fun/all_to_all | solution.py:518
  60.7 4.5 %far.18 = (f32[8,8,128]{2,1,0:T(8,128)S(1)}, f32[16,16,128]{2,1,0:T(8,128)S(1)}) custom-call(s32[16]{0:T(128)S(1)} %get-tuple-element.120.trunc_ref, f32[16,128]{1,0:T(8,128)S(1)} %get-tuple-element.121.names_ref, bf16[1056,256]{1,0:T(8,128)(2,1)S(1)} %get-tuple-element.122.pack_ref, bf16[16,704,128]{2,1,0:T(8,128)(2,1)S(1)} %all_to_all.74.recv_ref), custom_call_target="tpu_custom_call" | custom-call | tf_op jit(solution)/shard_map/cond/branch_6_fun/far/pallas_call | solution.py:519
  65.3 0.0 copy-done
  65.3 1.7 %first.1 = (f32[50,2,128]{2,1,0:T(2,128)}, f32[2,128,128]{2,1,0:T(8,128)S(1)}, f32[8,128]{1,0:T(8,128)S(1)}, f32[32,128]{1,0:T(8,128)S(1)}, f32[16,16,128]{2,1,0:T(8,128)S(1)}) custom-call(s32[50,128]{1,0:T(8,128)S(1)} %copy-done, s32[56,128]{1,0:T(8,128)S(1)} %get-tuple-element.168.code_ref, f32[8,128]{1,0:T(8,128)S(1)} %get-tuple-element.169.lists_ref, ...), custom_call_target="tpu_custom_call" | custom-call | tf_op jit(solution)/shard_map/first/pallas_call | solution.py:588
  67.0 9.6 %all_to_all.80.recv_ref = f32[16,16,128]{2,1,0:T(8,128)S(1)} all-to-all(f32[16,16,128]{2,1,0:T(8,128)S(1)} %get-tuple-element.182), channel_id=1, replica_groups=mesh['grp_0'=4,'grp_1'=2,'rep_0'=4,'rep_1'=4] {'rep_0','rep_1'}, dimensions={0} | all-to-all | bytes 262144 | tf_op jit(solution)/shard_map/all_to_all | solution.py:605
  76.6 0.6 middle.1
  77.2 9.8 %all_to_all.81.recv_ref = f32[16,16,128]{2,1,0:T(8,128)S(1)} all-to-all(f32[16,16,128]{2,1,0:T(8,128)S(1)} %get-tuple-element.186), channel_id=1, replica_groups=mesh['grp_0'=4,'grp_1'=2,'rep_0'=4,'rep_1'=4] {'rep_0','rep_1'}, dimensions={0} | all-to-all | bytes 262144 | tf_op jit(solution)/shard_map/all_to_all | solution.py:612
  87.1 0.6 last.1
  87.7 20.4 %all_to_all.82.grams_ref = f32[128,2,128]{2,1,0:T(2,128)S(1)} all-to-all(f32[128,2,128]{2,1,0:T(2,128)S(1)} %get-tuple-element.188), channel_id=1, replica_groups=mesh['grp_0'=4,'grp_1'=2,'rep_0'=4,'rep_1'=4] {'grp_0','grp_1','rep_0','..., dimensions={0} | all-to-all | bytes 262144 | tf_op jit(solution)/shard_map/all_to_all | solution.py:619
  108.1 1.3 %finish.1 = f32[32,128]{1,0:T(8,128)} custom-call(f32[128,2,128]{2,1,0:T(2,128)S(1)} %all_to_all.82.grams_ref, f32[32,128]{1,0:T(8,128)S(1)} %get-tuple-element.189.cur_ref), custom_call_target="tpu_custom_call" | custom-call | tf_op jit(solution)/shard_map/finish/pallas_call | solution.py:620
Async XLA Ops:
  3.8 15.0 %all-to-all-start.12 = ((f32[16,8,128]{2,1,0:T(8,128)}), f32[16,8,128]{2,1,0:T(8,128)S(1)}, u32[]{:S(2)}, u32[]{:S(2)}) async-start(f32[16,8,128]{2,1,0:T(8,128)} %get-tuple-element.171), calls=%async_computation.12 | async-start | bytes 131072 | tf_op jit(solution)/shard_map/all_to_all | solution.py:566
  12.2 6.5 %copy-start.1 = (s32[16]{0:T(128)S(1)}, s32[16]{0:T(128)}, u32[]{:S(2)}) copy-start(s32[16]{0:T(128)} %trunc_ref.3) | copy-start | bytes 196
  18.7 46.6 %copy-start = (s32[50,128]{1,0:T(8,128)S(1)}, s32[50,128]{1,0:T(8,128)}, u32[]{:S(2)}) copy-start(s32[50,128]{1,0:T(8,128)} %nb_ref.1) | copy-start | bytes 76804
